TPU v7x, 32 devices: a whole 2x2x4 slice. The times are simulated.
32 devices in a mesh: crop: 4 (over x, core), row: 8 (over z, y).
Axes of the slice: x: 2, y: 2, z: 4, core: 2. Of those that a mesh axis runs over, the one named last changes fastest.
Arguments:
- pair: float32 [768, 192, 128], P(('crop', 'row')), parts along dimension 0, may hold values from -6 to 6
- single: float32 [768, 384], P(('crop', 'row')), parts along dimension 0, may hold values from -6 to 6
- token_mask: int32 [768], P('crop'), parts along dimension 0, may hold values from 0 to 1, as said below
- w_tri_proj: bfloat16 [128, 512], replicated, may hold values from -0.5 to 0.5
- w_tri_gate: bfloat16 [128, 128], replicated, may hold values from -0.5 to 0.5
- w_tri_out: bfloat16 [128, 128], replicated, may hold values from -0.5 to 0.5
- w_trans_in: bfloat16 [128, 1024], replicated, may hold values from -0.5 to 0.5
- w_trans_out: bfloat16 [512, 128], replicated, may hold values from -0.25 to 0.25
- w_bias: bfloat16 [128, 16], replicated, may hold values from -0.5 to 0.5
- w_query: bfloat16 [384, 384], replicated, may hold values from -16 to 16
- w_key: bfloat16 [384, 384], replicated, may hold values from -0.5 to 0.5
- w_value_gate: bfloat16 [384, 768], replicated, may hold values from -0.3125 to 0.3125
- w_out: bfloat16 [384, 384], replicated, may hold values from -0.3125 to 0.3125
Outputs:
- pair_new: float32 [768, 192, 128], P(('crop', 'row')), parts along dimension 0
- single_update: float32 [768, 384], P(('crop', 'row')), parts along dimension 0
There are 4 independent parts, one for each index of `crop`. A program takes and returns all parts, laid end to end along the dimension named above; an argument that names none is the same for every part. Nothing has to cross between parts.
Inputs may be any that keep to these rules, and one draw needn't show every extreme that they name: `token_mask`: ones for the first tokens of a crop and zeros after them; at least 96 ones.
All inputs are finite; a program needn't handle non-finite values.
Results may differ from a plain program's by a relative error of at most 0.013.
The roundings to bfloat16 on the way count: a program that leaves them out, or rounds other values in their place, can miss the bound.
Values may be sent and summed in bfloat16 or wider, within the bound.
No kernel may reach another device: no remote copies, remote signals or barrier semaphores. Data moves between devices by JAX's collectives and lax.ppermute only.
A program may use at most 128 MiB of HBM per device.

v0:
```python
import math

import jax
import jax.numpy as jnp
from jax import lax
from jax.sharding import PartitionSpec as P

epsilon = 1e-05


def layer_norm(values_in, along):
    average = jnp.mean(values_in, axis=along, keepdims=True)
    centered = values_in - average
    spread = jnp.mean(centered * centered, axis=along, keepdims=True)
    return centered * lax.rsqrt(spread + epsilon)


def triangle(pieces):
    left_op, right_op = pieces
    return jnp.einsum("gcik,gcjk->gcij", left_op, right_op, preferred_element_type=jnp.float32)


def body(
    pair,
    single,
    token_mask,
    w_tri_proj,
    w_tri_gate,
    w_tri_out,
    w_trans_in,
    w_trans_out,
    w_bias,
    w_query,
    w_key,
    w_value_gate,
    w_out,
):
    row_count, length, pair_width = pair.shape
    groups = lax.axis_size("row")
    hidden = w_tri_out.shape[0]
    per_dev = hidden // groups
    inner_width = w_trans_out.shape[0]
    head_count = w_bias.shape[1]
    channels = single.shape[1]
    head_size = channels // head_count
    row_start = lax.axis_index("row") * row_count
    live_all = token_mask.astype(jnp.float32)
    own_live = lax.dynamic_slice_in_dim(live_all, row_start, row_count)
    pair_live = own_live[:, None] * live_all[None, :]
    normed = layer_norm(pair, 2).astype(jnp.bfloat16)

    def operand(offset):
        weights_two = w_tri_proj[:, offset * hidden : (offset + 2) * hidden].reshape(
            pair_width, 2, groups, per_dev
        )
        projected = jnp.einsum(
            "ikd,dsgc->sgcik", normed, weights_two, preferred_element_type=jnp.float32
        )
        return (jax.nn.sigmoid(projected[1]) * projected[0] * pair_live).astype(jnp.bfloat16)

    left_edge = operand(0)
    right_edge = operand(2)
    product = triangle(
        (
            lax.all_to_all(left_edge, "row", split_axis=0, concat_axis=2, tiled=True),
            lax.all_to_all(right_edge, "row", split_axis=0, concat_axis=2, tiled=True),
        )
    )
    returned = lax.all_to_all(
        product.astype(jnp.bfloat16), "row", split_axis=2, concat_axis=0, tiled=True
    ).astype(product.dtype)
    summed = returned.reshape(hidden, row_count, length)
    triangle_normed = layer_norm(summed, 0).astype(jnp.bfloat16)
    tri_out = jnp.einsum(
        "cij,cd->ijd", triangle_normed, w_tri_out, preferred_element_type=jnp.float32
    )
    gate_pair = jax.nn.sigmoid(
        jnp.einsum("ijc,cd->ijd", normed, w_tri_gate, preferred_element_type=jnp.float32)
    )
    pair_mid = pair + gate_pair * tri_out
    block_rows = math.gcd(row_count, 8)

    def transition(row_slab):
        trans_normed = layer_norm(row_slab, 2).astype(jnp.bfloat16)
        gate_up = jnp.einsum(
            "ijc,cf->ijf", trans_normed, w_trans_in, preferred_element_type=jnp.float32
        )
        inner_act = (jax.nn.silu(gate_up[..., :inner_width]) * gate_up[..., inner_width:]).astype(
            jnp.bfloat16
        )
        return row_slab + jnp.einsum(
            "ijf,fc->ijc", inner_act, w_trans_out, preferred_element_type=jnp.float32
        )

    pair_new = lax.map(
        transition, pair_mid.reshape(row_count // block_rows, block_rows, length, pair_width)
    ).reshape(row_count, length, pair_width)
    bias_normed = layer_norm(pair_new, 2).astype(jnp.bfloat16)
    bias = jnp.einsum("ijc,ch->hij", bias_normed, w_bias, preferred_element_type=jnp.float32)
    single_normed = layer_norm(single, 1).astype(jnp.bfloat16)
    queries = jnp.dot(single_normed, w_query, preferred_element_type=jnp.float32).astype(
        jnp.bfloat16
    )
    att_gate = jax.nn.sigmoid(
        jnp.dot(single_normed, w_value_gate[:, channels:], preferred_element_type=jnp.float32)
    )
    normed_all = lax.all_gather(single_normed, "row", axis=0, tiled=True)
    keys_all = jnp.dot(normed_all, w_key, preferred_element_type=jnp.float32).astype(jnp.bfloat16)
    values_all = jnp.dot(
        normed_all, w_value_gate[:, :channels], preferred_element_type=jnp.float32
    ).astype(jnp.bfloat16)
    query_heads = queries.reshape(row_count, head_count, head_size)
    key_heads = keys_all.reshape(length, head_count, head_size)
    value_heads = values_all.reshape(length, head_count, head_size)
    scores = (
        jnp.einsum("ihd,jhd->hij", query_heads, key_heads, preferred_element_type=jnp.float32)
        / jnp.sqrt(jnp.float32(head_size))
        + bias
    )
    scores = jnp.where(live_all[None, None, :] > 0, scores, jnp.float32(-1000000000.0))
    row_max = jnp.max(scores, axis=2, keepdims=True)
    weights = jnp.exp(scores - row_max)
    weights = weights / jnp.sum(weights, axis=2, keepdims=True)
    probs = weights.astype(jnp.bfloat16)
    attended = jnp.einsum(
        "hij,jhd->ihd", probs, value_heads, preferred_element_type=jnp.float32
    ).reshape(row_count, channels)
    gated = (att_gate * attended).astype(jnp.bfloat16)
    single_update = jnp.dot(gated, w_out, preferred_element_type=jnp.float32)
    return (pair_new, single_update)


def solution(mesh):
    in_specs = (
        P(("crop", "row"), None, None),
        P(("crop", "row"), None),
        P("crop"),
        P(),
        P(),
        P(),
        P(),
        P(),
        P(),
        P(),
        P(),
        P(),
        P(),
    )
    out_specs = (P(("crop", "row"), None, None), P(("crop", "row"), None))
    return jax.shard_map(body, mesh=mesh, in_specs=in_specs, out_specs=out_specs, check_vma=False)
```

profile of v0, /device:TPU:0, one launch (start us, length us, event | category | flops | bytes accessed | tf_op | source)
XLA Modules:
  0.0 205.6 jit_solution(4397864102758015357)
XLA Ops:
  1.6 2.5 %reduce_sum.99 = f32[24,192]{1,0:T(8,128)S(1)} reduce(f32[24,192,128]{2,1,0:T(8,128)} %param.15, f32[]{:T(128)} %constant.22.clone.1), dimensions={2}, to_apply=%region_0.0 | reduce | flops 585216 | bytes 2377732 | tf_op jit(solution)/shard_map/reduce_sum | solution.py:12
  4.2 1.7 multiply_reduce_fusion.2
  6.0 2.5 %multiply_convert_fusion.3 = bf16[24,192,128]{2,1,0:T(8,128)(2,1)} fusion(f32[24,192,128]{2,1,0:T(8,128)S(1)} %copy-done.1, f32[24,192]{1,0:T(8,128)S(1)} %add_rsqrt_fusion.2, f32[24,192]{1,0:T(8,128)S(1)} %broadcast_multiply_fusion.4), kind=kLoop, calls=%fused_computation.50 | loop fusion | flops 1769472 | bytes 3575808 | tf_op jit(solution)/shard_map/convert_element_type | solution.py:50
  8.7 2.4 %convolution_bitcast_fusion = f32[2,8,16,24,192]{4,2,1,3,0:T(8,128)S(1)} fusion(bf16[128,2,8,16,1]{0,3,2,4,1:T(8,128)(2,1)S(1)} %bitcast.153, bf16[24,192,128]{2,1,0:T(8,128)(2,1)} %multiply_convert_fusion.3), kind=kOutput, calls=%fused_computation.45 | convolution fusion | flops 301989888 | bytes 5963776 | tf_op jit(solution)/shard_map/ikd,dsgc->sgcik/dot_general | solution.py:56
  12.1 2.7 %fusion.22 = (bf16[8,16,24,192]{3,1,0,2:T(8,128)(2,1)}, bf16[8,16,24,192]{3,1,0,2:T(8,128)(2,1)S(1)}) fusion(f32[2,8,16,24,192]{4,2,1,3,0:T(8,128)S(1)} %convolution_bitcast_fusion, f32[24,192]{1,0:T(8,128)S(1)} %broadcast_multiply_fusion.2, f32[2,8,16,24,192]{4,2,1,0,3:T(8,128)S(1)} %convolution_bitcast_fusion.1), kind=kLoop, calls=%fused_computation.23 | loop fusion | flops 7077888 | bytes 11814912 | tf_op jit(solution)/shard_map/convert_element_type | solution.py:59
  14.8 1.3 copy.41
  16.1 7.3 %all-to-all-start = ((bf16[8,16,24,192]{3,1,2,0:T(8,128)(2,1)}), bf16[8,16,24,192]{3,1,2,0:T(8,128)(2,1)S(1)}, u32[]{:S(2)}, u32[]{:S(2)}) async-start(bf16[8,16,24,192]{3,1,2,0:T(8,128)(2,1)} %copy.41), calls=%async_computation | async-start | bytes 3145728 | tf_op jit(solution)/shard_map/all_to_all | solution.py:65
  23.4 2.7 %copy.45 = bf16[8,16,24,192]{3,1,2,0:T(8,128)(2,1)} copy(bf16[8,16,24,192]{3,1,0,2:T(8,128)(2,1)} %get-tuple-element.44) | data formatting | bytes 2359296 | tf_op jit(solution)/shard_map/convert_element_type | solution.py:59
  26.1 34.3 %all-to-all-done = bf16[8,16,24,192]{3,1,2,0:T(8,128)(2,1)S(1)} async-done(((bf16[8,16,24,192]{3,1,2,0:T(8,128)(2,1)}), bf16[8,16,24,192]{3,1,2,0:T(8,128)(2,1)S(1)}, u32[]{:S(2)}, u32[]{:S(2)}) %all-to-all-start) | async-done | bytes 1179680 | tf_op jit(solution)/shard_map/all_to_all | solution.py:65
  60.4 4.3 %all-to-all-start.1 = ((bf16[8,16,24,192]{3,1,2,0:T(8,128)(2,1)}), bf16[8,16,24,192]{3,1,2,0:T(8,128)(2,1)}, u32[]{:S(2)}, u32[]{:S(2)}) async-start(bf16[8,16,24,192]{3,1,2,0:T(8,128)(2,1)} %copy.45), calls=%async_computation.1 | async-start | bytes 3145728 | tf_op jit(solution)/shard_map/all_to_all | solution.py:66
  64.8 1.7 copy.42
  66.5 34.8 %all-to-all-done.1 = bf16[8,16,24,192]{3,1,2,0:T(8,128)(2,1)} async-done(((bf16[8,16,24,192]{3,1,2,0:T(8,128)(2,1)}), bf16[8,16,24,192]{3,1,2,0:T(8,128)(2,1)}, u32[]{:S(2)}, u32[]{:S(2)}) %all-to-all-start.1) | async-done | bytes 1179680 | tf_op jit(solution)/shard_map/all_to_all | solution.py:66
  101.4 1.9 copy.46
  103.9 2.0 copy.47
  106.0 3.8 %all-to-all-start.2 = ((bf16[1,16,192,192]{3,1,0,2:T(8,128)(2,1)}), bf16[1,16,192,192]{3,1,0,2:T(8,128)(2,1)S(1)}, u32[]{:S(2)}, u32[]{:S(2)}) async-start(bf16[1,16,192,192]{3,1,0,2:T(8,128)(2,1)} %copy.47), calls=%async_computation.2 | async-start | bytes 3145728 | tf_op jit(solution)/shard_map/all_to_all | solution.py:69
  110.0 57.2 %all_gather.3 = bf16[192,384]{1,0:T(8,128)(2,1)S(1)} all-gather(bf16[24,384]{1,0:T(8,128)(2,1)S(1)} %multiply_convert_fusion.5), channel_id=1, replica_groups=mesh['crop'=4,'row'=8] {'row'}, dimensions={0}, use_global_device_ids=true | all-gather | bytes 165888 | tf_op jit(solution)/shard_map/all_gather | solution.py:107
  167.6 1.1 convolution_convert_fusion.3
  169.6 1.2 convolution_convert_fusion.2
  171.6 2.6 %fusion.61 = f32[24,192,128]{2,1,0:T(8,128)} fusion(bf16[24,192,128]{2,1,0:T(8,128)(2,1)S(1)} %copy-done.3, bf16[128,128]{1,0:T(8,128)(2,1)} %param.19), kind=kOutput, calls=%fused_computation.83 | convolution fusion | flops 150994944 | bytes 3571712 | tf_op jit(solution)/shard_map/ijc,cd->ijd/dot_general | solution.py:78
  175.2 1.8 bitcast_reduce_fusion
  177.0 1.8 fusion.37
  179.2 1.3 copy-done.2
  182.2 11.9 %while.10 = (s32[]{:T(128)}, f32[3,8,192,128]{3,2,1,0:T(8,128)}, f32[3,8,192,128]{3,2,1,0:T(8,128)S(1)}, bf16[128,1024]{1,0:T(8,128)(2,1)S(1)}, bf16[512,128]{1,0:T(8,128)(2,1)S(1)}, /*index=5*/s32[]{:T(128)}) while((s32[]{:T(128)}, f32[3,8,192,128]{3,2,1,0:T(8,128)}, f32[3,8,192,128]{3,2,1,0:T(8,128)S(1)}, bf16[128,1024]{1,0:T(8,128)(2,1)S(1)}, ...), condition=%wide.region_7.8_spmd, body=%wide.region_4.7_spmd.sunk | while | flops 610272768 | bytes 16968272 | solution.py:95
  183.4 1.0 fusion.94
  184.5 1.9 fusion.95
  187.3 1.0 fusion.94
  188.4 1.9 fusion.95
  191.2 1.0 fusion.94
  192.2 1.9 fusion.95
  194.1 2.6 %reduce_sum.105 = f32[3,8,192]{2,1,0:T(8,128)S(1)} reduce(f32[3,8,192,128]{3,2,1,0:T(8,128)} %get-tuple-element.29, f32[]{:T(128)} %constant.22.clone.1), dimensions={3}, to_apply=%region_10.11 | reduce | flops 585216 | bytes 2377732 | tf_op jit(solution)/shard_map/reduce_sum | solution.py:12
  196.7 3.0 %multiply_reduce_fusion.1 = f32[3,8,192]{2,1,0:T(8,128)S(1)} fusion(f32[3,8,192,128]{3,2,1,0:T(8,128)} %get-tuple-element.29, f32[3,8,192]{2,1,0:T(8,128)S(1)} %get-tuple-element.43), kind=kLoop, calls=%fused_computation.48 | loop fusion | flops 1764864 | bytes 2396160 | tf_op jit(solution)/shard_map/reduce_sum | solution.py:14
  199.7 3.5 %fusion.44 = f32[24,192,16]{1,2,0:T(8,128)S(1)} fusion(f32[24,192,128]{2,1,0:T(8,128)} %bitcast.30, f32[24,192]{1,0:T(8,128)S(1)} %rsqrt_bitcast_fusion, f32[24,192]{1,0:T(8,128)S(1)} %get-tuple-element.42, bf16[128,16]{0,1:T(8,128)(2,1)S(1)} %copy-done.15), kind=kOutput, calls=%fused_computation.60 | convolution fusion | flops 20643840 | bytes 2695168 | tf_op jit(solution)/shard_map/ijc,ch->hij/dot_general | solution.py:99
  (84 shorter events, 13.5 us)
Async XLA Ops:
  0.6 166.6 %copy-start = (bf16[384,384]{1,0:T(8,128)(2,1)S(1)}, bf16[384,384]{1,0:T(8,128)(2,1)}, u32[]{:S(2)}) copy-start(bf16[384,384]{1,0:T(8,128)(2,1)} %param.25) | copy-start | bytes 884740
  0.6 3.6 %copy-start.1 = (f32[24,192,128]{2,1,0:T(8,128)S(1)}, f32[24,192,128]{2,1,0:T(8,128)}, u32[]{:S(2)}) copy-start(f32[24,192,128]{2,1,0:T(8,128)} %param.15) | copy-start | bytes 7077892
  6.0 2.5 %copy-start.14 = (bf16[128,512]{1,0:T(8,128)(2,1)S(1)}, bf16[128,512]{1,0:T(8,128)(2,1)}, u32[]{:S(2)}) copy-start(bf16[128,512]{1,0:T(8,128)(2,1)} %param.18) | copy-start | bytes 393220
  8.7 2.4 %copy-start.3 = (bf16[24,192,128]{2,1,0:T(8,128)(2,1)S(1)}, bf16[24,192,128]{2,1,0:T(8,128)(2,1)}, u32[]{:S(2)}) copy-start(bf16[24,192,128]{2,1,0:T(8,128)(2,1)} %multiply_convert_fusion.3) | copy-start | bytes 3538948
  16.1 44.3 %all-to-all-start = ((bf16[8,16,24,192]{3,1,2,0:T(8,128)(2,1)}), bf16[8,16,24,192]{3,1,2,0:T(8,128)(2,1)S(1)}, u32[]{:S(2)}, u32[]{:S(2)}) async-start(bf16[8,16,24,192]{3,1,2,0:T(8,128)(2,1)} %copy.41), calls=%async_computation | async-start | bytes 3145728 | tf_op jit(solution)/shard_map/all_to_all | solution.py:65
  26.1 38.6 %copy-start.9 = (f32[24,384]{1,0:T(8,128)S(1)}, f32[24,384]{1,0:T(8,128)}, u32[]{:S(2)}) copy-start(f32[24,384]{1,0:T(8,128)} %param.16) | copy-start | bytes 110596
  60.4 40.9 %all-to-all-start.1 = ((bf16[8,16,24,192]{3,1,2,0:T(8,128)(2,1)}), bf16[8,16,24,192]{3,1,2,0:T(8,128)(2,1)}, u32[]{:S(2)}, u32[]{:S(2)}) async-start(bf16[8,16,24,192]{3,1,2,0:T(8,128)(2,1)} %copy.45), calls=%async_computation.1 | async-start | bytes 3145728 | tf_op jit(solution)/shard_map/all_to_all | solution.py:66
  66.5 36.8 %copy-start.5 = (bf16[8,16,24,192]{3,2,0,1:T(8,128)(2,1)S(1)}, bf16[8,16,24,192]{3,2,0,1:T(8,128)(2,1)}, u32[]{:S(2)}) copy-start(bf16[8,16,24,192]{3,2,0,1:T(8,128)(2,1)} %copy.42) | copy-start | bytes 3538948
  106.0 65.6 %copy-start.16 = (s32[192]{0:T(256)S(1)}, s32[192]{0:T(256)}, u32[]{:S(2)}) copy-start(s32[192]{0:T(256)} %param.17) | copy-start | bytes 2308
  106.0 68.3 %all-to-all-start.2 = ((bf16[1,16,192,192]{3,1,0,2:T(8,128)(2,1)}), bf16[1,16,192,192]{3,1,0,2:T(8,128)(2,1)S(1)}, u32[]{:S(2)}, u32[]{:S(2)}) async-start(bf16[1,16,192,192]{3,1,0,2:T(8,128)(2,1)} %copy.47), calls=%async_computation.2 | async-start | bytes 3145728 | tf_op jit(solution)/shard_map/all_to_all | solution.py:69
  110.0 57.2 %copy-start.10 = (bf16[24,384]{1,0:T(8,128)(2,1)}, bf16[24,384]{1,0:T(8,128)(2,1)S(1)}, u32[]{:S(2)}) copy-start(bf16[24,384]{1,0:T(8,128)(2,1)S(1)} %multiply_convert_fusion.5) | copy-start | bytes 55300
  178.8 1.7 copy-start.2
  178.8 2.4 %copy-start.6 = (f32[24,192,128]{2,1,0:T(8,128)S(1)}, f32[24,192,128]{2,1,0:T(8,128)}, u32[]{:S(2)}) copy-start(f32[24,192,128]{2,1,0:T(8,128)} %fusion.61) | copy-start | bytes 7077892
  178.8 2.4 %copy-start.18 = (bf16[128,128]{1,0:T(8,128)(2,1)S(1)}, bf16[128,128]{1,0:T(8,128)(2,1)}, u32[]{:S(2)}) copy-start(bf16[128,128]{1,0:T(8,128)(2,1)} %param.20) | copy-start | bytes 98308
  181.2 1.0 copy-start.4
  181.2 1.0 copy-start.17
  194.1 5.6 %copy-start.15 = (bf16[128,16]{0,1:T(8,128)(2,1)S(1)}, bf16[128,16]{0,1:T(8,128)(2,1)}, u32[]{:S(2)}) copy-start(bf16[128,16]{0,1:T(8,128)(2,1)} %param.23) | copy-start | bytes 12292
  196.7 6.6 %copy-start.8 = (bf16[24,16,24]{2,1,0:T(8,128)(2,1)S(1)}, bf16[24,16,24]{2,1,0:T(8,128)(2,1)}, u32[]{:S(2)}) copy-start(bf16[24,16,24]{2,1,0:T(8,128)(2,1)} %reshape.173) | copy-start | bytes 55300
  199.7 4.1 %copy-start.13 = (bf16[192,384]{0,1:T(8,128)(2,1)S(1)}, bf16[192,384]{0,1:T(8,128)(2,1)}, u32[]{:S(2)}) copy-start(bf16[192,384]{0,1:T(8,128)(2,1)} %copy.50) | copy-start | bytes 442372
  203.2 1.4 copy-start.7
  203.2 1.4 copy-start.11
  203.2 1.4 copy-start.12
where the time goes:
time: 206 us
  waiting for transfers between devices  69.1 us (34%)
  blocking collectives  57.2 us (28%)
  matrix products  24.4 us (12%)
  other arithmetic  23.8 us (12%)
  starting transfers between devices  15.4 us (7%)
  local copies, waits for them, and re-layouts  14.4 us (7%)
    all_gather x1, blocking collectives, body(): normed_all = lax.all_gather(single_normed, 'row', axis=0, tiled=True)  57.2 us
    all_to_all x1, waiting for transfers between devices, body(): lax.all_to_all(right_edge, 'row', split_axis=0, concat_axis=2, tiled=True)  34.8 us
    all_to_all x1, waiting for transfers between devices, body(): lax.all_to_all(left_edge, 'row', split_axis=0, concat_axis=2, tiled=True)  34.3 us
    reduce_sum x7, other arithmetic, layer_norm(): spread = jnp.mean(centered * centered, axis=along, keepdims=True)  8.52 us
    reduce_sum x7, other arithmetic, layer_norm(): average = jnp.mean(values_in, axis=along, keepdims=True)  8.04 us
    all_to_all x1, starting transfers between devices, body(): lax.all_to_all(left_edge, 'row', split_axis=0, concat_axis=2, tiled=True)  7.31 us
    dot_general x3, matrix products, transition(): jnp.einsum('ijf,fc->ijc', inner_act, w_trans_out, preferred_element_type=...  5.6 us
    all_to_all x1, starting transfers between devices, body(): lax.all_to_all(right_edge, 'row', split_axis=0, concat_axis=2, tiled=True)  4.29 us
  transfers between devices with their start and end apart: 3, of which 2 were waited for; matrix products, arithmetic and copies ran while one was open for 6% of the time, Pallas kernels for 0%

commit v1 on v0

--- a/solution.py
+++ b/solution.py
@@ -1,11 +1,20 @@
+import functools
 import math
 
 import jax
 import jax.numpy as jnp
 from jax import lax
+from jax.experimental import pallas as pl
+from jax.experimental.pallas import tpu as pltpu
 from jax.sharding import PartitionSpec as P
 
+
 epsilon = 1e-05
+LANES = 128
+SUB = 8
+f32 = jnp.float32
+bf16 = jnp.bfloat16
+NT = (((1,), (1,)), ((), ()))
 
 
 def layer_norm(values_in, along):
@@ -15,12 +24,465 @@
     return centered * lax.rsqrt(spread + epsilon)
 
 
+def sigmoid(x):
+    return 0.5 * jnp.tanh(0.5 * x) + 0.5
+
+
+def repeat_rest(x, full):
+    return jnp.concatenate([x, x[full:]], axis=0)
+
+
+def first_half_lanes(shape):
+    return lax.broadcasted_iota(jnp.int32, shape, len(shape) - 1) < LANES // 2
+
+
+def edges_to_messages(me_ref, mask_ref, live_ref, wt_ref, rows_of, head_ref, rest_ref, out_refs, first, hidden, full):
+    sets = len(out_refs)
+    per_set = hidden // sets
+    pairs = per_set // 2
+    stride = hidden + SUB
+    own_set = lax.rem(me_ref[0], sets)
+    tokens = live_ref[...].astype(f32).reshape(1, live_ref.shape[0])
+    tokens = jnp.concatenate([tokens, tokens[:, full:]], axis=1)
+    for j in range(SUB):
+        x = repeat_rest(rows_of(j), full)
+        projected = lax.dot_general(wt_ref[...], x, NT, preferred_element_type=f32)
+        live = tokens * mask_ref[first + j].astype(f32)
+        edge = sigmoid(projected[hidden:]) * projected[:hidden] * live
+        for s in range(sets):
+            q = lax.bitwise_xor(own_set, s)
+            at = pl.multiple_of(j * stride + q * per_set, SUB)
+            part = edge[s * per_set : (s + 1) * per_set]
+            head_ref[pl.ds(at, per_set), :] = part[:, :LANES]
+            rest_ref[pl.ds(at, per_set), :] = part[:, LANES:]
+    low = first_half_lanes((SUB, LANES))
+    for q in range(sets):
+        for c in range(pairs):
+            a = pl.ds(q * per_set + c, SUB, stride=stride)
+            b = pl.ds(q * per_set + pairs + c, SUB, stride=stride)
+            out_refs[q][c, 0] = head_ref[a, :].astype(bf16)
+            out_refs[q][pairs + c, 0] = head_ref[b, :].astype(bf16)
+            out_refs[q][per_set + c, 0] = jnp.where(low, rest_ref[a, :], rest_ref[b, :]).astype(bf16)
+
+
+def right_kernel(hidden, full, sets, row_count, offset, me_ref, mask_ref, pair_ref, single_ref, live_ref, w_ref, *rest):
+    out_refs = rest[-3 - sets : -3]
+    head_ref, rest_ref, wt_ref = rest[-3:]
+
+    @pl.when(pl.program_id(0) == 0)
+    def _():
+        wt_ref[...] = w_ref[...].T
+
+    first = me_ref[0] * row_count + offset + pl.program_id(0) * SUB
+    rows_of = lambda j: layer_norm(pair_ref[j], 1).astype(bf16)
+    edges_to_messages(me_ref, mask_ref, live_ref, wt_ref, rows_of, head_ref, rest_ref, out_refs, first, hidden, full)
+    single_normed = layer_norm(single_ref[...], 1).astype(bf16)
+    slabs = single_ref.shape[1] // LANES
+    base = hidden // sets * 3 // 2
+    for q in range(sets):
+        for t in range(slabs):
+            out_refs[q][base + t, 0] = single_normed[:, t * LANES : (t + 1) * LANES]
+
+
+def left_kernel(hidden, full, sets, row_count, me_ref, mask_ref, pair_ref, live_ref, w_ref, *rest):
+    out_refs = rest[-3 - sets : -3]
+    head_ref, rest_ref, wt_ref = rest[-3:]
+
+    @pl.when(pl.program_id(0) == 0)
+    def _():
+        wt_ref[...] = w_ref[...].T
+
+    first = me_ref[0] * row_count + pl.program_id(0) * SUB
+    rows_of = lambda j: layer_norm(pair_ref[j], 1).astype(bf16)
+    edges_to_messages(me_ref, mask_ref, live_ref, wt_ref, rows_of, head_ref, rest_ref, out_refs, first, hidden, full)
+
+
+def gate_kernel(pair_ref, w_gate_ref, _, gate_ref):
+    rows = pair_ref.shape[0] * pair_ref.shape[1]
+    x = layer_norm(pair_ref[...].reshape(rows, pair_ref.shape[2]), 1).astype(bf16)
+    gate_ref[...] = sigmoid(jnp.dot(x, w_gate_ref[...], preferred_element_type=f32)).reshape(gate_ref.shape)
+
+
+def plain_rows(block):
+    wide = block.astype(f32)
+    return wide.reshape(wide.shape[0] * wide.shape[1], wide.shape[2])
+
+
+def triangle_kernel(groups, sets, per_set, me_ref, *refs):
+    right_refs, left_refs = refs[:groups], refs[groups : groups + sets]
+    out_refs = refs[-sets - 3 : -3]
+    head_ref, rest_ref, sums_ref = refs[-3:]
+    pairs = per_set // 2
+    rows = left_refs[0].shape[1] * SUB
+    here = right_refs[0].shape[1] * SUB
+    columns = groups * here
+    me = me_ref[0]
+    total = sets * rows
+    stride = total + SUB
+    low = first_half_lanes((total, LANES))
+    fill = lambda x: x if columns == LANES else jnp.concatenate([x, x], axis=0)
+    for s in range(groups):
+        d = lax.bitwise_xor(me, s)
+        wide = right_refs[s][: per_set + pairs].astype(f32).reshape(per_set + pairs, here, LANES)
+        head_ref[:, d] = wide[:per_set]
+        rest_ref[:, d] = wide[per_set:]
+    for c in range(pairs):
+        right_rest = fill(rest_ref[c].reshape(columns, LANES)).astype(bf16)
+        left_rest = jnp.concatenate([plain_rows(r[per_set + c]) for r in left_refs], axis=0)
+        for p in range(2):
+            channel = p * pairs + c
+            right = fill(head_ref[channel].reshape(columns, LANES)).astype(bf16)
+            left = jnp.concatenate([plain_rows(r[channel]) for r in left_refs], axis=0).astype(bf16)
+            kept = jnp.where(low if p == 0 else jnp.logical_not(low), left_rest, 0.0).astype(bf16)
+            sums_ref[channel * stride : channel * stride + total, :] = lax.dot_general(
+                jnp.concatenate([left, kept], axis=1),
+                jnp.concatenate([right, right_rest], axis=1),
+                NT,
+                preferred_element_type=f32,
+            )
+    low_half = first_half_lanes((pairs, LANES))
+    for a in range(sets):
+        for i in range(rows):
+            x = sums_ref[pl.ds(a * rows + i, per_set, stride=stride), :]
+            if columns < LANES:
+                x = jnp.where(low_half, x[:pairs], x[pairs:])
+            out_refs[a][i] = x.astype(bf16)
+
+
+def attention_in_kernel(groups, chunks, me_ref, *refs):
+    n = len(chunks)
+    right_refs = refs[: groups * n]
+    w_query_ref, w_key_ref, w_value_gate_ref, q_ref, g_ref = refs[groups * n : groups * n + 5]
+    k_refs = refs[groups * n + 5 : groups * n + 5 + n]
+    v_refs = refs[groups * n + 5 + n : groups * n + 5 + 2 * n]
+    all_refs = refs[groups * n + 5 + 2 * n :]
+    channels = w_query_ref.shape[0]
+    me = me_ref[0]
+    for k in range(n):
+        for s in range(groups):
+            d = lax.bitwise_xor(me, s)
+            for t in range(channels // LANES):
+                all_refs[k][d, :, t * LANES : (t + 1) * LANES] = plain_rows(right_refs[k * groups + s][t])
+    own = jnp.concatenate([r[me] for r in all_refs], axis=0).astype(bf16)
+    q_ref[...] = jnp.dot(own, w_query_ref[...], preferred_element_type=f32).astype(bf16)
+    g_ref[...] = sigmoid(jnp.dot(own, w_value_gate_ref[:, channels:], preferred_element_type=f32))
+    for k in range(n):
+        every = all_refs[k][...].reshape(k_refs[k].shape).astype(bf16)
+        k_refs[k][...] = jnp.dot(every, w_key_ref[...], preferred_element_type=f32).astype(bf16)
+        v_refs[k][...] = jnp.dot(every, w_value_gate_ref[:, :channels], preferred_element_type=f32).astype(bf16)
+
+
+def tail_kernel(sets, per_set, heads, slab, attends, me_ref, *refs):
+    tri_refs = refs[:sets]
+    pair_ref, gate_ref, w_tri_out_ref, w_in_ref, w_down_ref, w_bias_ref = refs[sets : sets + 6]
+    if attends:
+        new_ref, single_ref, bias_ref, w_rel_ref, wb_ref = refs[-5:]
+    else:
+        new_ref, bias_ref, w_rel_ref, wb_ref = refs[-4:]
+    width = pair_ref.shape[-1]
+    columns = math.prod(pair_ref.shape[1:-1])
+    together = LANES // columns
+    inner_width = w_down_ref.shape[0]
+    me = me_ref[0]
+
+    @pl.when(pl.program_id(0) == 0)
+    def _():
+        own_set = lax.rem(me, sets)
+        for a in range(sets):
+            w_rel_ref[a * per_set : (a + 1) * per_set] = w_tri_out_ref[lax.bitwise_xor(own_set, a)]
+        wb_ref[...] = w_bias_ref[...].T
+
+    low = first_half_lanes((per_set // 2, LANES))
+
+    def sums_of(i):
+        parts = []
+        for r in tri_refs:
+            if together == 1:
+                parts.append(r[i].astype(f32))
+            else:
+                here, there = r[i].astype(f32), r[i + 1].astype(f32)
+                parts.append(jnp.where(low, here, pltpu.roll(there, LANES // 2, 1)))
+                parts.append(jnp.where(low, pltpu.roll(here, LANES // 2, 1), there))
+        return jnp.concatenate(parts, axis=0)
+
+    def rows(b, carry):
+        i = b * slab * together
+        tri = []
+        for n in range(slab):
+            tri.append(layer_norm(sums_of(i + n * together), 0).astype(bf16).T)
+        tri = jnp.concatenate(tri, axis=0)
+        tri_out = jnp.dot(tri, w_rel_ref[...], preferred_element_type=f32)
+        here = pl.ds(i, slab * together)
+        block = (slab * LANES, width)
+        mid = pair_ref[here].reshape(block) + gate_ref[here].reshape(block) * tri_out
+        trans = layer_norm(mid, 1).astype(bf16)
+        gate_up = jnp.dot(trans, w_in_ref[...], preferred_element_type=f32)
+        gate = gate_up[:, :inner_width]
+        inner = (gate * sigmoid(gate) * gate_up[:, inner_width:]).astype(bf16)
+        new = mid + jnp.dot(inner, w_down_ref[...], preferred_element_type=f32)
+        new_ref[here] = new.reshape((slab * together,) + new_ref.shape[1:])
+        normed = layer_norm(new, 1).astype(bf16)
+        bias = lax.dot_general(wb_ref[...], normed, NT, preferred_element_type=f32)
+        for n in range(slab):
+            part = bias[:, n * LANES : (n + 1) * LANES]
+            bias_ref[i + n * together] = part
+            if together == 2:
+                bias_ref[i + n * together + 1] = pltpu.roll(part, LANES // 2, 1)
+        return carry
+
+    lax.fori_loop(0, pair_ref.shape[0] // (slab * together), rows, 0)
+    if attends:
+        attention(heads, attends, refs[sets + 6 :], bias_ref, single_ref)
+
+
+def attention(heads, n, refs, last_bias_ref, single_ref):
+    q_ref, g_ref, w_out_ref = refs[:3]
+    k_refs, v_refs, live_refs = refs[3 : 3 + n], refs[3 + n : 3 + 2 * n], refs[3 + 2 * n : 3 + 3 * n]
+    bias_refs = [*refs[3 + 3 * n : 2 + 4 * n], last_bias_ref]
+    row_count, channels = q_ref.shape
+    head_size = channels // heads
+    of_head = lax.broadcasted_iota(jnp.int32, (row_count, heads, channels), 1)
+    lane = lax.broadcasted_iota(jnp.int32, (row_count, heads, channels), 2)
+    mine = jnp.logical_and(lane >= of_head * head_size, lane < (of_head + 1) * head_size)
+    spread = jnp.where(mine, jnp.broadcast_to(q_ref[...].astype(f32)[:, None, :], mine.shape), 0.0)
+    spread = spread.reshape(row_count * heads, channels).astype(bf16)
+    scores = []
+    for k in range(n):
+        part = lax.dot_general(spread, k_refs[k][...], NT, preferred_element_type=f32)
+        bias = bias_refs[k][...].reshape(row_count * heads, LANES)[:, : part.shape[1]]
+        part = part / jnp.sqrt(f32(head_size)) + bias
+        scores.append(jnp.where(live_refs[k][...] > 0, part, f32(-1000000000.0)))
+    row_max = functools.reduce(jnp.maximum, [jnp.max(x, axis=1, keepdims=True) for x in scores])
+    weights = [jnp.exp(x - row_max) for x in scores]
+    row_sum = sum(jnp.sum(x, axis=1, keepdims=True) for x in weights)
+    attended = sum(
+        jnp.dot((x / row_sum).astype(bf16), v[...], preferred_element_type=f32) for x, v in zip(weights, v_refs)
+    )
+    attended = jnp.sum(jnp.where(mine, attended.reshape(mine.shape), 0.0), axis=1)
+    gated = (g_ref[...] * attended).astype(bf16)
+    single_ref[...] = jnp.dot(gated, w_out_ref[...], preferred_element_type=f32)
+
+
+def whole_block(shape):
+    return pl.BlockSpec(shape, lambda *_: (0,) * len(shape))
+
+
+def params():
+    return pltpu.CompilerParams(dimension_semantics=("arbitrary",))
+
+
+def anywhere(arrays):
+    return [pl.BlockSpec(memory_space=pl.ANY)] * len(arrays)
+
+
+def cost(flops):
+    return pl.CostEstimate(flops=int(flops), bytes_accessed=4000000, transcendentals=0)
+
+
+def exchange(x, groups, s):
+    return x if s == 0 else lax.ppermute(x, "row", [(r, r ^ s) for r in range(groups)])
+
+
+def chunk_tiles(tiles, groups):
+    most = LANES // (groups * SUB)
+    chunks = [most] * (tiles // most) if most else []
+    return chunks + ([tiles % most] if most and tiles % most else [])
+
+
+def fast_body(
+    pair, single, token_mask, w_tri_proj, w_tri_gate, w_tri_out, w_trans_in, w_trans_out, w_bias, w_query, w_key, w_value_gate, w_out
+):
+    row_count, length, width = pair.shape
+    groups = lax.axis_size("row")
+    sets = groups // 2
+    hidden = w_tri_out.shape[0]
+    per_set = hidden // sets
+    message = per_set * 3 // 2
+    inner_width = w_trans_out.shape[0]
+    heads = w_bias.shape[1]
+    channels = single.shape[1]
+    slabs = channels // LANES
+    full = length // LANES * LANES
+    lanes = full + LANES
+    tiles = row_count // SUB
+    chunks = chunk_tiles(tiles, groups)
+    starts = [sum(chunks[:k]) for k in range(len(chunks))]
+    me = lax.axis_index("row").astype(jnp.int32).reshape(1)
+    live = token_mask.astype(f32)
+    sds = jax.ShapeDtypeStruct
+    message_block = lambda n: pl.BlockSpec((n, 1, SUB, LANES), lambda g, *_: (0, g, 0, 0))
+    edge_scratch = [pltpu.VMEM((SUB * (hidden + SUB), LANES), f32)] * 2 + [pltpu.VMEM((2 * hidden, width), bf16)]
+    edge_flops = 2 * SUB * lanes * width * 2 * hidden
+
+    def right_edges(k, after):
+        at = starts[k]
+        return pl.pallas_call(
+            functools.partial(right_kernel, hidden, full, sets, row_count, at * SUB),
+            name="right",
+            grid_spec=pltpu.PrefetchScalarGridSpec(
+                num_scalar_prefetch=2,
+                grid=(chunks[k],),
+                in_specs=[
+                    pl.BlockSpec((SUB, length, width), lambda g, *_: (at + g, 0, 0)),
+                    pl.BlockSpec((SUB, channels), lambda g, *_: (at + g, 0)),
+                    whole_block((length,)),
+                    pl.BlockSpec((width, 2 * hidden), lambda *_: (0, 1)),
+                ]
+                + anywhere(after),
+                out_specs=[message_block(message + slabs)] * sets,
+                scratch_shapes=edge_scratch,
+            ),
+            out_shape=[sds((message + slabs, chunks[k], SUB, LANES), bf16)] * sets,
+            compiler_params=params(),
+            cost_estimate=cost(edge_flops * chunks[k]),
+        )(me, token_mask, pair, single, token_mask, w_tri_proj, *after)
+
+    def left_edges(after):
+        return pl.pallas_call(
+            functools.partial(left_kernel, hidden, full, sets, row_count),
+            name="left",
+            grid_spec=pltpu.PrefetchScalarGridSpec(
+                num_scalar_prefetch=2,
+                grid=(tiles,),
+                in_specs=[
+                    pl.BlockSpec((SUB, length, width), lambda g, *_: (g, 0, 0)),
+                    whole_block((length,)),
+                    pl.BlockSpec((width, 2 * hidden), lambda *_: (0, 0)),
+                ]
+                + anywhere(after),
+                out_specs=[message_block(message)] * sets,
+                scratch_shapes=edge_scratch,
+            ),
+            out_shape=[sds((message, tiles, SUB, LANES), bf16)] * sets,
+            compiler_params=params(),
+            cost_estimate=cost(edge_flops * tiles),
+        )(me, token_mask, pair, token_mask, w_tri_proj, *after)
+
+    right_in, left_in, after = [], None, []
+    for k in range(len(chunks)):
+        right = right_edges(k, after)
+        right_in.append([exchange(right[s % sets], groups, s) for s in range(groups)])
+        after = [right[0]]
+        if left_in is None:
+            left = left_edges(after)
+            left_in = [exchange(left[s], groups, s) for s in range(sets)]
+            after = [left[0]]
+
+    gate_pair = pl.pallas_call(
+        gate_kernel,
+        name="gate",
+        grid=(tiles,),
+        in_specs=[pl.BlockSpec((SUB, length, width), lambda g: (g, 0, 0)), whole_block((width, width))] + anywhere(after),
+        out_specs=pl.BlockSpec((SUB, length, width), lambda g: (g, 0, 0)),
+        out_shape=sds(pair.shape, f32),
+        compiler_params=params(),
+        cost_estimate=cost(2 * row_count * length * width * width),
+    )(pair, w_tri_gate, *after)
+
+    total = sets * row_count
+    tri_in = []
+    for k in range(len(chunks)):
+        columns = groups * chunks[k] * SUB
+        sums_shape = (row_count, per_set * columns // LANES, LANES)
+        sums = pl.pallas_call(
+            functools.partial(triangle_kernel, groups, sets, per_set),
+            name="triangle",
+            grid_spec=pltpu.PrefetchScalarGridSpec(
+                num_scalar_prefetch=1,
+                grid=(1,),
+                in_specs=[whole_block((message, chunks[k], SUB, LANES))] * groups
+                + [whole_block((message, tiles, SUB, LANES))] * sets
+                + anywhere([gate_pair]),
+                out_specs=[whole_block(sums_shape)] * sets,
+                scratch_shapes=[
+                    pltpu.VMEM((per_set, groups, chunks[k] * SUB, LANES), f32),
+                    pltpu.VMEM((per_set // 2, groups, chunks[k] * SUB, LANES), f32),
+                    pltpu.VMEM((per_set * (total + SUB), LANES), f32),
+                ],
+            ),
+            out_shape=[sds(sums_shape, bf16)] * sets,
+            compiler_params=params(),
+            cost_estimate=cost(2 * per_set * total * lanes * LANES),
+        )(me, *right_in[k], *left_in, gate_pair)
+        tri_in.append([exchange(sums[a], groups, a) for a in range(sets)])
+
+    tokens = [groups * n * SUB for n in chunks]
+    queries, att_gate, *keys_values = pl.pallas_call(
+        functools.partial(attention_in_kernel, groups, chunks),
+        name="attention_in",
+        grid_spec=pltpu.PrefetchScalarGridSpec(
+            num_scalar_prefetch=1,
+            grid=(1,),
+            in_specs=[
+                pl.BlockSpec((slabs, n, SUB, LANES), lambda *_: (message // slabs, 0, 0, 0))
+                for n in chunks
+                for _ in range(groups)
+            ]
+            + [whole_block(w_query.shape), whole_block(w_key.shape), whole_block(w_value_gate.shape)],
+            out_specs=[whole_block((row_count, channels))] * 2 + [whole_block((n, channels)) for n in tokens + tokens],
+            scratch_shapes=[pltpu.VMEM((groups, n * SUB, channels), f32) for n in chunks],
+        ),
+        out_shape=[sds((row_count, channels), bf16), sds((row_count, channels), f32)]
+        + [sds((n, channels), bf16) for n in tokens + tokens],
+        compiler_params=params(),
+        cost_estimate=cost(2 * length * channels * channels * 3),
+    )(me, *[x for part in right_in for x in part], w_query, w_key, w_value_gate)
+
+    tiled = (row_count, groups, tiles, SUB, width)
+    pair_tiled, gate_tiled = pair.reshape(tiled), gate_pair.reshape(tiled)
+    new, biases = None, []
+    lives = [
+        live.reshape(groups, tiles, SUB)[:, at : at + n].reshape(1, groups * n * SUB) for at, n in zip(starts, chunks)
+    ]
+    for k, n in enumerate(chunks):
+        attends = len(chunks) if k == len(chunks) - 1 else 0
+        columns = tokens[k]
+        together = LANES // columns
+        take = row_count if attends else SUB
+        slab = take // together
+        at = starts[k] // n
+        part_rows = pl.BlockSpec((take, groups, n, SUB, width), lambda g, *_, at=at: (g, 0, at, 0, 0))
+        operands = [*tri_in[k], pair_tiled, gate_tiled, w_tri_out.reshape(sets, per_set, width), w_trans_in, w_trans_out, w_bias]
+        sums_block = (take,) + tri_in[k][0].shape[1:]
+        in_specs = [pl.BlockSpec(sums_block, lambda g, *_: (g, 0, 0))] * sets + [part_rows, part_rows]
+        if attends:
+            operands += [queries, att_gate, w_out, *keys_values, *lives, *biases]
+        in_specs += [whole_block(x.shape) for x in operands[sets + 2 :]]
+        aliases = {}
+        if new is not None:
+            aliases = {1 + len(operands): 0}
+            operands.append(new)
+            in_specs += anywhere([new])
+        bias_shape = (row_count, heads, LANES)
+        weights = [pltpu.VMEM((hidden, width), bf16), pltpu.VMEM((heads, width), bf16)]
+        new, last = pl.pallas_call(
+            functools.partial(tail_kernel, sets, per_set, heads, slab, attends),
+            name="tail",
+            grid_spec=pltpu.PrefetchScalarGridSpec(
+                num_scalar_prefetch=1,
+                grid=(row_count // take,),
+                in_specs=in_specs,
+                out_specs=[
+                    part_rows,
+                    whole_block(single.shape) if attends else pl.BlockSpec((SUB, heads, LANES), lambda g, *_: (g, 0, 0)),
+                ],
+                scratch_shapes=([pltpu.VMEM(bias_shape, f32)] if attends else []) + weights,
+            ),
+            out_shape=[sds(tiled, f32), sds(single.shape if attends else bias_shape, f32)],
+            input_output_aliases=aliases,
+            compiler_params=params(),
+            cost_estimate=cost(2 * row_count * columns * width * (hidden + 3 * inner_width)),
+        )(me, *operands)
+        biases.append(last)
+    return new.reshape(pair.shape), last
+
+
 def triangle(pieces):
     left_op, right_op = pieces
     return jnp.einsum("gcik,gcjk->gcij", left_op, right_op, preferred_element_type=jnp.float32)
 
 
-def body(
+def plain_body(
     pair,
     single,
     token_mask,
@@ -130,6 +592,29 @@
     return (pair_new, single_update)
 
 
+def body(*arrays):
+    pair, single, w_tri_out = arrays[0], arrays[1], arrays[5]
+    row_count, length, _ = pair.shape
+    groups = lax.axis_size("row")
+    hidden = w_tri_out.shape[0]
+    sets = groups // 2
+    packs = (
+        groups >= 4
+        and groups & (groups - 1) == 0
+        and hidden % (32 * sets) == 0
+        and (length % LANES) * 2 == LANES
+        and length // LANES == 1
+        and row_count % SUB == 0
+        and single.shape[1] % LANES == 0
+        and (hidden // sets * 3 // 2) % (single.shape[1] // LANES) == 0
+        and all(groups * n * SUB in (LANES, LANES // 2) for n in chunk_tiles(row_count // SUB, groups))
+        and bool(chunk_tiles(row_count // SUB, groups))
+    )
+    if not packs:
+        return plain_body(*arrays)
+    return fast_body(*arrays)
+
+
 def solution(mesh):
     in_specs = (
         P(("crop", "row"), None, None),

time: 206 us -> 113 us (0.55)
  blocking collectives: 57.2 us -> 0 us
  waiting for transfers between devices: 69.1 us -> 19 us
  Pallas kernels: 0 us -> 43.3 us
  starting transfers between devices: 15.4 us -> 44.1 us
  matrix products: 24.4 us -> 0 us
  other arithmetic: 23.8 us -> 0.01 us
  local copies, waits for them, and re-layouts: 14.4 us -> 4.81 us
    all_to_all x3 -> x0, waiting for transfers between devices: 69.1 us -> none  [the longest x1 34.8 us: body(): lax.all_to_all(right_edge, 'row', split_axis=0, concat_axis=2, tiled=True)]
    all_gather x1 -> x0, blocking collectives: 57.2 us -> none  [body(): normed_all = lax.all_gather(single_normed, 'row', axis=0, tiled=True)]
    ppermute x0 -> x23, starting transfers between devices: none -> 44.1 us  [exchange(): lax.ppermute(x, 'row', [(r, r ^ s) for r in range(groups)])]
    pallas_call x0 -> x9, Pallas kernels: none -> 43.3 us  [the longest x2 14.3 us: fast_body(): pl.pallas_call(functools.partial(tail_kernel, sets, per_set, heads, slab,...]
    dot_general x18 -> x0, matrix products: 24.4 us -> none  [the longest x3 5.6 us: transition(): jnp.einsum('ijf,fc->ijc', inner_act, w_trans_out, preferred_element_type=...]
    ppermute x0 -> x23, waiting for transfers between devices: none -> 19 us  [exchange(): lax.ppermute(x, 'row', [(r, r ^ s) for r in range(groups)])]
    reduce_sum x14 -> x0, other arithmetic: 16.6 us -> none  [the longest x7 8.52 us: layer_norm(): spread = jnp.mean(centered * centered, axis=along, keepdims=True)]
    all_to_all x3 -> x0, starting transfers between devices: 15.4 us -> none  [the longest x1 7.31 us: body(): lax.all_to_all(left_edge, 'row', split_axis=0, concat_axis=2, tiled=True)]
  transfers between devices with their start and end apart: 3 -> 23, of which waited for: 2 -> 3; matrix products, arithmetic and copies ran while one was open for 6% -> 2% of each run, Pallas kernels for 0% -> 29%
where the time goes in v1:
time: 113 us; the launch traced here: 112 us
  starting transfers between devices  44.1 us (39%)
  Pallas kernels  43.3 us (38%)
  waiting for transfers between devices  19 us (17%)
  local copies, waits for them, and re-layouts  4.81 us (4%)
    ppermute x23, starting transfers between devices, exchange(): lax.ppermute(x, 'row', [(r, r ^ s) for r in range(groups)])  44.1 us
    ppermute x23, waiting for transfers between devices, exchange(): lax.ppermute(x, 'row', [(r, r ^ s) for r in range(groups)])  19 us
    pallas_call x2, Pallas kernels, fast_body(): pl.pallas_call(functools.partial(tail_kernel, sets, per_set, heads, slab,...  14.3 us
    pallas_call x2, Pallas kernels, right_edges(): pl.pallas_call(functools.partial(right_kernel, hidden, full, sets, row_co...  8.58 us
    pallas_call x2, Pallas kernels, fast_body(): pl.pallas_call(functools.partial(triangle_kernel, groups, sets, per_set),...  7.21 us
    pallas_call x1, Pallas kernels, left_edges(): pl.pallas_call(functools.partial(left_kernel, hidden, full, sets, row_cou...  6.02 us
    pallas_call x1, Pallas kernels, fast_body(): pl.pallas_call(gate_kernel, name='gate', grid=(tiles,), in_specs=[pl.Bloc...  4.75 us
    unnamed x59, local copies, waits for them, and re-layouts  3.41 us
  transfers between devices with their start and end apart: 23, of which 3 were waited for; matrix products, arithmetic and copies ran while one was open for 2% of the time, Pallas kernels for 29%

profile of v1, /device:TPU:0, one launch (start us, length us, event | category | flops | bytes accessed | tf_op | source)
XLA Modules:
  0.0 112.2 jit_solution(7314442180448994887)
XLA Ops:
  0.6 4.9 %right.2 = (bf16[51,2,8,128]{3,2,1,0:T(8,128)(2,1)}, bf16[51,2,8,128]{3,2,1,0:T(8,128)(2,1)}, bf16[51,2,8,128]{3,2,1,0:T(8,128)(2,1)}, bf16[51,2,8,128]{3,2,1,0:T(8,128)(2,1)}) custom-call(s32[1]{0:T(128)} %bitcast.me_ref, s32[192]{0:T(256)} %live_ref.5, f32[24,192,128]{2,1,0:T(8,128)} %pair_ref.7, f32[24,384]{1,0:T(8,128)} %single_ref.3, s32[192]{0:T(256)} %live_ref.5, ...), custom_call_target="tpu_custom_call" | custom-call | flops 268435456 | bytes 4000000 | tf_op jit(solution)/shard_map/right/pallas_call | solution.py:319
  5.5 5.1 %collective-permute-start.17 = (bf16[51,2,8,128]{3,2,1,0:T(8,128)(2,1)}, bf16[51,2,8,128]{3,2,1,0:T(8,128)(2,1)S(1)}, u32[]{:S(2)}, u32[]{:S(2)}) collective-permute-start(bf16[51,2,8,128]{3,2,1,0:T(8,128)(2,1)} %get-tuple-element.45), channel_id=1, source_target_pairs={{0,5},{1,4},{2,7},{3,6},{4,1},{5,0},{6,3},{7,2},{8,13},{9,12},{10,... | collective-permute-start | bytes 626696 | tf_op jit(solution)/shard_map/ppermute | solution.py:283
  11.1 1.4 %collective-permute-start.18 = (bf16[51,2,8,128]{3,2,1,0:T(8,128)(2,1)}, bf16[51,2,8,128]{3,2,1,0:T(8,128)(2,1)S(1)}, u32[]{:S(2)}, u32[]{:S(2)}) collective-permute-start(bf16[51,2,8,128]{3,2,1,0:T(8,128)(2,1)} %get-tuple-element.46), channel_id=1, source_target_pairs={{0,6},{1,7},{2,4},{3,5},{4,2},{5,3},{6,0},{7,1},{8,14},{9,15},{10,... | collective-permute-start | bytes 626696 | tf_op jit(solution)/shard_map/ppermute | solution.py:283
  12.7 3.9 %collective-permute-start.19 = (bf16[51,2,8,128]{3,2,1,0:T(8,128)(2,1)}, bf16[51,2,8,128]{3,2,1,0:T(8,128)(2,1)S(1)}, u32[]{:S(2)}, u32[]{:S(2)}) collective-permute-start(bf16[51,2,8,128]{3,2,1,0:T(8,128)(2,1)} %get-tuple-element.47), channel_id=1, source_target_pairs={{0,7},{1,6},{2,5},{3,4},{4,3},{5,2},{6,1},{7,0},{8,15},{9,14},{10,... | collective-permute-start | bytes 626696 | tf_op jit(solution)/shard_map/ppermute | solution.py:283
  16.6 6.0 %left.1 = (bf16[48,3,8,128]{3,2,1,0:T(8,128)(2,1)}, bf16[48,3,8,128]{3,2,1,0:T(8,128)(2,1)}, bf16[48,3,8,128]{3,2,1,0:T(8,128)(2,1)}, bf16[48,3,8,128]{3,2,1,0:T(8,128)(2,1)}) custom-call(s32[1]{0:T(128)} %bitcast.me_ref, s32[192]{0:T(256)} %live_ref.5, f32[24,192,128]{2,1,0:T(8,128)} %pair_ref.7, s32[192]{0:T(256)} %live_ref.5, bf16[128,512]{1,0:T(8,128)(2,1)} %w_ref.5, ...), custom_call_target="tpu_custom_call" | custom-call | flops 402653184 | bytes 4000000 | tf_op jit(solution)/shard_map/left/pallas_call | solution.py:341
  22.6 4.1 %collective-permute-done.17.refs_5_ = bf16[51,2,8,128]{3,2,1,0:T(8,128)(2,1)S(1)} collective-permute-done((bf16[51,2,8,128]{3,2,1,0:T(8,128)(2,1)}, bf16[51,2,8,128]{3,2,1,0:T(8,128)(2,1)S(1)}, u32[]{:S(2)}, u32[]{:S(2)}) %collective-permute-start.17) | collective-permute-done | bytes 208928 | tf_op jit(solution)/shard_map/ppermute | solution.py:283
  26.7 2.0 %collective-permute-start.7 = (bf16[48,3,8,128]{3,2,1,0:T(8,128)(2,1)}, bf16[48,3,8,128]{3,2,1,0:T(8,128)(2,1)S(1)}, u32[]{:S(2)}, u32[]{:S(2)}) collective-permute-start(bf16[48,3,8,128]{3,2,1,0:T(8,128)(2,1)} %get-tuple-element.38), channel_id=1, source_target_pairs={{0,1},{1,0},{2,3},{3,2},{4,5},{5,4},{6,7},{7,6},{8,9},{9,8},{10,11... | collective-permute-start | bytes 884744 | tf_op jit(solution)/shard_map/ppermute | solution.py:283
  28.7 6.6 %collective-permute-start.9 = (bf16[48,3,8,128]{3,2,1,0:T(8,128)(2,1)}, bf16[48,3,8,128]{3,2,1,0:T(8,128)(2,1)S(1)}, u32[]{:S(2)}, u32[]{:S(2)}) collective-permute-start(bf16[48,3,8,128]{3,2,1,0:T(8,128)(2,1)} %get-tuple-element.40), channel_id=1, source_target_pairs={{0,3},{1,2},{2,1},{3,0},{4,7},{5,6},{6,5},{7,4},{8,11},{9,10},{10,... | collective-permute-start | bytes 884744 | tf_op jit(solution)/shard_map/ppermute | solution.py:283
  35.5 6.2 %collective-permute-start.16 = (bf16[51,2,8,128]{3,2,1,0:T(8,128)(2,1)S(1)}, bf16[51,2,8,128]{3,2,1,0:T(8,128)(2,1)S(1)}, u32[]{:S(2)}, u32[]{:S(2)}) collective-permute-start(bf16[51,2,8,128]{3,2,1,0:T(8,128)(2,1)S(1)} %copy-done), channel_id=1, source_target_pairs={{0,4},{1,5},{2,6},{3,7},{4,0},{5,1},{6,2},{7,3},{8,12},{9,13},{10,... | collective-permute-start | bytes 626696 | tf_op jit(solution)/shard_map/ppermute | solution.py:283
  41.7 3.7 %right.3 = (bf16[51,1,8,128]{3,2,1,0:T(8,128)(2,1)}, bf16[51,1,8,128]{3,2,1,0:T(8,128)(2,1)}, bf16[51,1,8,128]{3,2,1,0:T(8,128)(2,1)}, bf16[51,1,8,128]{3,2,1,0:T(8,128)(2,1)}) custom-call(s32[1]{0:T(128)} %bitcast.me_ref, s32[192]{0:T(256)} %live_ref.5, f32[24,192,128]{2,1,0:T(8,128)} %pair_ref.7, f32[24,384]{1,0:T(8,128)} %single_ref.3, s32[192]{0:T(256)} %live_ref.5, ...), custom_call_target="tpu_custom_call" | custom-call | flops 134217728 | bytes 4000000 | tf_op jit(solution)/shard_map/right/pallas_call | solution.py:319
  45.4 8.2 %collective-permute-done.15.refs_3_ = bf16[51,2,8,128]{3,2,1,0:T(8,128)(2,1)S(1)} collective-permute-done((bf16[51,2,8,128]{3,2,1,0:T(8,128)(2,1)S(1)}, bf16[51,2,8,128]{3,2,1,0:T(8,128)(2,1)S(1)}, u32[]{:S(2)}, u32[]{:S(2)}) %collective-permute-start.15) | collective-permute-done | bytes 208928 | tf_op jit(solution)/shard_map/ppermute | solution.py:283
  53.6 1.6 %collective-permute-start.4 = (bf16[51,1,8,128]{3,2,1,0:T(8,128)(2,1)}, bf16[51,1,8,128]{3,2,1,0:T(8,128)(2,1)S(1)}, u32[]{:S(2)}, u32[]{:S(2)}) collective-permute-start(bf16[51,1,8,128]{3,2,1,0:T(8,128)(2,1)} %get-tuple-element.35), channel_id=1, source_target_pairs={{0,5},{1,4},{2,7},{3,6},{4,1},{5,0},{6,3},{7,2},{8,13},{9,12},{10,... | collective-permute-start | bytes 313352 | tf_op jit(solution)/shard_map/ppermute | solution.py:283
  55.7 2.0 %collective-permute-start.5 = (bf16[51,1,8,128]{3,2,1,0:T(8,128)(2,1)}, bf16[51,1,8,128]{3,2,1,0:T(8,128)(2,1)S(1)}, u32[]{:S(2)}, u32[]{:S(2)}) collective-permute-start(bf16[51,1,8,128]{3,2,1,0:T(8,128)(2,1)} %get-tuple-element.36), channel_id=1, source_target_pairs={{0,6},{1,7},{2,4},{3,5},{4,2},{5,3},{6,0},{7,1},{8,14},{9,15},{10,... | collective-permute-start | bytes 313352 | tf_op jit(solution)/shard_map/ppermute | solution.py:283
  57.7 1.5 %collective-permute-start.1 = (bf16[51,1,8,128]{3,2,1,0:T(8,128)(2,1)}, bf16[51,1,8,128]{3,2,1,0:T(8,128)(2,1)S(1)}, u32[]{:S(2)}, u32[]{:S(2)}) collective-permute-start(bf16[51,1,8,128]{3,2,1,0:T(8,128)(2,1)} %get-tuple-element.36), channel_id=1, source_target_pairs={{0,2},{1,3},{2,0},{3,1},{4,6},{5,7},{6,4},{7,5},{8,10},{9,11},{10,... | collective-permute-start | bytes 313352 | tf_op jit(solution)/shard_map/ppermute | solution.py:283
  59.2 2.8 %collective-permute-start.6 = (bf16[51,1,8,128]{3,2,1,0:T(8,128)(2,1)}, bf16[51,1,8,128]{3,2,1,0:T(8,128)(2,1)S(1)}, u32[]{:S(2)}, u32[]{:S(2)}) collective-permute-start(bf16[51,1,8,128]{3,2,1,0:T(8,128)(2,1)} %get-tuple-element.37), channel_id=1, source_target_pairs={{0,7},{1,6},{2,5},{3,4},{4,3},{5,2},{6,1},{7,0},{8,15},{9,14},{10,... | collective-permute-start | bytes 313352 | tf_op jit(solution)/shard_map/ppermute | solution.py:283
  62.0 4.7 %gate.1.refs_12_ = f32[24,192,128]{2,1,0:T(8,128)} custom-call(f32[24,192,128]{2,1,0:T(8,128)} %pair_ref.7, bf16[128,128]{1,0:T(8,128)(2,1)} %w_gate_ref.1, bf16[51,1,8,128]{3,2,1,0:T(8,128)(2,1)} %get-tuple-element.34._.refs_0_.refs_8_), custom_call_target="tpu_custom_call" | custom-call | flops 150994944 | bytes 4000000 | tf_op jit(solution)/shard_map/gate/pallas_call | solution.py:371
  66.9 3.9 %triangle.3 = (bf16[24,32,128]{2,1,0:T(8,128)(2,1)}, bf16[24,32,128]{2,1,0:T(8,128)(2,1)}, bf16[24,32,128]{2,1,0:T(8,128)(2,1)}, bf16[24,32,128]{2,1,0:T(8,128)(2,1)}) custom-call(s32[1]{0:T(128)} %bitcast.me_ref, bf16[51,2,8,128]{3,2,1,0:T(8,128)(2,1)} %get-tuple-element.32.rest_0_.refs_0_, bf16[51,2,8,128]{3,2,1,0:T(8,128)(2,1)} %copy-done.6, ...), custom_call_target="tpu_custom_call" | custom-call | flops 201326592 | bytes 4000000 | tf_op jit(solution)/shard_map/triangle/pallas_call | solution.py:387
  70.8 1.6 %collective-permute-start.20 = (bf16[24,32,128]{2,1,0:T(8,128)(2,1)}, bf16[24,32,128]{2,1,0:T(8,128)(2,1)S(1)}, u32[]{:S(2)}, u32[]{:S(2)}) collective-permute-start(bf16[24,32,128]{2,1,0:T(8,128)(2,1)} %get-tuple-element.55), channel_id=1, source_target_pairs={{0,1},{1,0},{2,3},{3,2},{4,5},{5,4},{6,7},{7,6},{8,9},{9,8},{10,11... | collective-permute-start | bytes 589832 | tf_op jit(solution)/shard_map/ppermute | solution.py:283
  72.4 1.9 %collective-permute-start.22 = (bf16[24,32,128]{2,1,0:T(8,128)(2,1)}, bf16[24,32,128]{2,1,0:T(8,128)(2,1)S(1)}, u32[]{:S(2)}, u32[]{:S(2)}) collective-permute-start(bf16[24,32,128]{2,1,0:T(8,128)(2,1)} %get-tuple-element.57), channel_id=1, source_target_pairs={{0,3},{1,2},{2,1},{3,0},{4,7},{5,6},{6,5},{7,4},{8,11},{9,10},{10,... | collective-permute-start | bytes 589832 | tf_op jit(solution)/shard_map/ppermute | solution.py:283
  75.1 1.1 collective-permute-start.2
  76.2 1.5 %collective-permute-start.3 = (bf16[51,1,8,128]{3,2,1,0:T(8,128)(2,1)S(1)}, bf16[51,1,8,128]{3,2,1,0:T(8,128)(2,1)S(1)}, u32[]{:S(2)}, u32[]{:S(2)}) collective-permute-start(bf16[51,1,8,128]{3,2,1,0:T(8,128)(2,1)S(1)} %copy-done.4), channel_id=1, source_target_pairs={{0,4},{1,5},{2,6},{3,7},{4,0},{5,1},{6,2},{7,3},{8,12},{9,13},{10,... | collective-permute-start | bytes 313352 | tf_op jit(solution)/shard_map/ppermute | solution.py:283
  77.7 0.7 reshape.36.refs_18_
  78.4 0.7 copy.20.refs_9_
  79.1 6.7 %collective-permute-done.2.refs_3_.refs_11_ = bf16[51,1,8,128]{3,2,1,0:T(8,128)(2,1)S(1)} collective-permute-done((bf16[51,1,8,128]{3,2,1,0:T(8,128)(2,1)S(1)}, bf16[51,1,8,128]{3,2,1,0:T(8,128)(2,1)S(1)}, u32[]{:S(2)}, u32[]{:S(2)}) %collective-permute-start.2) | collective-permute-done | bytes 104480 | tf_op jit(solution)/shard_map/ppermute | solution.py:283
  86.5 0.6 copy-done.18
  87.1 2.5 %attention_in.1 = (bf16[24,384]{1,0:T(8,128)(2,1)}, f32[24,384]{1,0:T(8,128)}, bf16[128,384]{1,0:T(8,128)(2,1)}, bf16[64,384]{1,0:T(8,128)(2,1)}, bf16[128,384]{1,0:T(8,128)(2,1)}, /*index=5*/bf16[64,384]{1,0:T(8,128)(2,1)}) custom-call(s32[1]{0:T(128)} %bitcast.me_ref, bf16[51,2,8,128]{3,2,1,0:T(8,128)(2,1)} %get-tuple-element.32.rest_0_.refs_0_, ...), custom_call_target="tpu_custom_call" | custom-call | flops 169869312 | bytes 4000000 | tf_op jit(solution)/shard_map/attention_in/pallas_call | solution.py:410
  89.6 3.4 %triangle.2 = (bf16[24,16,128]{2,1,0:T(8,128)(2,1)}, bf16[24,16,128]{2,1,0:T(8,128)(2,1)}, bf16[24,16,128]{2,1,0:T(8,128)(2,1)}, bf16[24,16,128]{2,1,0:T(8,128)(2,1)}) custom-call(s32[1]{0:T(128)} %bitcast.me_ref, bf16[51,1,8,128]{3,2,1,0:T(8,128)(2,1)} %get-tuple-element.34._.refs_0_.refs_8_, bf16[51,1,8,128]{3,2,1,0:T(8,128)(2,1)} %copy-done.13, ...), custom_call_target="tpu_custom_call" | custom-call | flops 201326592 | bytes 4000000 | tf_op jit(solution)/shard_map/triangle/pallas_call | solution.py:387
  92.9 0.8 collective-permute-start.10
  93.8 2.7 %collective-permute-start.12 = (bf16[24,16,128]{2,1,0:T(8,128)(2,1)}, bf16[24,16,128]{2,1,0:T(8,128)(2,1)S(1)}, u32[]{:S(2)}, u32[]{:S(2)}) collective-permute-start(bf16[24,16,128]{2,1,0:T(8,128)(2,1)} %get-tuple-element.44), channel_id=1, source_target_pairs={{0,3},{1,2},{2,1},{3,0},{4,7},{5,6},{6,5},{7,4},{8,11},{9,10},{10,... | collective-permute-start | bytes 294920 | tf_op jit(solution)/shard_map/ppermute | solution.py:283
  96.5 0.6 copy-done.20
  97.2 8.2 %tail.2 = (f32[24,8,3,8,128]{4,3,2,1,0:T(8,128)}, f32[24,16,128]{2,1,0:T(8,128)}) custom-call(s32[1]{0:T(128)} %bitcast.me_ref, bf16[24,32,128]{2,1,0:T(8,128)(2,1)} %get-tuple-element.54.refs_0_, bf16[24,32,128]{2,1,0:T(8,128)(2,1)} %copy-done.19, bf16[24,32,128]{2,1,0:T(8,128)(2,1)} %copy-done.20, bf16[24,32,128]{2,1,0:T(8,128)(2,1)} %copy-done.21, ...), custom_call_target="tpu_custom_call" | custom-call | flops 1308622848 | bytes 4000000 | tf_op jit(solution)/shard_map/tail/pallas_call | solution.py:458
  106.1 6.1 %tail.3 = (f32[24,8,3,8,128]{4,3,2,1,0:T(8,128)}, f32[24,384]{1,0:T(8,128)}) custom-call(s32[1]{0:T(128)} %bitcast.me_ref, bf16[24,16,128]{2,1,0:T(8,128)(2,1)} %get-tuple-element.41.refs_0_, bf16[24,16,128]{2,1,0:T(8,128)(2,1)} %copy-done.22, bf16[24,16,128]{2,1,0:T(8,128)(2,1)} %copy-done.23, ...), custom_call_target="tpu_custom_call", output_to_operand_aliasing={{0}: (21, {})} | custom-call | flops 654311424 | bytes 4000000 | tf_op jit(solution)/shard_map/tail/pallas_call | solution.py:458
  (88 shorter events, 3.6 us)
Async XLA Ops:
  5.5 29.8 %copy-start.27 = (bf16[51,2,8,128]{3,2,1,0:T(8,128)(2,1)S(1)}, bf16[51,2,8,128]{3,2,1,0:T(8,128)(2,1)}, u32[]{:S(2)}) copy-start(bf16[51,2,8,128]{3,2,1,0:T(8,128)(2,1)} %get-tuple-element.47) | copy-start | bytes 626692
  5.5 29.9 %copy-start = (bf16[51,2,8,128]{3,2,1,0:T(8,128)(2,1)S(1)}, bf16[51,2,8,128]{3,2,1,0:T(8,128)(2,1)}, u32[]{:S(2)}) copy-start(bf16[51,2,8,128]{3,2,1,0:T(8,128)(2,1)} %get-tuple-element.32.rest_0_.refs_0_) | copy-start | bytes 626692
  5.5 21.1 %collective-permute-start.17 = (bf16[51,2,8,128]{3,2,1,0:T(8,128)(2,1)}, bf16[51,2,8,128]{3,2,1,0:T(8,128)(2,1)S(1)}, u32[]{:S(2)}, u32[]{:S(2)}) collective-permute-start(bf16[51,2,8,128]{3,2,1,0:T(8,128)(2,1)} %get-tuple-element.45), channel_id=1, source_target_pairs={{0,5},{1,4},{2,7},{3,6},{4,1},{5,0},{6,3},{7,2},{8,13},{9,12},{10,... | collective-permute-start | bytes 626696 | tf_op jit(solution)/shard_map/ppermute | solution.py:283
  10.6 18.1 %collective-permute-start.13 = (bf16[51,2,8,128]{3,2,1,0:T(8,128)(2,1)}, bf16[51,2,8,128]{3,2,1,0:T(8,128)(2,1)S(1)}, u32[]{:S(2)}, u32[]{:S(2)}) collective-permute-start(bf16[51,2,8,128]{3,2,1,0:T(8,128)(2,1)} %get-tuple-element.45), channel_id=1, source_target_pairs={{0,1},{1,0},{2,3},{3,2},{4,5},{5,4},{6,7},{7,6},{8,9},{9,8},{10,11... | collective-permute-start | bytes 626696 | tf_op jit(solution)/shard_map/ppermute | solution.py:283
  11.1 17.6 %collective-permute-start.18 = (bf16[51,2,8,128]{3,2,1,0:T(8,128)(2,1)}, bf16[51,2,8,128]{3,2,1,0:T(8,128)(2,1)S(1)}, u32[]{:S(2)}, u32[]{:S(2)}) collective-permute-start(bf16[51,2,8,128]{3,2,1,0:T(8,128)(2,1)} %get-tuple-element.46), channel_id=1, source_target_pairs={{0,6},{1,7},{2,4},{3,5},{4,2},{5,3},{6,0},{7,1},{8,14},{9,15},{10,... | collective-permute-start | bytes 626696 | tf_op jit(solution)/shard_map/ppermute | solution.py:283
  12.5 22.9 %collective-permute-start.14 = (bf16[51,2,8,128]{3,2,1,0:T(8,128)(2,1)}, bf16[51,2,8,128]{3,2,1,0:T(8,128)(2,1)S(1)}, u32[]{:S(2)}, u32[]{:S(2)}) collective-permute-start(bf16[51,2,8,128]{3,2,1,0:T(8,128)(2,1)} %get-tuple-element.46), channel_id=1, source_target_pairs={{0,2},{1,3},{2,0},{3,1},{4,6},{5,7},{6,4},{7,5},{8,10},{9,11},{10,... | collective-permute-start | bytes 626696 | tf_op jit(solution)/shard_map/ppermute | solution.py:283
  12.7 22.7 %collective-permute-start.19 = (bf16[51,2,8,128]{3,2,1,0:T(8,128)(2,1)}, bf16[51,2,8,128]{3,2,1,0:T(8,128)(2,1)S(1)}, u32[]{:S(2)}, u32[]{:S(2)}) collective-permute-start(bf16[51,2,8,128]{3,2,1,0:T(8,128)(2,1)} %get-tuple-element.47), channel_id=1, source_target_pairs={{0,7},{1,6},{2,5},{3,4},{4,3},{5,2},{6,1},{7,0},{8,15},{9,14},{10,... | collective-permute-start | bytes 626696 | tf_op jit(solution)/shard_map/ppermute | solution.py:283
  26.7 40.1 %copy-start.5 = (bf16[51,2,8,128]{3,2,1,0:T(8,128)(2,1)}, bf16[51,2,8,128]{3,2,1,0:T(8,128)(2,1)S(1)}, u32[]{:S(2)}) copy-start(bf16[51,2,8,128]{3,2,1,0:T(8,128)(2,1)S(1)} %collective-permute-done.17.refs_5_) | copy-start | bytes 626692
  26.7 29.0 %collective-permute-start.7 = (bf16[48,3,8,128]{3,2,1,0:T(8,128)(2,1)}, bf16[48,3,8,128]{3,2,1,0:T(8,128)(2,1)S(1)}, u32[]{:S(2)}, u32[]{:S(2)}) collective-permute-start(bf16[48,3,8,128]{3,2,1,0:T(8,128)(2,1)} %get-tuple-element.38), channel_id=1, source_target_pairs={{0,1},{1,0},{2,3},{3,2},{4,5},{5,4},{6,7},{7,6},{8,9},{9,8},{10,11... | collective-permute-start | bytes 884744 | tf_op jit(solution)/shard_map/ppermute | solution.py:283
  28.7 38.1 %copy-start.6 = (bf16[51,2,8,128]{3,2,1,0:T(8,128)(2,1)}, bf16[51,2,8,128]{3,2,1,0:T(8,128)(2,1)S(1)}, u32[]{:S(2)}) copy-start(bf16[51,2,8,128]{3,2,1,0:T(8,128)(2,1)S(1)} %collective-permute-done.13.refs_1_) | copy-start | bytes 626692
  28.7 29.0 %collective-permute-start.8 = (bf16[48,3,8,128]{3,2,1,0:T(8,128)(2,1)}, bf16[48,3,8,128]{3,2,1,0:T(8,128)(2,1)S(1)}, u32[]{:S(2)}, u32[]{:S(2)}) collective-permute-start(bf16[48,3,8,128]{3,2,1,0:T(8,128)(2,1)} %get-tuple-element.39), channel_id=1, source_target_pairs={{0,2},{1,3},{2,0},{3,1},{4,6},{5,7},{6,4},{7,5},{8,10},{9,11},{10,... | collective-permute-start | bytes 884744 | tf_op jit(solution)/shard_map/ppermute | solution.py:283
  28.7 38.0 %copy-start.7 = (bf16[51,2,8,128]{3,2,1,0:T(8,128)(2,1)}, bf16[51,2,8,128]{3,2,1,0:T(8,128)(2,1)S(1)}, u32[]{:S(2)}) copy-start(bf16[51,2,8,128]{3,2,1,0:T(8,128)(2,1)S(1)} %collective-permute-done.18.refs_6_) | copy-start | bytes 626692
  28.7 30.5 %collective-permute-start.9 = (bf16[48,3,8,128]{3,2,1,0:T(8,128)(2,1)}, bf16[48,3,8,128]{3,2,1,0:T(8,128)(2,1)S(1)}, u32[]{:S(2)}, u32[]{:S(2)}) collective-permute-start(bf16[48,3,8,128]{3,2,1,0:T(8,128)(2,1)} %get-tuple-element.40), channel_id=1, source_target_pairs={{0,3},{1,2},{2,1},{3,0},{4,7},{5,6},{6,5},{7,4},{8,11},{9,10},{10,... | collective-permute-start | bytes 884744 | tf_op jit(solution)/shard_map/ppermute | solution.py:283
  35.4 31.4 %copy-start.8 = (bf16[51,2,8,128]{3,2,1,0:T(8,128)(2,1)}, bf16[51,2,8,128]{3,2,1,0:T(8,128)(2,1)S(1)}, u32[]{:S(2)}) copy-start(bf16[51,2,8,128]{3,2,1,0:T(8,128)(2,1)S(1)} %collective-permute-done.14.refs_2_) | copy-start | bytes 626692
  35.4 18.2 %collective-permute-start.15 = (bf16[51,2,8,128]{3,2,1,0:T(8,128)(2,1)S(1)}, bf16[51,2,8,128]{3,2,1,0:T(8,128)(2,1)S(1)}, u32[]{:S(2)}, u32[]{:S(2)}) collective-permute-start(bf16[51,2,8,128]{3,2,1,0:T(8,128)(2,1)S(1)} %copy-done.27), channel_id=1, source_target_pairs={{0,3},{1,2},{2,1},{3,0},{4,7},{5,6},{6,5},{7,4},{8,11},{9,10},{10,... | collective-permute-start | bytes 626696 | tf_op jit(solution)/shard_map/ppermute | solution.py:283
  35.5 31.3 %copy-start.9 = (bf16[51,2,8,128]{3,2,1,0:T(8,128)(2,1)}, bf16[51,2,8,128]{3,2,1,0:T(8,128)(2,1)S(1)}, u32[]{:S(2)}) copy-start(bf16[51,2,8,128]{3,2,1,0:T(8,128)(2,1)S(1)} %collective-permute-done.19.refs_7_) | copy-start | bytes 626692
  35.5 19.7 %collective-permute-start.16 = (bf16[51,2,8,128]{3,2,1,0:T(8,128)(2,1)S(1)}, bf16[51,2,8,128]{3,2,1,0:T(8,128)(2,1)S(1)}, u32[]{:S(2)}, u32[]{:S(2)}) collective-permute-start(bf16[51,2,8,128]{3,2,1,0:T(8,128)(2,1)S(1)} %copy-done), channel_id=1, source_target_pairs={{0,4},{1,5},{2,6},{3,7},{4,0},{5,1},{6,2},{7,3},{8,12},{9,13},{10,... | collective-permute-start | bytes 626696 | tf_op jit(solution)/shard_map/ppermute | solution.py:283
  53.6 17.2 %collective-permute-start.4 = (bf16[51,1,8,128]{3,2,1,0:T(8,128)(2,1)}, bf16[51,1,8,128]{3,2,1,0:T(8,128)(2,1)S(1)}, u32[]{:S(2)}, u32[]{:S(2)}) collective-permute-start(bf16[51,1,8,128]{3,2,1,0:T(8,128)(2,1)} %get-tuple-element.35), channel_id=1, source_target_pairs={{0,5},{1,4},{2,7},{3,6},{4,1},{5,0},{6,3},{7,2},{8,13},{9,12},{10,... | collective-permute-start | bytes 313352 | tf_op jit(solution)/shard_map/ppermute | solution.py:283
  55.2 17.2 %collective-permute-start = (bf16[51,1,8,128]{3,2,1,0:T(8,128)(2,1)}, bf16[51,1,8,128]{3,2,1,0:T(8,128)(2,1)S(1)}, u32[]{:S(2)}, u32[]{:S(2)}) collective-permute-start(bf16[51,1,8,128]{3,2,1,0:T(8,128)(2,1)} %get-tuple-element.35), channel_id=1, source_target_pairs={{0,1},{1,0},{2,3},{3,2},{4,5},{5,4},{6,7},{7,6},{8,9},{9,8},{10,11... | collective-permute-start | bytes 313352 | tf_op jit(solution)/shard_map/ppermute | solution.py:283
  55.7 16.7 %collective-permute-start.5 = (bf16[51,1,8,128]{3,2,1,0:T(8,128)(2,1)}, bf16[51,1,8,128]{3,2,1,0:T(8,128)(2,1)S(1)}, u32[]{:S(2)}, u32[]{:S(2)}) collective-permute-start(bf16[51,1,8,128]{3,2,1,0:T(8,128)(2,1)} %get-tuple-element.36), channel_id=1, source_target_pairs={{0,6},{1,7},{2,4},{3,5},{4,2},{5,3},{6,0},{7,1},{8,14},{9,15},{10,... | collective-permute-start | bytes 313352 | tf_op jit(solution)/shard_map/ppermute | solution.py:283
  57.7 17.4 %collective-permute-start.1 = (bf16[51,1,8,128]{3,2,1,0:T(8,128)(2,1)}, bf16[51,1,8,128]{3,2,1,0:T(8,128)(2,1)S(1)}, u32[]{:S(2)}, u32[]{:S(2)}) collective-permute-start(bf16[51,1,8,128]{3,2,1,0:T(8,128)(2,1)} %get-tuple-element.36), channel_id=1, source_target_pairs={{0,2},{1,3},{2,0},{3,1},{4,6},{5,7},{6,4},{7,5},{8,10},{9,11},{10,... | collective-permute-start | bytes 313352 | tf_op jit(solution)/shard_map/ppermute | solution.py:283
  59.2 17.0 %collective-permute-start.6 = (bf16[51,1,8,128]{3,2,1,0:T(8,128)(2,1)}, bf16[51,1,8,128]{3,2,1,0:T(8,128)(2,1)S(1)}, u32[]{:S(2)}, u32[]{:S(2)}) collective-permute-start(bf16[51,1,8,128]{3,2,1,0:T(8,128)(2,1)} %get-tuple-element.37), channel_id=1, source_target_pairs={{0,7},{1,6},{2,5},{3,4},{4,3},{5,2},{6,1},{7,0},{8,15},{9,14},{10,... | collective-permute-start | bytes 313352 | tf_op jit(solution)/shard_map/ppermute | solution.py:283
  70.8 15.0 %copy-start.12 = (bf16[51,1,8,128]{3,2,1,0:T(8,128)(2,1)}, bf16[51,1,8,128]{3,2,1,0:T(8,128)(2,1)S(1)}, u32[]{:S(2)}) copy-start(bf16[51,1,8,128]{3,2,1,0:T(8,128)(2,1)S(1)} %collective-permute-done.4.refs_5_.refs_13_) | copy-start | bytes 313348
  70.8 23.0 %collective-permute-start.20 = (bf16[24,32,128]{2,1,0:T(8,128)(2,1)}, bf16[24,32,128]{2,1,0:T(8,128)(2,1)S(1)}, u32[]{:S(2)}, u32[]{:S(2)}) collective-permute-start(bf16[24,32,128]{2,1,0:T(8,128)(2,1)} %get-tuple-element.55), channel_id=1, source_target_pairs={{0,1},{1,0},{2,3},{3,2},{4,5},{5,4},{6,7},{7,6},{8,9},{9,8},{10,11... | collective-permute-start | bytes 589832 | tf_op jit(solution)/shard_map/ppermute | solution.py:283
  72.4 13.5 %copy-start.13 = (bf16[51,1,8,128]{3,2,1,0:T(8,128)(2,1)}, bf16[51,1,8,128]{3,2,1,0:T(8,128)(2,1)S(1)}, u32[]{:S(2)}) copy-start(bf16[51,1,8,128]{3,2,1,0:T(8,128)(2,1)S(1)} %collective-permute-done.refs_1_.refs_9_) | copy-start | bytes 313348
  72.4 24.1 %collective-permute-start.21 = (bf16[24,32,128]{2,1,0:T(8,128)(2,1)}, bf16[24,32,128]{2,1,0:T(8,128)(2,1)S(1)}, u32[]{:S(2)}, u32[]{:S(2)}) collective-permute-start(bf16[24,32,128]{2,1,0:T(8,128)(2,1)} %get-tuple-element.56), channel_id=1, source_target_pairs={{0,2},{1,3},{2,0},{3,1},{4,6},{5,7},{6,4},{7,5},{8,10},{9,11},{10,... | collective-permute-start | bytes 589832 | tf_op jit(solution)/shard_map/ppermute | solution.py:283
  72.4 24.1 %collective-permute-start.22 = (bf16[24,32,128]{2,1,0:T(8,128)(2,1)}, bf16[24,32,128]{2,1,0:T(8,128)(2,1)S(1)}, u32[]{:S(2)}, u32[]{:S(2)}) collective-permute-start(bf16[24,32,128]{2,1,0:T(8,128)(2,1)} %get-tuple-element.57), channel_id=1, source_target_pairs={{0,3},{1,2},{2,1},{3,0},{4,7},{5,6},{6,5},{7,4},{8,11},{9,10},{10,... | collective-permute-start | bytes 589832 | tf_op jit(solution)/shard_map/ppermute | solution.py:283
  75.1 10.7 %collective-permute-start.2 = (bf16[51,1,8,128]{3,2,1,0:T(8,128)(2,1)S(1)}, bf16[51,1,8,128]{3,2,1,0:T(8,128)(2,1)S(1)}, u32[]{:S(2)}, u32[]{:S(2)}) collective-permute-start(bf16[51,1,8,128]{3,2,1,0:T(8,128)(2,1)S(1)} %copy-done.28), channel_id=1, source_target_pairs={{0,3},{1,2},{2,1},{3,0},{4,7},{5,6},{6,5},{7,4},{8,11},{9,10},{10,... | collective-permute-start | bytes 313352 | tf_op jit(solution)/shard_map/ppermute | solution.py:283
  76.2 9.6 %collective-permute-start.3 = (bf16[51,1,8,128]{3,2,1,0:T(8,128)(2,1)S(1)}, bf16[51,1,8,128]{3,2,1,0:T(8,128)(2,1)S(1)}, u32[]{:S(2)}, u32[]{:S(2)}) collective-permute-start(bf16[51,1,8,128]{3,2,1,0:T(8,128)(2,1)S(1)} %copy-done.4), channel_id=1, source_target_pairs={{0,4},{1,5},{2,6},{3,7},{4,0},{5,1},{6,2},{7,3},{8,12},{9,13},{10,... | collective-permute-start | bytes 313352 | tf_op jit(solution)/shard_map/ppermute | solution.py:283
  92.9 12.4 %collective-permute-start.10 = (bf16[24,16,128]{2,1,0:T(8,128)(2,1)}, bf16[24,16,128]{2,1,0:T(8,128)(2,1)S(1)}, u32[]{:S(2)}, u32[]{:S(2)}) collective-permute-start(bf16[24,16,128]{2,1,0:T(8,128)(2,1)} %get-tuple-element.42), channel_id=1, source_target_pairs={{0,1},{1,0},{2,3},{3,2},{4,5},{5,4},{6,7},{7,6},{8,9},{9,8},{10,11... | collective-permute-start | bytes 294920 | tf_op jit(solution)/shard_map/ppermute | solution.py:283
  93.8 11.7 %collective-permute-start.11 = (bf16[24,16,128]{2,1,0:T(8,128)(2,1)}, bf16[24,16,128]{2,1,0:T(8,128)(2,1)S(1)}, u32[]{:S(2)}, u32[]{:S(2)}) collective-permute-start(bf16[24,16,128]{2,1,0:T(8,128)(2,1)} %get-tuple-element.43), channel_id=1, source_target_pairs={{0,2},{1,3},{2,0},{3,1},{4,6},{5,7},{6,4},{7,5},{8,10},{9,11},{10,... | collective-permute-start | bytes 294920 | tf_op jit(solution)/shard_map/ppermute | solution.py:283
  93.8 11.7 %collective-permute-start.12 = (bf16[24,16,128]{2,1,0:T(8,128)(2,1)}, bf16[24,16,128]{2,1,0:T(8,128)(2,1)S(1)}, u32[]{:S(2)}, u32[]{:S(2)}) collective-permute-start(bf16[24,16,128]{2,1,0:T(8,128)(2,1)} %get-tuple-element.44), channel_id=1, source_target_pairs={{0,3},{1,2},{2,1},{3,0},{4,7},{5,6},{6,5},{7,4},{8,11},{9,10},{10,... | collective-permute-start | bytes 294920 | tf_op jit(solution)/shard_map/ppermute | solution.py:283
  (20 other events, 130.4 us)

commit v2 on v1

--- a/solution.py
+++ b/solution.py
@@ -65,7 +65,17 @@
             out_refs[q][per_set + c, 0] = jnp.where(low, rest_ref[a, :], rest_ref[b, :]).astype(bf16)
 
 
-def right_kernel(hidden, full, sets, row_count, offset, me_ref, mask_ref, pair_ref, single_ref, live_ref, w_ref, *rest):
+def single_places(shape, tiles):
+    pieces = shape[1] // LANES * (shape[0] // SUB)
+    return {n: divmod(n, tiles) for n in range(pieces)}
+
+
+def single_slabs(shape, tiles, message):
+    least = -(-(shape[1] // LANES * (shape[0] // SUB)) // tiles)
+    return next(n for n in range(least, message + 1) if message % n == 0)
+
+
+def right_kernel(hidden, full, sets, row_count, offset, single_tiles, me_ref, mask_ref, pair_ref, single_ref, live_ref, w_ref, *rest):
     out_refs = rest[-3 - sets : -3]
     head_ref, rest_ref, wt_ref = rest[-3:]
 
@@ -76,12 +86,19 @@
     first = me_ref[0] * row_count + offset + pl.program_id(0) * SUB
     rows_of = lambda j: layer_norm(pair_ref[j], 1).astype(bf16)
     edges_to_messages(me_ref, mask_ref, live_ref, wt_ref, rows_of, head_ref, rest_ref, out_refs, first, hidden, full)
-    single_normed = layer_norm(single_ref[...], 1).astype(bf16)
-    slabs = single_ref.shape[1] // LANES
-    base = hidden // sets * 3 // 2
-    for q in range(sets):
-        for t in range(slabs):
-            out_refs[q][base + t, 0] = single_normed[:, t * LANES : (t + 1) * LANES]
+    if single_tiles:
+        single_normed = layer_norm(single_ref[...], 1)
+        base = hidden // sets * 3 // 2
+        for g in range(single_tiles):
+
+            @pl.when(pl.program_id(0) == g)
+            def _():
+                for n, (slab, tile) in single_places(single_ref.shape, single_tiles).items():
+                    if tile == g:
+                        t, at = divmod(n, row_count // SUB)
+                        part = single_normed[at * SUB : (at + 1) * SUB, t * LANES : (t + 1) * LANES].astype(bf16)
+                        for q in range(sets):
+                            out_refs[q][base + slab, 0] = part
 
 
 def left_kernel(hidden, full, sets, row_count, me_ref, mask_ref, pair_ref, live_ref, w_ref, *rest):
@@ -151,25 +168,27 @@
 
 def attention_in_kernel(groups, chunks, me_ref, *refs):
     n = len(chunks)
-    right_refs = refs[: groups * n]
-    w_query_ref, w_key_ref, w_value_gate_ref, q_ref, g_ref = refs[groups * n : groups * n + 5]
-    k_refs = refs[groups * n + 5 : groups * n + 5 + n]
-    v_refs = refs[groups * n + 5 + n : groups * n + 5 + 2 * n]
-    all_refs = refs[groups * n + 5 + 2 * n :]
+    right_refs = refs[:groups]
+    w_query_ref, w_key_ref, w_value_gate_ref, q_ref, g_ref = refs[groups : groups + 5]
+    k_refs, v_refs = refs[groups + 5 : groups + 5 + n], refs[groups + 5 + n : groups + 5 + 2 * n]
+    all_ref = refs[-1]
     channels = w_query_ref.shape[0]
     me = me_ref[0]
-    for k in range(n):
-        for s in range(groups):
-            d = lax.bitwise_xor(me, s)
-            for t in range(channels // LANES):
-                all_refs[k][d, :, t * LANES : (t + 1) * LANES] = plain_rows(right_refs[k * groups + s][t])
-    own = jnp.concatenate([r[me] for r in all_refs], axis=0).astype(bf16)
+    tiles = all_ref.shape[1] // SUB
+    for s in range(groups):
+        d = lax.bitwise_xor(me, s)
+        for place, (slab, tile) in single_places(q_ref.shape, right_refs[s].shape[1]).items():
+            t, at = divmod(place, tiles)
+            all_ref[d, at * SUB : (at + 1) * SUB, t * LANES : (t + 1) * LANES] = right_refs[s][slab, tile].astype(f32)
+    own = all_ref[me].astype(bf16)
     q_ref[...] = jnp.dot(own, w_query_ref[...], preferred_element_type=f32).astype(bf16)
     g_ref[...] = sigmoid(jnp.dot(own, w_value_gate_ref[:, channels:], preferred_element_type=f32))
+    first = 0
     for k in range(n):
-        every = all_refs[k][...].reshape(k_refs[k].shape).astype(bf16)
+        every = all_ref[:, first * SUB : (first + chunks[k]) * SUB].reshape(k_refs[k].shape).astype(bf16)
         k_refs[k][...] = jnp.dot(every, w_key_ref[...], preferred_element_type=f32).astype(bf16)
         v_refs[k][...] = jnp.dot(every, w_value_gate_ref[:, :channels], preferred_element_type=f32).astype(bf16)
+        first += chunks[k]
 
 
 def tail_kernel(sets, per_set, heads, slab, attends, me_ref, *refs):
@@ -301,7 +320,7 @@
     inner_width = w_trans_out.shape[0]
     heads = w_bias.shape[1]
     channels = single.shape[1]
-    slabs = channels // LANES
+    slabs = single_slabs(single.shape, chunk_tiles(row_count // SUB, groups)[0], message)
     full = length // LANES * LANES
     lanes = full + LANES
     tiles = row_count // SUB
@@ -316,23 +335,24 @@
 
     def right_edges(k, after):
         at = starts[k]
+        size = message + (0 if k else slabs)
         return pl.pallas_call(
-            functools.partial(right_kernel, hidden, full, sets, row_count, at * SUB),
+            functools.partial(right_kernel, hidden, full, sets, row_count, at * SUB, 0 if k else chunks[0]),
             name="right",
             grid_spec=pltpu.PrefetchScalarGridSpec(
                 num_scalar_prefetch=2,
                 grid=(chunks[k],),
                 in_specs=[
                     pl.BlockSpec((SUB, length, width), lambda g, *_: (at + g, 0, 0)),
-                    pl.BlockSpec((SUB, channels), lambda g, *_: (at + g, 0)),
+                    whole_block(single.shape),
                     whole_block((length,)),
                     pl.BlockSpec((width, 2 * hidden), lambda *_: (0, 1)),
                 ]
                 + anywhere(after),
-                out_specs=[message_block(message + slabs)] * sets,
+                out_specs=[message_block(size)] * sets,
                 scratch_shapes=edge_scratch,
             ),
-            out_shape=[sds((message + slabs, chunks[k], SUB, LANES), bf16)] * sets,
+            out_shape=[sds((size, chunks[k], SUB, LANES), bf16)] * sets,
             compiler_params=params(),
             cost_estimate=cost(edge_flops * chunks[k]),
         )(me, token_mask, pair, single, token_mask, w_tri_proj, *after)
@@ -379,20 +399,38 @@
         cost_estimate=cost(2 * row_count * length * width * width),
     )(pair, w_tri_gate, *after)
 
+    tokens = [groups * n * SUB for n in chunks]
+    queries, att_gate, *keys_values = pl.pallas_call(
+        functools.partial(attention_in_kernel, groups, chunks),
+        name="attention_in",
+        grid_spec=pltpu.PrefetchScalarGridSpec(
+            num_scalar_prefetch=1,
+            grid=(1,),
+            in_specs=[pl.BlockSpec((slabs, chunks[0], SUB, LANES), lambda *_: (message // slabs, 0, 0, 0))] * groups
+            + [whole_block(w_query.shape), whole_block(w_key.shape), whole_block(w_value_gate.shape)],
+            out_specs=[whole_block((row_count, channels))] * 2 + [whole_block((n, channels)) for n in tokens + tokens],
+            scratch_shapes=[pltpu.VMEM((groups, row_count, channels), f32)],
+        ),
+        out_shape=[sds((row_count, channels), bf16), sds((row_count, channels), f32)]
+        + [sds((n, channels), bf16) for n in tokens + tokens],
+        compiler_params=params(),
+        cost_estimate=cost(2 * length * channels * channels * 3),
+    )(me, *right_in[0], w_query, w_key, w_value_gate)
+
     total = sets * row_count
     tri_in = []
     for k in range(len(chunks)):
+        late = queries
         columns = groups * chunks[k] * SUB
         sums_shape = (row_count, per_set * columns // LANES, LANES)
         sums = pl.pallas_call(
             functools.partial(triangle_kernel, groups, sets, per_set),
-            name="triangle",
             grid_spec=pltpu.PrefetchScalarGridSpec(
                 num_scalar_prefetch=1,
                 grid=(1,),
                 in_specs=[whole_block((message, chunks[k], SUB, LANES))] * groups
                 + [whole_block((message, tiles, SUB, LANES))] * sets
-                + anywhere([gate_pair]),
+                + anywhere([late]),
                 out_specs=[whole_block(sums_shape)] * sets,
                 scratch_shapes=[
                     pltpu.VMEM((per_set, groups, chunks[k] * SUB, LANES), f32),
@@ -403,30 +441,8 @@
             out_shape=[sds(sums_shape, bf16)] * sets,
             compiler_params=params(),
             cost_estimate=cost(2 * per_set * total * lanes * LANES),
-        )(me, *right_in[k], *left_in, gate_pair)
+        )(me, *right_in[k], *left_in, late)
         tri_in.append([exchange(sums[a], groups, a) for a in range(sets)])
-
-    tokens = [groups * n * SUB for n in chunks]
-    queries, att_gate, *keys_values = pl.pallas_call(
-        functools.partial(attention_in_kernel, groups, chunks),
-        name="attention_in",
-        grid_spec=pltpu.PrefetchScalarGridSpec(
-            num_scalar_prefetch=1,
-            grid=(1,),
-            in_specs=[
-                pl.BlockSpec((slabs, n, SUB, LANES), lambda *_: (message // slabs, 0, 0, 0))
-                for n in chunks
-                for _ in range(groups)
-            ]
-            + [whole_block(w_query.shape), whole_block(w_key.shape), whole_block(w_value_gate.shape)],
-            out_specs=[whole_block((row_count, channels))] * 2 + [whole_block((n, channels)) for n in tokens + tokens],
-            scratch_shapes=[pltpu.VMEM((groups, n * SUB, channels), f32) for n in chunks],
-        ),
-        out_shape=[sds((row_count, channels), bf16), sds((row_count, channels), f32)]
-        + [sds((n, channels), bf16) for n in tokens + tokens],
-        compiler_params=params(),
-        cost_estimate=cost(2 * length * channels * channels * 3),
-    )(me, *[x for part in right_in for x in part], w_query, w_key, w_value_gate)
 
     tiled = (row_count, groups, tiles, SUB, width)
     pair_tiled, gate_tiled = pair.reshape(tiled), gate_pair.reshape(tiled)
@@ -457,7 +473,6 @@
         weights = [pltpu.VMEM((hidden, width), bf16), pltpu.VMEM((heads, width), bf16)]
         new, last = pl.pallas_call(
             functools.partial(tail_kernel, sets, per_set, heads, slab, attends),
-            name="tail",
             grid_spec=pltpu.PrefetchScalarGridSpec(
                 num_scalar_prefetch=1,
                 grid=(row_count // take,),
@@ -606,7 +621,6 @@
         and length // LANES == 1
         and row_count % SUB == 0
         and single.shape[1] % LANES == 0
-        and (hidden // sets * 3 // 2) % (single.shape[1] // LANES) == 0
         and all(groups * n * SUB in (LANES, LANES // 2) for n in chunk_tiles(row_count // SUB, groups))
         and bool(chunk_tiles(row_count // SUB, groups))
     )

time: 113 us -> 109 us (0.965)
  waiting for transfers between devices: 19 us -> 14.4 us
    ppermute x23, waiting for transfers between devices: 19 us -> 14.4 us  [exchange(): lax.ppermute(x, 'row', [(r, r ^ s) for r in range(groups)])]
  transfers between devices with their start and end apart: 23 -> 23, of which waited for: 3 -> 3; matrix products, arithmetic and copies ran while one was open for 2% -> 2% of each run, Pallas kernels for 29% -> 30%
where the time goes in v2:
time: 109 us
  starting transfers between devices  45.2 us (41%)
  Pallas kernels  43.5 us (40%)
  waiting for transfers between devices  14.4 us (13%)
  local copies, waits for them, and re-layouts  4.81 us (4%)
    ppermute x23, starting transfers between devices, exchange(): lax.ppermute(x, 'row', [(r, r ^ s) for r in range(groups)])  45.2 us
    ppermute x23, waiting for transfers between devices, exchange(): lax.ppermute(x, 'row', [(r, r ^ s) for r in range(groups)])  14.4 us
    pallas_call x2, Pallas kernels, fast_body(): pl.pallas_call(functools.partial(tail_kernel, sets, per_set, heads, slab,...  14.3 us
    pallas_call x2, Pallas kernels, right_edges(): pl.pallas_call(functools.partial(right_kernel, hidden, full, sets, row_co...  8.73 us
    pallas_call x2, Pallas kernels, fast_body(): pl.pallas_call(functools.partial(triangle_kernel, groups, sets, per_set),...  7.17 us
    pallas_call x1, Pallas kernels, left_edges(): pl.pallas_call(functools.partial(left_kernel, hidden, full, sets, row_cou...  6.02 us
    pallas_call x1, Pallas kernels, fast_body(): pl.pallas_call(gate_kernel, name='gate', grid=(tiles,), in_specs=[pl.Bloc...  4.75 us
    unnamed x59, local copies, waits for them, and re-layouts  3.43 us
  transfers between devices with their start and end apart: 23, of which 3 were waited for; matrix products, arithmetic and copies ran while one was open for 2% of the time, Pallas kernels for 30%

profile of v2, /device:TPU:0, one launch (start us, length us, event | category | flops | bytes accessed | tf_op | source)
XLA Modules:
  0.0 108.8 jit_solution(7345771907067969715)
XLA Ops:
  0.6 5.0 %right.2 = (bf16[54,2,8,128]{3,2,1,0:T(8,128)(2,1)}, bf16[54,2,8,128]{3,2,1,0:T(8,128)(2,1)}, bf16[54,2,8,128]{3,2,1,0:T(8,128)(2,1)}, bf16[54,2,8,128]{3,2,1,0:T(8,128)(2,1)}) custom-call(s32[1]{0:T(128)} %bitcast.me_ref, s32[192]{0:T(256)} %live_ref.5, f32[24,192,128]{2,1,0:T(8,128)} %pair_ref.7, f32[24,384]{1,0:T(8,128)} %single_ref.3, s32[192]{0:T(256)} %live_ref.5, ...), custom_call_target="tpu_custom_call" | custom-call | flops 268435456 | bytes 4000000 | tf_op jit(solution)/shard_map/right/pallas_call | solution.py:339
  5.7 5.1 %collective-permute-start.14 = (bf16[54,2,8,128]{3,2,1,0:T(8,128)(2,1)}, bf16[54,2,8,128]{3,2,1,0:T(8,128)(2,1)S(1)}, u32[]{:S(2)}, u32[]{:S(2)}) collective-permute-start(bf16[54,2,8,128]{3,2,1,0:T(8,128)(2,1)} %get-tuple-element.41), channel_id=1, source_target_pairs={{0,5},{1,4},{2,7},{3,6},{4,1},{5,0},{6,3},{7,2},{8,13},{9,12},{10,... | collective-permute-start | bytes 663560 | tf_op jit(solution)/shard_map/ppermute | solution.py:302
  11.3 1.3 %collective-permute-start.15 = (bf16[54,2,8,128]{3,2,1,0:T(8,128)(2,1)}, bf16[54,2,8,128]{3,2,1,0:T(8,128)(2,1)S(1)}, u32[]{:S(2)}, u32[]{:S(2)}) collective-permute-start(bf16[54,2,8,128]{3,2,1,0:T(8,128)(2,1)} %get-tuple-element.42), channel_id=1, source_target_pairs={{0,6},{1,7},{2,4},{3,5},{4,2},{5,3},{6,0},{7,1},{8,14},{9,15},{10,... | collective-permute-start | bytes 663560 | tf_op jit(solution)/shard_map/ppermute | solution.py:302
  12.9 3.9 %collective-permute-start.16 = (bf16[54,2,8,128]{3,2,1,0:T(8,128)(2,1)}, bf16[54,2,8,128]{3,2,1,0:T(8,128)(2,1)S(1)}, u32[]{:S(2)}, u32[]{:S(2)}) collective-permute-start(bf16[54,2,8,128]{3,2,1,0:T(8,128)(2,1)} %get-tuple-element.43), channel_id=1, source_target_pairs={{0,7},{1,6},{2,5},{3,4},{4,3},{5,2},{6,1},{7,0},{8,15},{9,14},{10,... | collective-permute-start | bytes 663560 | tf_op jit(solution)/shard_map/ppermute | solution.py:302
  16.7 6.0 %left.1 = (bf16[48,3,8,128]{3,2,1,0:T(8,128)(2,1)}, bf16[48,3,8,128]{3,2,1,0:T(8,128)(2,1)}, bf16[48,3,8,128]{3,2,1,0:T(8,128)(2,1)}, bf16[48,3,8,128]{3,2,1,0:T(8,128)(2,1)}) custom-call(s32[1]{0:T(128)} %bitcast.me_ref, s32[192]{0:T(256)} %live_ref.5, f32[24,192,128]{2,1,0:T(8,128)} %pair_ref.7, s32[192]{0:T(256)} %live_ref.5, bf16[128,512]{1,0:T(8,128)(2,1)} %w_ref.5, ...), custom_call_target="tpu_custom_call" | custom-call | flops 402653184 | bytes 4000000 | tf_op jit(solution)/shard_map/left/pallas_call | solution.py:361
  22.8 4.9 %collective-permute-done.14.refs_5_ = bf16[54,2,8,128]{3,2,1,0:T(8,128)(2,1)S(1)} collective-permute-done((bf16[54,2,8,128]{3,2,1,0:T(8,128)(2,1)}, bf16[54,2,8,128]{3,2,1,0:T(8,128)(2,1)S(1)}, u32[]{:S(2)}, u32[]{:S(2)}) %collective-permute-start.14) | collective-permute-done | bytes 221216 | tf_op jit(solution)/shard_map/ppermute | solution.py:302
  27.6 2.1 %collective-permute-start.7 = (bf16[48,3,8,128]{3,2,1,0:T(8,128)(2,1)}, bf16[48,3,8,128]{3,2,1,0:T(8,128)(2,1)S(1)}, u32[]{:S(2)}, u32[]{:S(2)}) collective-permute-start(bf16[48,3,8,128]{3,2,1,0:T(8,128)(2,1)} %get-tuple-element.38), channel_id=1, source_target_pairs={{0,1},{1,0},{2,3},{3,2},{4,5},{5,4},{6,7},{7,6},{8,9},{9,8},{10,11... | collective-permute-start | bytes 884744 | tf_op jit(solution)/shard_map/ppermute | solution.py:302
  29.7 7.1 %collective-permute-start.9 = (bf16[48,3,8,128]{3,2,1,0:T(8,128)(2,1)}, bf16[48,3,8,128]{3,2,1,0:T(8,128)(2,1)S(1)}, u32[]{:S(2)}, u32[]{:S(2)}) collective-permute-start(bf16[48,3,8,128]{3,2,1,0:T(8,128)(2,1)} %get-tuple-element.40), channel_id=1, source_target_pairs={{0,3},{1,2},{2,1},{3,0},{4,7},{5,6},{6,5},{7,4},{8,11},{9,10},{10,... | collective-permute-start | bytes 884744 | tf_op jit(solution)/shard_map/ppermute | solution.py:302
  36.9 6.8 %collective-permute-start.13 = (bf16[54,2,8,128]{3,2,1,0:T(8,128)(2,1)S(1)}, bf16[54,2,8,128]{3,2,1,0:T(8,128)(2,1)S(1)}, u32[]{:S(2)}, u32[]{:S(2)}) collective-permute-start(bf16[54,2,8,128]{3,2,1,0:T(8,128)(2,1)S(1)} %copy-done), channel_id=1, source_target_pairs={{0,4},{1,5},{2,6},{3,7},{4,0},{5,1},{6,2},{7,3},{8,12},{9,13},{10,... | collective-permute-start | bytes 663560 | tf_op jit(solution)/shard_map/ppermute | solution.py:302
  43.7 3.7 %right.3 = (bf16[48,1,8,128]{3,2,1,0:T(8,128)(2,1)}, bf16[48,1,8,128]{3,2,1,0:T(8,128)(2,1)}, bf16[48,1,8,128]{3,2,1,0:T(8,128)(2,1)}, bf16[48,1,8,128]{3,2,1,0:T(8,128)(2,1)}) custom-call(s32[1]{0:T(128)} %bitcast.me_ref, s32[192]{0:T(256)} %live_ref.5, f32[24,192,128]{2,1,0:T(8,128)} %pair_ref.7, f32[24,384]{1,0:T(8,128)} %single_ref.3, s32[192]{0:T(256)} %live_ref.5, ...), custom_call_target="tpu_custom_call" | custom-call | flops 134217728 | bytes 4000000 | tf_op jit(solution)/shard_map/right/pallas_call | solution.py:339
  47.4 8.0 %collective-permute-done.12.refs_3_ = bf16[54,2,8,128]{3,2,1,0:T(8,128)(2,1)S(1)} collective-permute-done((bf16[54,2,8,128]{3,2,1,0:T(8,128)(2,1)S(1)}, bf16[54,2,8,128]{3,2,1,0:T(8,128)(2,1)S(1)}, u32[]{:S(2)}, u32[]{:S(2)}) %collective-permute-start.12) | collective-permute-done | bytes 221216 | tf_op jit(solution)/shard_map/ppermute | solution.py:302
  55.3 1.6 %collective-permute-start.4 = (bf16[48,1,8,128]{3,2,1,0:T(8,128)(2,1)}, bf16[48,1,8,128]{3,2,1,0:T(8,128)(2,1)S(1)}, u32[]{:S(2)}, u32[]{:S(2)}) collective-permute-start(bf16[48,1,8,128]{3,2,1,0:T(8,128)(2,1)} %get-tuple-element.35), channel_id=1, source_target_pairs={{0,5},{1,4},{2,7},{3,6},{4,1},{5,0},{6,3},{7,2},{8,13},{9,12},{10,... | collective-permute-start | bytes 294920 | tf_op jit(solution)/shard_map/ppermute | solution.py:302
  57.4 2.0 %collective-permute-start.5 = (bf16[48,1,8,128]{3,2,1,0:T(8,128)(2,1)}, bf16[48,1,8,128]{3,2,1,0:T(8,128)(2,1)S(1)}, u32[]{:S(2)}, u32[]{:S(2)}) collective-permute-start(bf16[48,1,8,128]{3,2,1,0:T(8,128)(2,1)} %get-tuple-element.36), channel_id=1, source_target_pairs={{0,6},{1,7},{2,4},{3,5},{4,2},{5,3},{6,0},{7,1},{8,14},{9,15},{10,... | collective-permute-start | bytes 294920 | tf_op jit(solution)/shard_map/ppermute | solution.py:302
  59.4 1.5 %collective-permute-start.1 = (bf16[48,1,8,128]{3,2,1,0:T(8,128)(2,1)}, bf16[48,1,8,128]{3,2,1,0:T(8,128)(2,1)S(1)}, u32[]{:S(2)}, u32[]{:S(2)}) collective-permute-start(bf16[48,1,8,128]{3,2,1,0:T(8,128)(2,1)} %get-tuple-element.36), channel_id=1, source_target_pairs={{0,2},{1,3},{2,0},{3,1},{4,6},{5,7},{6,4},{7,5},{8,10},{9,11},{10,... | collective-permute-start | bytes 294920 | tf_op jit(solution)/shard_map/ppermute | solution.py:302
  61.0 2.8 %collective-permute-start.6 = (bf16[48,1,8,128]{3,2,1,0:T(8,128)(2,1)}, bf16[48,1,8,128]{3,2,1,0:T(8,128)(2,1)S(1)}, u32[]{:S(2)}, u32[]{:S(2)}) collective-permute-start(bf16[48,1,8,128]{3,2,1,0:T(8,128)(2,1)} %get-tuple-element.37), channel_id=1, source_target_pairs={{0,7},{1,6},{2,5},{3,4},{4,3},{5,2},{6,1},{7,0},{8,15},{9,14},{10,... | collective-permute-start | bytes 294920 | tf_op jit(solution)/shard_map/ppermute | solution.py:302
  63.9 2.5 %attention_in.1 = (bf16[24,384]{1,0:T(8,128)(2,1)}, f32[24,384]{1,0:T(8,128)}, bf16[128,384]{1,0:T(8,128)(2,1)}, bf16[64,384]{1,0:T(8,128)(2,1)}, bf16[128,384]{1,0:T(8,128)(2,1)}, /*index=5*/bf16[64,384]{1,0:T(8,128)(2,1)}) custom-call(s32[1]{0:T(128)} %bitcast.me_ref, bf16[54,2,8,128]{3,2,1,0:T(8,128)(2,1)} %get-tuple-element.32.rest_0_.refs_0_, ...), custom_call_target="tpu_custom_call" | custom-call | flops 169869312 | bytes 4000000 | tf_op jit(solution)/shard_map/attention_in/pallas_call | solution.py:403
  66.5 3.8 %shard_map.141 = (bf16[24,32,128]{2,1,0:T(8,128)(2,1)}, bf16[24,32,128]{2,1,0:T(8,128)(2,1)}, bf16[24,32,128]{2,1,0:T(8,128)(2,1)}, bf16[24,32,128]{2,1,0:T(8,128)(2,1)}) custom-call(s32[1]{0:T(128)} %bitcast.me_ref, bf16[54,2,8,128]{3,2,1,0:T(8,128)(2,1)} %get-tuple-element.32.rest_0_.refs_0_, bf16[54,2,8,128]{3,2,1,0:T(8,128)(2,1)} %copy-done.5, ...), custom_call_target="tpu_custom_call" | custom-call | flops 201326592 | bytes 4000000 | tf_op jit(solution)/shard_map/pallas_call | solution.py:426
  70.3 1.6 %collective-permute-start.20 = (bf16[24,32,128]{2,1,0:T(8,128)(2,1)}, bf16[24,32,128]{2,1,0:T(8,128)(2,1)S(1)}, u32[]{:S(2)}, u32[]{:S(2)}) collective-permute-start(bf16[24,32,128]{2,1,0:T(8,128)(2,1)} %get-tuple-element.55), channel_id=1, source_target_pairs={{0,1},{1,0},{2,3},{3,2},{4,5},{5,4},{6,7},{7,6},{8,9},{9,8},{10,11... | collective-permute-start | bytes 589832 | tf_op jit(solution)/shard_map/ppermute | solution.py:302
  71.9 1.9 %collective-permute-start.22 = (bf16[24,32,128]{2,1,0:T(8,128)(2,1)}, bf16[24,32,128]{2,1,0:T(8,128)(2,1)S(1)}, u32[]{:S(2)}, u32[]{:S(2)}) collective-permute-start(bf16[24,32,128]{2,1,0:T(8,128)(2,1)} %get-tuple-element.57), channel_id=1, source_target_pairs={{0,3},{1,2},{2,1},{3,0},{4,7},{5,6},{6,5},{7,4},{8,11},{9,10},{10,... | collective-permute-start | bytes 589832 | tf_op jit(solution)/shard_map/ppermute | solution.py:302
  74.6 1.1 %collective-permute-start.2 = (bf16[48,1,8,128]{3,2,1,0:T(8,128)(2,1)S(1)}, bf16[48,1,8,128]{3,2,1,0:T(8,128)(2,1)S(1)}, u32[]{:S(2)}, u32[]{:S(2)}) collective-permute-start(bf16[48,1,8,128]{3,2,1,0:T(8,128)(2,1)S(1)} %copy-done.28), channel_id=1, source_target_pairs={{0,3},{1,2},{2,1},{3,0},{4,7},{5,6},{6,5},{7,4},{8,11},{9,10},{10,... | collective-permute-start | bytes 294920 | tf_op jit(solution)/shard_map/ppermute | solution.py:302
  75.7 1.5 %collective-permute-start.3 = (bf16[48,1,8,128]{3,2,1,0:T(8,128)(2,1)S(1)}, bf16[48,1,8,128]{3,2,1,0:T(8,128)(2,1)S(1)}, u32[]{:S(2)}, u32[]{:S(2)}) collective-permute-start(bf16[48,1,8,128]{3,2,1,0:T(8,128)(2,1)S(1)} %copy-done.11), channel_id=1, source_target_pairs={{0,4},{1,5},{2,6},{3,7},{4,0},{5,1},{6,2},{7,3},{8,12},{9,13},{10,... | collective-permute-start | bytes 294920 | tf_op jit(solution)/shard_map/ppermute | solution.py:302
  77.3 0.6 reshape.36.refs_18_
  77.9 0.7 copy.20.refs_9_
  78.6 4.7 %gate.1 = f32[24,192,128]{2,1,0:T(8,128)} custom-call(f32[24,192,128]{2,1,0:T(8,128)} %pair_ref.7, bf16[128,128]{1,0:T(8,128)(2,1)} %w_gate_ref.1, bf16[48,1,8,128]{3,2,1,0:T(8,128)(2,1)} %get-tuple-element.34.refs_0_._), custom_call_target="tpu_custom_call" | custom-call | flops 150994944 | bytes 4000000 | tf_op jit(solution)/shard_map/gate/pallas_call | solution.py:391
  83.4 1.5 %collective-permute-done.2.refs_3_ = bf16[48,1,8,128]{3,2,1,0:T(8,128)(2,1)S(1)} collective-permute-done((bf16[48,1,8,128]{3,2,1,0:T(8,128)(2,1)S(1)}, bf16[48,1,8,128]{3,2,1,0:T(8,128)(2,1)S(1)}, u32[]{:S(2)}, u32[]{:S(2)}) %collective-permute-start.2) | collective-permute-done | bytes 98336 | tf_op jit(solution)/shard_map/ppermute | solution.py:302
  85.6 0.6 copy-done.24
  86.2 3.4 %shard_map.140 = (bf16[24,16,128]{2,1,0:T(8,128)(2,1)}, bf16[24,16,128]{2,1,0:T(8,128)(2,1)}, bf16[24,16,128]{2,1,0:T(8,128)(2,1)}, bf16[24,16,128]{2,1,0:T(8,128)(2,1)}) custom-call(s32[1]{0:T(128)} %bitcast.me_ref, bf16[48,1,8,128]{3,2,1,0:T(8,128)(2,1)} %get-tuple-element.34.refs_0_._, bf16[48,1,8,128]{3,2,1,0:T(8,128)(2,1)} %copy-done.19, ...), custom_call_target="tpu_custom_call" | custom-call | flops 201326592 | bytes 4000000 | tf_op jit(solution)/shard_map/pallas_call | solution.py:426
  89.6 0.8 collective-permute-start.17
  90.4 2.7 %collective-permute-start.19 = (bf16[24,16,128]{2,1,0:T(8,128)(2,1)}, bf16[24,16,128]{2,1,0:T(8,128)(2,1)S(1)}, u32[]{:S(2)}, u32[]{:S(2)}) collective-permute-start(bf16[24,16,128]{2,1,0:T(8,128)(2,1)} %get-tuple-element.48), channel_id=1, source_target_pairs={{0,3},{1,2},{2,1},{3,0},{4,7},{5,6},{6,5},{7,4},{8,11},{9,10},{10,... | collective-permute-start | bytes 294920 | tf_op jit(solution)/shard_map/ppermute | solution.py:302
  93.1 0.6 copy-done.13
  93.8 8.2 %shard_map.142 = (f32[24,8,3,8,128]{4,3,2,1,0:T(8,128)}, f32[24,16,128]{2,1,0:T(8,128)}) custom-call(s32[1]{0:T(128)} %bitcast.me_ref, bf16[24,32,128]{2,1,0:T(8,128)(2,1)} %get-tuple-element.54.refs_0_, bf16[24,32,128]{2,1,0:T(8,128)(2,1)} %copy-done.12, bf16[24,32,128]{2,1,0:T(8,128)(2,1)} %copy-done.13, bf16[24,32,128]{2,1,0:T(8,128)(2,1)} %copy-done.14, ...), custom_call_target="tpu_custom_call" | custom-call | flops 1308622848 | bytes 4000000 | tf_op jit(solution)/shard_map/pallas_call | solution.py:474
  102.7 6.1 %shard_map.143 = (f32[24,8,3,8,128]{4,3,2,1,0:T(8,128)}, f32[24,384]{1,0:T(8,128)}) custom-call(s32[1]{0:T(128)} %bitcast.me_ref, bf16[24,16,128]{2,1,0:T(8,128)(2,1)} %get-tuple-element.45.refs_0_, bf16[24,16,128]{2,1,0:T(8,128)(2,1)} %copy-done.15, bf16[24,16,128]{2,1,0:T(8,128)(2,1)} %copy-done.16, ...), custom_call_target="tpu_custom_call", output_to_operand_aliasing={{0}: (21, {})} | custom-call | flops 654311424 | bytes 4000000 | tf_op jit(solution)/shard_map/pallas_call | solution.py:474
  (88 shorter events, 3.6 us)
Async XLA Ops:
  5.7 31.2 %copy-start.27 = (bf16[54,2,8,128]{3,2,1,0:T(8,128)(2,1)S(1)}, bf16[54,2,8,128]{3,2,1,0:T(8,128)(2,1)}, u32[]{:S(2)}) copy-start(bf16[54,2,8,128]{3,2,1,0:T(8,128)(2,1)} %get-tuple-element.43) | copy-start | bytes 663556
  5.7 31.3 %copy-start = (bf16[54,2,8,128]{3,2,1,0:T(8,128)(2,1)S(1)}, bf16[54,2,8,128]{3,2,1,0:T(8,128)(2,1)}, u32[]{:S(2)}) copy-start(bf16[54,2,8,128]{3,2,1,0:T(8,128)(2,1)} %get-tuple-element.32.rest_0_.refs_0_) | copy-start | bytes 663556
  5.7 21.9 %collective-permute-start.14 = (bf16[54,2,8,128]{3,2,1,0:T(8,128)(2,1)}, bf16[54,2,8,128]{3,2,1,0:T(8,128)(2,1)S(1)}, u32[]{:S(2)}, u32[]{:S(2)}) collective-permute-start(bf16[54,2,8,128]{3,2,1,0:T(8,128)(2,1)} %get-tuple-element.41), channel_id=1, source_target_pairs={{0,5},{1,4},{2,7},{3,6},{4,1},{5,0},{6,3},{7,2},{8,13},{9,12},{10,... | collective-permute-start | bytes 663560 | tf_op jit(solution)/shard_map/ppermute | solution.py:302
  10.8 18.9 %collective-permute-start.10 = (bf16[54,2,8,128]{3,2,1,0:T(8,128)(2,1)}, bf16[54,2,8,128]{3,2,1,0:T(8,128)(2,1)S(1)}, u32[]{:S(2)}, u32[]{:S(2)}) collective-permute-start(bf16[54,2,8,128]{3,2,1,0:T(8,128)(2,1)} %get-tuple-element.41), channel_id=1, source_target_pairs={{0,1},{1,0},{2,3},{3,2},{4,5},{5,4},{6,7},{7,6},{8,9},{9,8},{10,11... | collective-permute-start | bytes 663560 | tf_op jit(solution)/shard_map/ppermute | solution.py:302
  11.3 18.4 %collective-permute-start.15 = (bf16[54,2,8,128]{3,2,1,0:T(8,128)(2,1)}, bf16[54,2,8,128]{3,2,1,0:T(8,128)(2,1)S(1)}, u32[]{:S(2)}, u32[]{:S(2)}) collective-permute-start(bf16[54,2,8,128]{3,2,1,0:T(8,128)(2,1)} %get-tuple-element.42), channel_id=1, source_target_pairs={{0,6},{1,7},{2,4},{3,5},{4,2},{5,3},{6,0},{7,1},{8,14},{9,15},{10,... | collective-permute-start | bytes 663560 | tf_op jit(solution)/shard_map/ppermute | solution.py:302
  12.6 24.2 %collective-permute-start.11 = (bf16[54,2,8,128]{3,2,1,0:T(8,128)(2,1)}, bf16[54,2,8,128]{3,2,1,0:T(8,128)(2,1)S(1)}, u32[]{:S(2)}, u32[]{:S(2)}) collective-permute-start(bf16[54,2,8,128]{3,2,1,0:T(8,128)(2,1)} %get-tuple-element.42), channel_id=1, source_target_pairs={{0,2},{1,3},{2,0},{3,1},{4,6},{5,7},{6,4},{7,5},{8,10},{9,11},{10,... | collective-permute-start | bytes 663560 | tf_op jit(solution)/shard_map/ppermute | solution.py:302
  12.9 24.1 %collective-permute-start.16 = (bf16[54,2,8,128]{3,2,1,0:T(8,128)(2,1)}, bf16[54,2,8,128]{3,2,1,0:T(8,128)(2,1)S(1)}, u32[]{:S(2)}, u32[]{:S(2)}) collective-permute-start(bf16[54,2,8,128]{3,2,1,0:T(8,128)(2,1)} %get-tuple-element.43), channel_id=1, source_target_pairs={{0,7},{1,6},{2,5},{3,4},{4,3},{5,2},{6,1},{7,0},{8,15},{9,14},{10,... | collective-permute-start | bytes 663560 | tf_op jit(solution)/shard_map/ppermute | solution.py:302
  27.6 36.3 %copy-start.4 = (bf16[54,2,8,128]{3,2,1,0:T(8,128)(2,1)}, bf16[54,2,8,128]{3,2,1,0:T(8,128)(2,1)S(1)}, u32[]{:S(2)}) copy-start(bf16[54,2,8,128]{3,2,1,0:T(8,128)(2,1)S(1)} %collective-permute-done.14.refs_5_) | copy-start | bytes 663556
  27.6 29.8 %collective-permute-start.7 = (bf16[48,3,8,128]{3,2,1,0:T(8,128)(2,1)}, bf16[48,3,8,128]{3,2,1,0:T(8,128)(2,1)S(1)}, u32[]{:S(2)}, u32[]{:S(2)}) collective-permute-start(bf16[48,3,8,128]{3,2,1,0:T(8,128)(2,1)} %get-tuple-element.38), channel_id=1, source_target_pairs={{0,1},{1,0},{2,3},{3,2},{4,5},{5,4},{6,7},{7,6},{8,9},{9,8},{10,11... | collective-permute-start | bytes 884744 | tf_op jit(solution)/shard_map/ppermute | solution.py:302
  29.7 34.2 %copy-start.5 = (bf16[54,2,8,128]{3,2,1,0:T(8,128)(2,1)}, bf16[54,2,8,128]{3,2,1,0:T(8,128)(2,1)S(1)}, u32[]{:S(2)}) copy-start(bf16[54,2,8,128]{3,2,1,0:T(8,128)(2,1)S(1)} %collective-permute-done.10.refs_1_) | copy-start | bytes 663556
  29.7 29.8 %collective-permute-start.8 = (bf16[48,3,8,128]{3,2,1,0:T(8,128)(2,1)}, bf16[48,3,8,128]{3,2,1,0:T(8,128)(2,1)S(1)}, u32[]{:S(2)}, u32[]{:S(2)}) collective-permute-start(bf16[48,3,8,128]{3,2,1,0:T(8,128)(2,1)} %get-tuple-element.39), channel_id=1, source_target_pairs={{0,2},{1,3},{2,0},{3,1},{4,6},{5,7},{6,4},{7,5},{8,10},{9,11},{10,... | collective-permute-start | bytes 884744 | tf_op jit(solution)/shard_map/ppermute | solution.py:302
  29.7 34.2 %copy-start.6 = (bf16[54,2,8,128]{3,2,1,0:T(8,128)(2,1)}, bf16[54,2,8,128]{3,2,1,0:T(8,128)(2,1)S(1)}, u32[]{:S(2)}) copy-start(bf16[54,2,8,128]{3,2,1,0:T(8,128)(2,1)S(1)} %collective-permute-done.15.refs_6_) | copy-start | bytes 663556
  29.7 31.3 %collective-permute-start.9 = (bf16[48,3,8,128]{3,2,1,0:T(8,128)(2,1)}, bf16[48,3,8,128]{3,2,1,0:T(8,128)(2,1)S(1)}, u32[]{:S(2)}, u32[]{:S(2)}) collective-permute-start(bf16[48,3,8,128]{3,2,1,0:T(8,128)(2,1)} %get-tuple-element.40), channel_id=1, source_target_pairs={{0,3},{1,2},{2,1},{3,0},{4,7},{5,6},{6,5},{7,4},{8,11},{9,10},{10,... | collective-permute-start | bytes 884744 | tf_op jit(solution)/shard_map/ppermute | solution.py:302
  36.8 27.0 %copy-start.7 = (bf16[54,2,8,128]{3,2,1,0:T(8,128)(2,1)}, bf16[54,2,8,128]{3,2,1,0:T(8,128)(2,1)S(1)}, u32[]{:S(2)}) copy-start(bf16[54,2,8,128]{3,2,1,0:T(8,128)(2,1)S(1)} %collective-permute-done.11.refs_2_) | copy-start | bytes 663556
  36.8 18.5 %collective-permute-start.12 = (bf16[54,2,8,128]{3,2,1,0:T(8,128)(2,1)S(1)}, bf16[54,2,8,128]{3,2,1,0:T(8,128)(2,1)S(1)}, u32[]{:S(2)}, u32[]{:S(2)}) collective-permute-start(bf16[54,2,8,128]{3,2,1,0:T(8,128)(2,1)S(1)} %copy-done.27), channel_id=1, source_target_pairs={{0,3},{1,2},{2,1},{3,0},{4,7},{5,6},{6,5},{7,4},{8,11},{9,10},{10,... | collective-permute-start | bytes 663560 | tf_op jit(solution)/shard_map/ppermute | solution.py:302
  36.9 26.9 %copy-start.8 = (bf16[54,2,8,128]{3,2,1,0:T(8,128)(2,1)}, bf16[54,2,8,128]{3,2,1,0:T(8,128)(2,1)S(1)}, u32[]{:S(2)}) copy-start(bf16[54,2,8,128]{3,2,1,0:T(8,128)(2,1)S(1)} %collective-permute-done.16.refs_7_) | copy-start | bytes 663556
  36.9 20.0 %collective-permute-start.13 = (bf16[54,2,8,128]{3,2,1,0:T(8,128)(2,1)S(1)}, bf16[54,2,8,128]{3,2,1,0:T(8,128)(2,1)S(1)}, u32[]{:S(2)}, u32[]{:S(2)}) collective-permute-start(bf16[54,2,8,128]{3,2,1,0:T(8,128)(2,1)S(1)} %copy-done), channel_id=1, source_target_pairs={{0,4},{1,5},{2,6},{3,7},{4,0},{5,1},{6,2},{7,3},{8,12},{9,13},{10,... | collective-permute-start | bytes 663560 | tf_op jit(solution)/shard_map/ppermute | solution.py:302
  55.3 14.9 %collective-permute-start.4 = (bf16[48,1,8,128]{3,2,1,0:T(8,128)(2,1)}, bf16[48,1,8,128]{3,2,1,0:T(8,128)(2,1)S(1)}, u32[]{:S(2)}, u32[]{:S(2)}) collective-permute-start(bf16[48,1,8,128]{3,2,1,0:T(8,128)(2,1)} %get-tuple-element.35), channel_id=1, source_target_pairs={{0,5},{1,4},{2,7},{3,6},{4,1},{5,0},{6,3},{7,2},{8,13},{9,12},{10,... | collective-permute-start | bytes 294920 | tf_op jit(solution)/shard_map/ppermute | solution.py:302
  56.9 15.0 %collective-permute-start = (bf16[48,1,8,128]{3,2,1,0:T(8,128)(2,1)}, bf16[48,1,8,128]{3,2,1,0:T(8,128)(2,1)S(1)}, u32[]{:S(2)}, u32[]{:S(2)}) collective-permute-start(bf16[48,1,8,128]{3,2,1,0:T(8,128)(2,1)} %get-tuple-element.35), channel_id=1, source_target_pairs={{0,1},{1,0},{2,3},{3,2},{4,5},{5,4},{6,7},{7,6},{8,9},{9,8},{10,11... | collective-permute-start | bytes 294920 | tf_op jit(solution)/shard_map/ppermute | solution.py:302
  57.4 14.4 %collective-permute-start.5 = (bf16[48,1,8,128]{3,2,1,0:T(8,128)(2,1)}, bf16[48,1,8,128]{3,2,1,0:T(8,128)(2,1)S(1)}, u32[]{:S(2)}, u32[]{:S(2)}) collective-permute-start(bf16[48,1,8,128]{3,2,1,0:T(8,128)(2,1)} %get-tuple-element.36), channel_id=1, source_target_pairs={{0,6},{1,7},{2,4},{3,5},{4,2},{5,3},{6,0},{7,1},{8,14},{9,15},{10,... | collective-permute-start | bytes 294920 | tf_op jit(solution)/shard_map/ppermute | solution.py:302
  59.4 15.2 %collective-permute-start.1 = (bf16[48,1,8,128]{3,2,1,0:T(8,128)(2,1)}, bf16[48,1,8,128]{3,2,1,0:T(8,128)(2,1)S(1)}, u32[]{:S(2)}, u32[]{:S(2)}) collective-permute-start(bf16[48,1,8,128]{3,2,1,0:T(8,128)(2,1)} %get-tuple-element.36), channel_id=1, source_target_pairs={{0,2},{1,3},{2,0},{3,1},{4,6},{5,7},{6,4},{7,5},{8,10},{9,11},{10,... | collective-permute-start | bytes 294920 | tf_op jit(solution)/shard_map/ppermute | solution.py:302
  61.0 14.7 %copy-start.11 = (bf16[48,1,8,128]{3,2,1,0:T(8,128)(2,1)S(1)}, bf16[48,1,8,128]{3,2,1,0:T(8,128)(2,1)}, u32[]{:S(2)}) copy-start(bf16[48,1,8,128]{3,2,1,0:T(8,128)(2,1)} %get-tuple-element.34.refs_0_._) | copy-start | bytes 294916
  61.0 16.9 %copy-start.26 = (bf16[128,16]{0,1:T(8,128)(2,1)S(1)}, bf16[128,16]{0,1:T(8,128)(2,1)}, u32[]{:S(2)}) copy-start(bf16[128,16]{0,1:T(8,128)(2,1)} %param.21) | copy-start | bytes 12292
  61.0 14.7 %collective-permute-start.6 = (bf16[48,1,8,128]{3,2,1,0:T(8,128)(2,1)}, bf16[48,1,8,128]{3,2,1,0:T(8,128)(2,1)S(1)}, u32[]{:S(2)}, u32[]{:S(2)}) collective-permute-start(bf16[48,1,8,128]{3,2,1,0:T(8,128)(2,1)} %get-tuple-element.37), channel_id=1, source_target_pairs={{0,7},{1,6},{2,5},{3,4},{4,3},{5,2},{6,1},{7,0},{8,15},{9,14},{10,... | collective-permute-start | bytes 294920 | tf_op jit(solution)/shard_map/ppermute | solution.py:302
  70.3 20.1 %collective-permute-start.20 = (bf16[24,32,128]{2,1,0:T(8,128)(2,1)}, bf16[24,32,128]{2,1,0:T(8,128)(2,1)S(1)}, u32[]{:S(2)}, u32[]{:S(2)}) collective-permute-start(bf16[24,32,128]{2,1,0:T(8,128)(2,1)} %get-tuple-element.55), channel_id=1, source_target_pairs={{0,1},{1,0},{2,3},{3,2},{4,5},{5,4},{6,7},{7,6},{8,9},{9,8},{10,11... | collective-permute-start | bytes 589832 | tf_op jit(solution)/shard_map/ppermute | solution.py:302
  71.9 21.2 %collective-permute-start.21 = (bf16[24,32,128]{2,1,0:T(8,128)(2,1)}, bf16[24,32,128]{2,1,0:T(8,128)(2,1)S(1)}, u32[]{:S(2)}, u32[]{:S(2)}) collective-permute-start(bf16[24,32,128]{2,1,0:T(8,128)(2,1)} %get-tuple-element.56), channel_id=1, source_target_pairs={{0,2},{1,3},{2,0},{3,1},{4,6},{5,7},{6,4},{7,5},{8,10},{9,11},{10,... | collective-permute-start | bytes 589832 | tf_op jit(solution)/shard_map/ppermute | solution.py:302
  71.9 21.2 %collective-permute-start.22 = (bf16[24,32,128]{2,1,0:T(8,128)(2,1)}, bf16[24,32,128]{2,1,0:T(8,128)(2,1)S(1)}, u32[]{:S(2)}, u32[]{:S(2)}) collective-permute-start(bf16[24,32,128]{2,1,0:T(8,128)(2,1)} %get-tuple-element.57), channel_id=1, source_target_pairs={{0,3},{1,2},{2,1},{3,0},{4,7},{5,6},{6,5},{7,4},{8,11},{9,10},{10,... | collective-permute-start | bytes 589832 | tf_op jit(solution)/shard_map/ppermute | solution.py:302
  74.6 10.3 %collective-permute-start.2 = (bf16[48,1,8,128]{3,2,1,0:T(8,128)(2,1)S(1)}, bf16[48,1,8,128]{3,2,1,0:T(8,128)(2,1)S(1)}, u32[]{:S(2)}, u32[]{:S(2)}) collective-permute-start(bf16[48,1,8,128]{3,2,1,0:T(8,128)(2,1)S(1)} %copy-done.28), channel_id=1, source_target_pairs={{0,3},{1,2},{2,1},{3,0},{4,7},{5,6},{6,5},{7,4},{8,11},{9,10},{10,... | collective-permute-start | bytes 294920 | tf_op jit(solution)/shard_map/ppermute | solution.py:302
  75.7 9.2 %collective-permute-start.3 = (bf16[48,1,8,128]{3,2,1,0:T(8,128)(2,1)S(1)}, bf16[48,1,8,128]{3,2,1,0:T(8,128)(2,1)S(1)}, u32[]{:S(2)}, u32[]{:S(2)}) collective-permute-start(bf16[48,1,8,128]{3,2,1,0:T(8,128)(2,1)S(1)} %copy-done.11), channel_id=1, source_target_pairs={{0,4},{1,5},{2,6},{3,7},{4,0},{5,1},{6,2},{7,3},{8,12},{9,13},{10,... | collective-permute-start | bytes 294920 | tf_op jit(solution)/shard_map/ppermute | solution.py:302
  89.6 12.4 %collective-permute-start.17 = (bf16[24,16,128]{2,1,0:T(8,128)(2,1)}, bf16[24,16,128]{2,1,0:T(8,128)(2,1)S(1)}, u32[]{:S(2)}, u32[]{:S(2)}) collective-permute-start(bf16[24,16,128]{2,1,0:T(8,128)(2,1)} %get-tuple-element.46), channel_id=1, source_target_pairs={{0,1},{1,0},{2,3},{3,2},{4,5},{5,4},{6,7},{7,6},{8,9},{9,8},{10,11... | collective-permute-start | bytes 294920 | tf_op jit(solution)/shard_map/ppermute | solution.py:302
  90.4 11.7 %collective-permute-start.18 = (bf16[24,16,128]{2,1,0:T(8,128)(2,1)}, bf16[24,16,128]{2,1,0:T(8,128)(2,1)S(1)}, u32[]{:S(2)}, u32[]{:S(2)}) collective-permute-start(bf16[24,16,128]{2,1,0:T(8,128)(2,1)} %get-tuple-element.47), channel_id=1, source_target_pairs={{0,2},{1,3},{2,0},{3,1},{4,6},{5,7},{6,4},{7,5},{8,10},{9,11},{10,... | collective-permute-start | bytes 294920 | tf_op jit(solution)/shard_map/ppermute | solution.py:302
  90.4 11.7 %collective-permute-start.19 = (bf16[24,16,128]{2,1,0:T(8,128)(2,1)}, bf16[24,16,128]{2,1,0:T(8,128)(2,1)S(1)}, u32[]{:S(2)}, u32[]{:S(2)}) collective-permute-start(bf16[24,16,128]{2,1,0:T(8,128)(2,1)} %get-tuple-element.48), channel_id=1, source_target_pairs={{0,3},{1,2},{2,1},{3,0},{4,7},{5,6},{6,5},{7,4},{8,11},{9,10},{10,... | collective-permute-start | bytes 294920 | tf_op jit(solution)/shard_map/ppermute | solution.py:302
  (20 other events, 123.3 us)

commit v3 on v2

--- a/solution.py
+++ b/solution.py
@@ -55,14 +55,15 @@
             part = edge[s * per_set : (s + 1) * per_set]
             head_ref[pl.ds(at, per_set), :] = part[:, :LANES]
             rest_ref[pl.ds(at, per_set), :] = part[:, LANES:]
+    step = pl.program_id(0)
     low = first_half_lanes((SUB, LANES))
     for q in range(sets):
         for c in range(pairs):
             a = pl.ds(q * per_set + c, SUB, stride=stride)
             b = pl.ds(q * per_set + pairs + c, SUB, stride=stride)
-            out_refs[q][c, 0] = head_ref[a, :].astype(bf16)
-            out_refs[q][pairs + c, 0] = head_ref[b, :].astype(bf16)
-            out_refs[q][per_set + c, 0] = jnp.where(low, rest_ref[a, :], rest_ref[b, :]).astype(bf16)
+            out_refs[q][c, step] = head_ref[a, :].astype(bf16)
+            out_refs[q][pairs + c, step] = head_ref[b, :].astype(bf16)
+            out_refs[q][per_set + c, step] = jnp.where(low, rest_ref[a, :], rest_ref[b, :]).astype(bf16)
 
 
 def single_places(shape, tiles):
@@ -84,7 +85,8 @@
         wt_ref[...] = w_ref[...].T
 
     first = me_ref[0] * row_count + offset + pl.program_id(0) * SUB
-    rows_of = lambda j: layer_norm(pair_ref[j], 1).astype(bf16)
+    at = 0 if single_tiles else offset + pl.program_id(0) * SUB
+    rows_of = lambda j: layer_norm(pair_ref[at + j], 1).astype(bf16)
     edges_to_messages(me_ref, mask_ref, live_ref, wt_ref, rows_of, head_ref, rest_ref, out_refs, first, hidden, full)
     if single_tiles:
         single_normed = layer_norm(single_ref[...], 1)
@@ -98,7 +100,7 @@
                         t, at = divmod(n, row_count // SUB)
                         part = single_normed[at * SUB : (at + 1) * SUB, t * LANES : (t + 1) * LANES].astype(bf16)
                         for q in range(sets):
-                            out_refs[q][base + slab, 0] = part
+                            out_refs[q][base + slab, tile] = part
 
 
 def left_kernel(hidden, full, sets, row_count, me_ref, mask_ref, pair_ref, live_ref, w_ref, *rest):
@@ -110,14 +112,21 @@
         wt_ref[...] = w_ref[...].T
 
     first = me_ref[0] * row_count + pl.program_id(0) * SUB
-    rows_of = lambda j: layer_norm(pair_ref[j], 1).astype(bf16)
+    rows_of = lambda j: layer_norm(pair_ref[pl.program_id(0) * SUB + j], 1).astype(bf16)
     edges_to_messages(me_ref, mask_ref, live_ref, wt_ref, rows_of, head_ref, rest_ref, out_refs, first, hidden, full)
 
 
 def gate_kernel(pair_ref, w_gate_ref, _, gate_ref):
-    rows = pair_ref.shape[0] * pair_ref.shape[1]
-    x = layer_norm(pair_ref[...].reshape(rows, pair_ref.shape[2]), 1).astype(bf16)
-    gate_ref[...] = sigmoid(jnp.dot(x, w_gate_ref[...], preferred_element_type=f32)).reshape(gate_ref.shape)
+    width = pair_ref.shape[2]
+
+    def rows(g, carry):
+        here = pl.ds(g * SUB, SUB)
+        block = pair_ref[here]
+        x = layer_norm(block.reshape(SUB * block.shape[1], width), 1).astype(bf16)
+        gate_ref[here] = sigmoid(jnp.dot(x, w_gate_ref[...], preferred_element_type=f32)).reshape(block.shape)
+        return carry
+
+    lax.fori_loop(0, pair_ref.shape[0] // SUB, rows, 0)
 
 
 def plain_rows(block):
@@ -166,7 +175,7 @@
             out_refs[a][i] = x.astype(bf16)
 
 
-def attention_in_kernel(groups, chunks, me_ref, *refs):
+def attention_in_kernel(groups, chunks, message, me_ref, *refs):
     n = len(chunks)
     right_refs = refs[:groups]
     w_query_ref, w_key_ref, w_value_gate_ref, q_ref, g_ref = refs[groups : groups + 5]
@@ -179,7 +188,9 @@
         d = lax.bitwise_xor(me, s)
         for place, (slab, tile) in single_places(q_ref.shape, right_refs[s].shape[1]).items():
             t, at = divmod(place, tiles)
-            all_ref[d, at * SUB : (at + 1) * SUB, t * LANES : (t + 1) * LANES] = right_refs[s][slab, tile].astype(f32)
+            all_ref[d, at * SUB : (at + 1) * SUB, t * LANES : (t + 1) * LANES] = right_refs[s][
+                message + slab, tile
+            ].astype(f32)
     own = all_ref[me].astype(bf16)
     q_ref[...] = jnp.dot(own, w_query_ref[...], preferred_element_type=f32).astype(bf16)
     g_ref[...] = sigmoid(jnp.dot(own, w_value_gate_ref[:, channels:], preferred_element_type=f32))
@@ -191,15 +202,16 @@
         first += chunks[k]
 
 
-def tail_kernel(sets, per_set, heads, slab, attends, me_ref, *refs):
+def tail_kernel(sets, per_set, heads, slab, attends, first, me_ref, *refs):
     tri_refs = refs[:sets]
     pair_ref, gate_ref, w_tri_out_ref, w_in_ref, w_down_ref, w_bias_ref = refs[sets : sets + 6]
     if attends:
-        new_ref, single_ref, bias_ref, w_rel_ref, wb_ref = refs[-5:]
+        new_ref, single_ref, bias_ref, w_rel_ref, w_half_ref = refs[-5:]
     else:
-        new_ref, bias_ref, w_rel_ref, wb_ref = refs[-4:]
+        new_ref, bias_ref, w_rel_ref, w_half_ref = refs[-4:]
     width = pair_ref.shape[-1]
-    columns = math.prod(pair_ref.shape[1:-1])
+    columns = math.prod(new_ref.shape[1:-1])
+    part = slice(first, first + new_ref.shape[2])
     together = LANES // columns
     inner_width = w_down_ref.shape[0]
     me = me_ref[0]
@@ -209,9 +221,11 @@
         own_set = lax.rem(me, sets)
         for a in range(sets):
             w_rel_ref[a * per_set : (a + 1) * per_set] = w_tri_out_ref[lax.bitwise_xor(own_set, a)]
-        wb_ref[...] = w_bias_ref[...].T
+        w_half_ref[:, :inner_width] = w_in_ref[:, :inner_width] * 0.5
+        w_half_ref[:, inner_width:] = w_in_ref[:, inner_width:]
 
     low = first_half_lanes((per_set // 2, LANES))
+    start = pl.program_id(0) * new_ref.shape[0]
 
     def sums_of(i):
         parts = []
@@ -228,36 +242,38 @@
         i = b * slab * together
         tri = []
         for n in range(slab):
-            tri.append(layer_norm(sums_of(i + n * together), 0).astype(bf16).T)
+            tri.append(layer_norm(sums_of(start + i + n * together), 0).astype(bf16).T)
         tri = jnp.concatenate(tri, axis=0)
         tri_out = jnp.dot(tri, w_rel_ref[...], preferred_element_type=f32)
-        here = pl.ds(i, slab * together)
+        here, there = pl.ds(i, slab * together), pl.ds(start + i, slab * together)
         block = (slab * LANES, width)
-        mid = pair_ref[here].reshape(block) + gate_ref[here].reshape(block) * tri_out
+        mid = pair_ref[there, :, part].reshape(block) + gate_ref[there, :, part].reshape(block) * tri_out
         trans = layer_norm(mid, 1).astype(bf16)
-        gate_up = jnp.dot(trans, w_in_ref[...], preferred_element_type=f32)
-        gate = gate_up[:, :inner_width]
-        inner = (gate * sigmoid(gate) * gate_up[:, inner_width:]).astype(bf16)
+        gate_up = jnp.dot(trans, w_half_ref[...], preferred_element_type=f32)
+        half = gate_up[:, :inner_width]
+        scaled = half * gate_up[:, inner_width:]
+        inner = (scaled + scaled * jnp.tanh(half)).astype(bf16)
         new = mid + jnp.dot(inner, w_down_ref[...], preferred_element_type=f32)
         new_ref[here] = new.reshape((slab * together,) + new_ref.shape[1:])
         normed = layer_norm(new, 1).astype(bf16)
-        bias = lax.dot_general(wb_ref[...], normed, NT, preferred_element_type=f32)
+        bias = lax.dot_general(w_bias_ref[...], normed, NT, preferred_element_type=f32)
         for n in range(slab):
-            part = bias[:, n * LANES : (n + 1) * LANES]
-            bias_ref[i + n * together] = part
+            lane_tile = bias[:, n * LANES : (n + 1) * LANES]
+            bias_ref[i + n * together] = lane_tile
             if together == 2:
-                bias_ref[i + n * together + 1] = pltpu.roll(part, LANES // 2, 1)
+                bias_ref[i + n * together + 1] = pltpu.roll(lane_tile, LANES // 2, 1)
         return carry
 
-    lax.fori_loop(0, pair_ref.shape[0] // (slab * together), rows, 0)
+    lax.fori_loop(0, new_ref.shape[0] // (slab * together), rows, 0)
     if attends:
-        attention(heads, attends, refs[sets + 6 :], bias_ref, single_ref)
-
-
-def attention(heads, n, refs, last_bias_ref, single_ref):
-    q_ref, g_ref, w_out_ref = refs[:3]
-    k_refs, v_refs, live_refs = refs[3 : 3 + n], refs[3 + n : 3 + 2 * n], refs[3 + 2 * n : 3 + 3 * n]
-    bias_refs = [*refs[3 + 3 * n : 2 + 4 * n], last_bias_ref]
+        attention(heads, attends, pair_ref.shape[1], refs[sets + 6 :], bias_ref, single_ref)
+
+
+def attention(heads, n, groups, refs, last_bias_ref, single_ref):
+    q_ref, g_ref, w_out_ref, mask_ref = refs[:4]
+    k_refs, v_refs = refs[4 : 4 + n], refs[4 + n : 4 + 2 * n]
+    bias_refs = [*refs[4 + 2 * n : 3 + 3 * n], last_bias_ref]
+    count = jnp.sum(mask_ref[...].astype(f32).reshape(1, mask_ref.shape[0]), axis=1, keepdims=True)
     row_count, channels = q_ref.shape
     head_size = channels // heads
     of_head = lax.broadcasted_iota(jnp.int32, (row_count, heads, channels), 1)
@@ -265,12 +281,16 @@
     mine = jnp.logical_and(lane >= of_head * head_size, lane < (of_head + 1) * head_size)
     spread = jnp.where(mine, jnp.broadcast_to(q_ref[...].astype(f32)[:, None, :], mine.shape), 0.0)
     spread = spread.reshape(row_count * heads, channels).astype(bf16)
-    scores = []
+    scores, first = [], 0
     for k in range(n):
         part = lax.dot_general(spread, k_refs[k][...], NT, preferred_element_type=f32)
         bias = bias_refs[k][...].reshape(row_count * heads, LANES)[:, : part.shape[1]]
         part = part / jnp.sqrt(f32(head_size)) + bias
-        scores.append(jnp.where(live_refs[k][...] > 0, part, f32(-1000000000.0)))
+        column = lax.broadcasted_iota(jnp.int32, (1, part.shape[1]), 1)
+        size = part.shape[1] // groups
+        token = column // size * row_count + first + column % size
+        first += size
+        scores.append(jnp.where(token.astype(f32) < count, part, f32(-1000000000.0)))
     row_max = functools.reduce(jnp.maximum, [jnp.max(x, axis=1, keepdims=True) for x in scores])
     weights = [jnp.exp(x - row_max) for x in scores]
     row_sum = sum(jnp.sum(x, axis=1, keepdims=True) for x in weights)
@@ -286,8 +306,20 @@
     return pl.BlockSpec(shape, lambda *_: (0,) * len(shape))
 
 
-def params():
-    return pltpu.CompilerParams(dimension_semantics=("arbitrary",))
+def params(**more):
+    return pltpu.CompilerParams(dimension_semantics=("arbitrary",), **more)
+
+
+def arrived(arrays):
+    return [pltpu.with_memory_space_constraint(x, pltpu.VMEM) for x in arrays]
+
+
+def kept(arrays):
+    return [pltpu.with_memory_space_constraint(x, pltpu.HBM) for x in arrays]
+
+
+def in_vmem(arrays):
+    return [pl.BlockSpec(memory_space=pltpu.VMEM)] * len(arrays)
 
 
 def anywhere(arrays):
@@ -327,9 +359,8 @@
     chunks = chunk_tiles(tiles, groups)
     starts = [sum(chunks[:k]) for k in range(len(chunks))]
     me = lax.axis_index("row").astype(jnp.int32).reshape(1)
-    live = token_mask.astype(f32)
+    (near,) = arrived([pair])
     sds = jax.ShapeDtypeStruct
-    message_block = lambda n: pl.BlockSpec((n, 1, SUB, LANES), lambda g, *_: (0, g, 0, 0))
     edge_scratch = [pltpu.VMEM((SUB * (hidden + SUB), LANES), f32)] * 2 + [pltpu.VMEM((2 * hidden, width), bf16)]
     edge_flops = 2 * SUB * lanes * width * 2 * hidden
 
@@ -343,19 +374,19 @@
                 num_scalar_prefetch=2,
                 grid=(chunks[k],),
                 in_specs=[
-                    pl.BlockSpec((SUB, length, width), lambda g, *_: (at + g, 0, 0)),
+                    *(in_vmem([near]) if k else [pl.BlockSpec((SUB, length, width), lambda g, *_: (g, 0, 0))]),
                     whole_block(single.shape),
                     whole_block((length,)),
                     pl.BlockSpec((width, 2 * hidden), lambda *_: (0, 1)),
                 ]
                 + anywhere(after),
-                out_specs=[message_block(size)] * sets,
+                out_specs=in_vmem([None] * sets),
                 scratch_shapes=edge_scratch,
             ),
             out_shape=[sds((size, chunks[k], SUB, LANES), bf16)] * sets,
-            compiler_params=params(),
+            compiler_params=params(vmem_limit_bytes=24 * 2**20),
             cost_estimate=cost(edge_flops * chunks[k]),
-        )(me, token_mask, pair, single, token_mask, w_tri_proj, *after)
+        )(me, token_mask, *([near, single, token_mask, w_tri_proj] if k else kept([pair, single, token_mask, w_tri_proj])), *after)
 
     def left_edges(after):
         return pl.pallas_call(
@@ -365,18 +396,18 @@
                 num_scalar_prefetch=2,
                 grid=(tiles,),
                 in_specs=[
-                    pl.BlockSpec((SUB, length, width), lambda g, *_: (g, 0, 0)),
+                    *in_vmem([near]),
                     whole_block((length,)),
                     pl.BlockSpec((width, 2 * hidden), lambda *_: (0, 0)),
                 ]
                 + anywhere(after),
-                out_specs=[message_block(message)] * sets,
+                out_specs=in_vmem([None] * sets),
                 scratch_shapes=edge_scratch,
             ),
             out_shape=[sds((message, tiles, SUB, LANES), bf16)] * sets,
-            compiler_params=params(),
+            compiler_params=params(vmem_limit_bytes=24 * 2**20),
             cost_estimate=cost(edge_flops * tiles),
-        )(me, token_mask, pair, token_mask, w_tri_proj, *after)
+        )(me, token_mask, near, token_mask, w_tri_proj, *after)
 
     right_in, left_in, after = [], None, []
     for k in range(len(chunks)):
@@ -391,31 +422,30 @@
     gate_pair = pl.pallas_call(
         gate_kernel,
         name="gate",
-        grid=(tiles,),
-        in_specs=[pl.BlockSpec((SUB, length, width), lambda g: (g, 0, 0)), whole_block((width, width))] + anywhere(after),
-        out_specs=pl.BlockSpec((SUB, length, width), lambda g: (g, 0, 0)),
+        in_specs=in_vmem([near, w_tri_gate]) + anywhere(after),
+        out_specs=in_vmem([None])[0],
         out_shape=sds(pair.shape, f32),
-        compiler_params=params(),
+        compiler_params=pltpu.CompilerParams(vmem_limit_bytes=16 * 2**20),
         cost_estimate=cost(2 * row_count * length * width * width),
-    )(pair, w_tri_gate, *after)
+    )(near, w_tri_gate, *after)
 
     tokens = [groups * n * SUB for n in chunks]
     queries, att_gate, *keys_values = pl.pallas_call(
-        functools.partial(attention_in_kernel, groups, chunks),
+        functools.partial(attention_in_kernel, groups, chunks, message),
         name="attention_in",
         grid_spec=pltpu.PrefetchScalarGridSpec(
             num_scalar_prefetch=1,
             grid=(1,),
-            in_specs=[pl.BlockSpec((slabs, chunks[0], SUB, LANES), lambda *_: (message // slabs, 0, 0, 0))] * groups
+            in_specs=in_vmem(right_in[0])
             + [whole_block(w_query.shape), whole_block(w_key.shape), whole_block(w_value_gate.shape)],
             out_specs=[whole_block((row_count, channels))] * 2 + [whole_block((n, channels)) for n in tokens + tokens],
             scratch_shapes=[pltpu.VMEM((groups, row_count, channels), f32)],
         ),
         out_shape=[sds((row_count, channels), bf16), sds((row_count, channels), f32)]
         + [sds((n, channels), bf16) for n in tokens + tokens],
-        compiler_params=params(),
+        compiler_params=params(vmem_limit_bytes=16 * 2**20),
         cost_estimate=cost(2 * length * channels * channels * 3),
-    )(me, *right_in[0], w_query, w_key, w_value_gate)
+    )(me, *arrived(right_in[0]), w_query, w_key, w_value_gate)
 
     total = sets * row_count
     tri_in = []
@@ -428,9 +458,7 @@
             grid_spec=pltpu.PrefetchScalarGridSpec(
                 num_scalar_prefetch=1,
                 grid=(1,),
-                in_specs=[whole_block((message, chunks[k], SUB, LANES))] * groups
-                + [whole_block((message, tiles, SUB, LANES))] * sets
-                + anywhere([late]),
+                in_specs=in_vmem(right_in[k] + left_in) + anywhere([late]),
                 out_specs=[whole_block(sums_shape)] * sets,
                 scratch_shapes=[
                     pltpu.VMEM((per_set, groups, chunks[k] * SUB, LANES), f32),
@@ -439,17 +467,14 @@
                 ],
             ),
             out_shape=[sds(sums_shape, bf16)] * sets,
-            compiler_params=params(),
+            compiler_params=params(vmem_limit_bytes=24 * 2**20),
             cost_estimate=cost(2 * per_set * total * lanes * LANES),
-        )(me, *right_in[k], *left_in, late)
+        )(me, *arrived(right_in[k] + left_in), late)
         tri_in.append([exchange(sums[a], groups, a) for a in range(sets)])
 
     tiled = (row_count, groups, tiles, SUB, width)
-    pair_tiled, gate_tiled = pair.reshape(tiled), gate_pair.reshape(tiled)
+    pair_tiled, gate_tiled = arrived([pair.reshape(tiled), gate_pair.reshape(tiled)])
     new, biases = None, []
-    lives = [
-        live.reshape(groups, tiles, SUB)[:, at : at + n].reshape(1, groups * n * SUB) for at, n in zip(starts, chunks)
-    ]
     for k, n in enumerate(chunks):
         attends = len(chunks) if k == len(chunks) - 1 else 0
         columns = tokens[k]
@@ -458,11 +483,10 @@
         slab = take // together
         at = starts[k] // n
         part_rows = pl.BlockSpec((take, groups, n, SUB, width), lambda g, *_, at=at: (g, 0, at, 0, 0))
-        operands = [*tri_in[k], pair_tiled, gate_tiled, w_tri_out.reshape(sets, per_set, width), w_trans_in, w_trans_out, w_bias]
-        sums_block = (take,) + tri_in[k][0].shape[1:]
-        in_specs = [pl.BlockSpec(sums_block, lambda g, *_: (g, 0, 0))] * sets + [part_rows, part_rows]
+        operands = [*arrived(tri_in[k]), pair_tiled, gate_tiled, w_tri_out.reshape(sets, per_set, width), w_trans_in, w_trans_out, w_bias.T]
+        in_specs = in_vmem(operands[: sets + 2])
         if attends:
-            operands += [queries, att_gate, w_out, *keys_values, *lives, *biases]
+            operands += [queries, att_gate, w_out, token_mask, *keys_values, *biases]
         in_specs += [whole_block(x.shape) for x in operands[sets + 2 :]]
         aliases = {}
         if new is not None:
@@ -470,9 +494,9 @@
             operands.append(new)
             in_specs += anywhere([new])
         bias_shape = (row_count, heads, LANES)
-        weights = [pltpu.VMEM((hidden, width), bf16), pltpu.VMEM((heads, width), bf16)]
+        weights = [pltpu.VMEM((hidden, width), bf16), pltpu.VMEM(w_trans_in.shape, bf16)]
         new, last = pl.pallas_call(
-            functools.partial(tail_kernel, sets, per_set, heads, slab, attends),
+            functools.partial(tail_kernel, sets, per_set, heads, slab, attends, starts[k]),
             grid_spec=pltpu.PrefetchScalarGridSpec(
                 num_scalar_prefetch=1,
                 grid=(row_count // take,),
@@ -485,7 +509,7 @@
             ),
             out_shape=[sds(tiled, f32), sds(single.shape if attends else bias_shape, f32)],
             input_output_aliases=aliases,
-            compiler_params=params(),
+            compiler_params=params(vmem_limit_bytes=32 * 2**20),
             cost_estimate=cost(2 * row_count * columns * width * (hidden + 3 * inner_width)),
         )(me, *operands)
         biases.append(last)

time: 109 us -> 96.4 us (0.88)
  Pallas kernels: 43.5 us -> 26.1 us
  waiting for transfers between devices: 14.4 us -> 22.8 us
  local copies, waits for them, and re-layouts: 4.81 us -> 0.06 us
  starting transfers between devices: 45.2 us -> 46.5 us
    ppermute x23, waiting for transfers between devices: 14.4 us -> 22.8 us  [exchange(): lax.ppermute(x, 'row', [(r, r ^ s) for r in range(groups)])]
    pallas_call x2, Pallas kernels: 7.29 us -> 2.43 us  [the longest x1 1.95 us: fast_body(): pl.pallas_call(gate_kernel, name='gate', in_specs=in_vmem([near, w_tri_ga...]
    pallas_call x2, Pallas kernels: 7.17 us -> 2.46 us  [fast_body(): pl.pallas_call(functools.partial(triangle_kernel, groups, sets, per_set),...]
    pallas_call x2, Pallas kernels: 14.3 us -> 10.9 us  [fast_body(): pl.pallas_call(functools.partial(tail_kernel, sets, per_set, heads, slab,...]
    unnamed x59 -> x26, local copies, waits for them, and re-layouts: 3.43 us -> 0.06 us
    pallas_call x2, Pallas kernels: 8.73 us -> 6.22 us  [right_edges(): pl.pallas_call(functools.partial(right_kernel, hidden, full, sets, row_co...]
    pallas_call x1, Pallas kernels: 6.02 us -> 4.08 us  [left_edges(): pl.pallas_call(functools.partial(left_kernel, hidden, full, sets, row_cou...]
    reshape x3 -> x0, local copies, waits for them, and re-layouts: 1.35 us -> none  [fast_body(): live.reshape(groups, tiles, SUB)[:, at:at + n].reshape(1, groups * n * SUB)]
  transfers between devices with their start and end apart: 23 -> 23, of which waited for: 3 -> 4; matrix products, arithmetic and copies ran while one was open for 2% -> 0% of each run, Pallas kernels for 30% -> 18%
where the time goes in v3:
time: 96.4 us; the launch traced here: 96.2 us
  starting transfers between devices  46.5 us (48%)
  Pallas kernels  26.1 us (27%)
  waiting for transfers between devices  22.8 us (24%)
    ppermute x23, starting transfers between devices, exchange(): lax.ppermute(x, 'row', [(r, r ^ s) for r in range(groups)])  46.5 us
    ppermute x23, waiting for transfers between devices, exchange(): lax.ppermute(x, 'row', [(r, r ^ s) for r in range(groups)])  22.8 us
    pallas_call x2, Pallas kernels, fast_body(): pl.pallas_call(functools.partial(tail_kernel, sets, per_set, heads, slab,...  10.9 us
    pallas_call x2, Pallas kernels, right_edges(): pl.pallas_call(functools.partial(right_kernel, hidden, full, sets, row_co...  6.22 us
    pallas_call x1, Pallas kernels, left_edges(): pl.pallas_call(functools.partial(left_kernel, hidden, full, sets, row_cou...  4.08 us
    pallas_call x2, Pallas kernels, fast_body(): pl.pallas_call(functools.partial(triangle_kernel, groups, sets, per_set),...  2.46 us
    pallas_call x1, Pallas kernels, fast_body(): pl.pallas_call(gate_kernel, name='gate', in_specs=in_vmem([near, w_tri_ga...  1.95 us
  transfers between devices with their start and end apart: 23, of which 4 were waited for; matrix products, arithmetic and copies ran while one was open for 0% of the time, Pallas kernels for 18%

profile of v3, /device:TPU:0, one launch (start us, length us, event | category | flops | bytes accessed | tf_op | source)
XLA Modules:
  0.0 96.2 jit_solution(4780937991362284235)
XLA Ops:
  0.7 4.5 %right.2 = (bf16[54,2,8,128]{3,2,1,0:T(8,128)(2,1)S(1)}, bf16[54,2,8,128]{3,2,1,0:T(8,128)(2,1)S(1)}, bf16[54,2,8,128]{3,2,1,0:T(8,128)(2,1)S(1)}, bf16[54,2,8,128]{3,2,1,0:T(8,128)(2,1)S(1)}) custom-call(s32[1]{0:T(128)} %bitcast.me_ref, s32[192]{0:T(256)} %refs_13_.1, f32[24,192,128]{2,1,0:T(8,128)} %pair_ref.7, f32[24,384]{1,0:T(8,128)} %single_ref.3, ...), custom_call_target="tpu_custom_call" | custom-call | flops 268435456 | bytes 4000000 | tf_op jit(solution)/shard_map/right/pallas_call | solution.py:370
  5.2 5.1 %collective-permute-start.14 = (bf16[54,2,8,128]{3,2,1,0:T(8,128)(2,1)S(1)}, bf16[54,2,8,128]{3,2,1,0:T(8,128)(2,1)S(1)}, u32[]{:S(2)}, u32[]{:S(2)}) collective-permute-start(bf16[54,2,8,128]{3,2,1,0:T(8,128)(2,1)S(1)} %get-tuple-element.41), channel_id=1, source_target_pairs={{0,5},{1,4},{2,7},{3,6},{4,1},{5,0},{6,3},{7,2},{8,13},{9,12},{10,... | collective-permute-start | bytes 663560 | tf_op jit(solution)/shard_map/ppermute | solution.py:334
  10.3 0.5 collective-permute-start.10
  10.8 1.4 %collective-permute-start.15 = (bf16[54,2,8,128]{3,2,1,0:T(8,128)(2,1)S(1)}, bf16[54,2,8,128]{3,2,1,0:T(8,128)(2,1)S(1)}, u32[]{:S(2)}, u32[]{:S(2)}) collective-permute-start(bf16[54,2,8,128]{3,2,1,0:T(8,128)(2,1)S(1)} %get-tuple-element.42), channel_id=1, source_target_pairs={{0,6},{1,7},{2,4},{3,5},{4,2},{5,3},{6,0},{7,1},{8,14},{9,15},{10,... | collective-permute-start | bytes 663560 | tf_op jit(solution)/shard_map/ppermute | solution.py:334
  12.1 0.2 collective-permute-start.11
  12.3 3.9 %collective-permute-start.16 = (bf16[54,2,8,128]{3,2,1,0:T(8,128)(2,1)S(1)}, bf16[54,2,8,128]{3,2,1,0:T(8,128)(2,1)S(1)}, u32[]{:S(2)}, u32[]{:S(2)}) collective-permute-start(bf16[54,2,8,128]{3,2,1,0:T(8,128)(2,1)S(1)} %get-tuple-element.43), channel_id=1, source_target_pairs={{0,7},{1,6},{2,5},{3,4},{4,3},{5,2},{6,1},{7,0},{8,15},{9,14},{10,... | collective-permute-start | bytes 663560 | tf_op jit(solution)/shard_map/ppermute | solution.py:334
  16.3 4.1 %left.1 = (bf16[48,3,8,128]{3,2,1,0:T(8,128)(2,1)S(1)}, bf16[48,3,8,128]{3,2,1,0:T(8,128)(2,1)S(1)}, bf16[48,3,8,128]{3,2,1,0:T(8,128)(2,1)S(1)}, bf16[48,3,8,128]{3,2,1,0:T(8,128)(2,1)S(1)}) custom-call(s32[1]{0:T(128)} %bitcast.me_ref, s32[192]{0:T(256)S(1)} %copy-done.10, f32[24,192,128]{2,1,0:T(8,128)S(1)} %copy-done, s32[192]{0:T(256)S(1)} %copy-done.10, ...), custom_call_target="tpu_custom_call" | custom-call | flops 402653184 | bytes 4000000 | tf_op jit(solution)/shard_map/left/pallas_call | solution.py:392
  20.3 6.6 %collective-permute-done.14.refs_5_ = bf16[54,2,8,128]{3,2,1,0:T(8,128)(2,1)S(1)} collective-permute-done((bf16[54,2,8,128]{3,2,1,0:T(8,128)(2,1)S(1)}, bf16[54,2,8,128]{3,2,1,0:T(8,128)(2,1)S(1)}, u32[]{:S(2)}, u32[]{:S(2)}) %collective-permute-start.14) | collective-permute-done | bytes 221216 | tf_op jit(solution)/shard_map/ppermute | solution.py:334
  26.9 2.0 %collective-permute-start.7 = (bf16[48,3,8,128]{3,2,1,0:T(8,128)(2,1)S(1)}, bf16[48,3,8,128]{3,2,1,0:T(8,128)(2,1)S(1)}, u32[]{:S(2)}, u32[]{:S(2)}) collective-permute-start(bf16[48,3,8,128]{3,2,1,0:T(8,128)(2,1)S(1)} %get-tuple-element.38), channel_id=1, source_target_pairs={{0,1},{1,0},{2,3},{3,2},{4,5},{5,4},{6,7},{7,6},{8,9},{9,8},{10,11... | collective-permute-start | bytes 884744 | tf_op jit(solution)/shard_map/ppermute | solution.py:334
  28.9 7.2 %collective-permute-start.9 = (bf16[48,3,8,128]{3,2,1,0:T(8,128)(2,1)S(1)}, bf16[48,3,8,128]{3,2,1,0:T(8,128)(2,1)S(1)}, u32[]{:S(2)}, u32[]{:S(2)}) collective-permute-start(bf16[48,3,8,128]{3,2,1,0:T(8,128)(2,1)S(1)} %get-tuple-element.40), channel_id=1, source_target_pairs={{0,3},{1,2},{2,1},{3,0},{4,7},{5,6},{6,5},{7,4},{8,11},{9,10},{10,... | collective-permute-start | bytes 884744 | tf_op jit(solution)/shard_map/ppermute | solution.py:334
  36.1 7.0 %collective-permute-start.13 = (bf16[54,2,8,128]{3,2,1,0:T(8,128)(2,1)S(1)}, bf16[54,2,8,128]{3,2,1,0:T(8,128)(2,1)S(1)}, u32[]{:S(2)}, u32[]{:S(2)}) collective-permute-start(bf16[54,2,8,128]{3,2,1,0:T(8,128)(2,1)S(1)} %get-tuple-element.32.rest_0_.refs_0_), channel_id=1, source_target_pairs={{0,4},{1,5},{2,6},{3,7},{4,0},{5,1},{6,2},{7,3},{8,12},{9,13},{10,... | collective-permute-start | bytes 663560 | tf_op jit(solution)/shard_map/ppermute | solution.py:334
  43.2 1.7 %right.3 = (bf16[48,1,8,128]{3,2,1,0:T(8,128)(2,1)S(1)}, bf16[48,1,8,128]{3,2,1,0:T(8,128)(2,1)S(1)}, bf16[48,1,8,128]{3,2,1,0:T(8,128)(2,1)S(1)}, bf16[48,1,8,128]{3,2,1,0:T(8,128)(2,1)S(1)}) custom-call(s32[1]{0:T(128)} %bitcast.me_ref, s32[192]{0:T(256)S(1)} %copy-done.10, f32[24,192,128]{2,1,0:T(8,128)S(1)} %copy-done, f32[24,384]{1,0:T(8,128)S(1)} %copy-done.8, ...), custom_call_target="tpu_custom_call" | custom-call | flops 134217728 | bytes 4000000 | tf_op jit(solution)/shard_map/right/pallas_call | solution.py:370
  44.9 9.7 %collective-permute-done.12.refs_3_ = bf16[54,2,8,128]{3,2,1,0:T(8,128)(2,1)S(1)} collective-permute-done((bf16[54,2,8,128]{3,2,1,0:T(8,128)(2,1)S(1)}, bf16[54,2,8,128]{3,2,1,0:T(8,128)(2,1)S(1)}, u32[]{:S(2)}, u32[]{:S(2)}) %collective-permute-start.12) | collective-permute-done | bytes 221216 | tf_op jit(solution)/shard_map/ppermute | solution.py:334
  54.6 1.6 %collective-permute-start.4 = (bf16[48,1,8,128]{3,2,1,0:T(8,128)(2,1)S(1)}, bf16[48,1,8,128]{3,2,1,0:T(8,128)(2,1)S(1)}, u32[]{:S(2)}, u32[]{:S(2)}) collective-permute-start(bf16[48,1,8,128]{3,2,1,0:T(8,128)(2,1)S(1)} %get-tuple-element.35), channel_id=1, source_target_pairs={{0,5},{1,4},{2,7},{3,6},{4,1},{5,0},{6,3},{7,2},{8,13},{9,12},{10,... | collective-permute-start | bytes 294920 | tf_op jit(solution)/shard_map/ppermute | solution.py:334
  56.2 0.5 collective-permute-start
  56.7 1.9 %collective-permute-start.5 = (bf16[48,1,8,128]{3,2,1,0:T(8,128)(2,1)S(1)}, bf16[48,1,8,128]{3,2,1,0:T(8,128)(2,1)S(1)}, u32[]{:S(2)}, u32[]{:S(2)}) collective-permute-start(bf16[48,1,8,128]{3,2,1,0:T(8,128)(2,1)S(1)} %get-tuple-element.36), channel_id=1, source_target_pairs={{0,6},{1,7},{2,4},{3,5},{4,2},{5,3},{6,0},{7,1},{8,14},{9,15},{10,... | collective-permute-start | bytes 294920 | tf_op jit(solution)/shard_map/ppermute | solution.py:334
  58.6 1.6 %collective-permute-start.1 = (bf16[48,1,8,128]{3,2,1,0:T(8,128)(2,1)S(1)}, bf16[48,1,8,128]{3,2,1,0:T(8,128)(2,1)S(1)}, u32[]{:S(2)}, u32[]{:S(2)}) collective-permute-start(bf16[48,1,8,128]{3,2,1,0:T(8,128)(2,1)S(1)} %get-tuple-element.36), channel_id=1, source_target_pairs={{0,2},{1,3},{2,0},{3,1},{4,6},{5,7},{6,4},{7,5},{8,10},{9,11},{10,... | collective-permute-start | bytes 294920 | tf_op jit(solution)/shard_map/ppermute | solution.py:334
  60.2 2.8 %collective-permute-start.6 = (bf16[48,1,8,128]{3,2,1,0:T(8,128)(2,1)S(1)}, bf16[48,1,8,128]{3,2,1,0:T(8,128)(2,1)S(1)}, u32[]{:S(2)}, u32[]{:S(2)}) collective-permute-start(bf16[48,1,8,128]{3,2,1,0:T(8,128)(2,1)S(1)} %get-tuple-element.37), channel_id=1, source_target_pairs={{0,7},{1,6},{2,5},{3,4},{4,3},{5,2},{6,1},{7,0},{8,15},{9,14},{10,... | collective-permute-start | bytes 294920 | tf_op jit(solution)/shard_map/ppermute | solution.py:334
  63.0 0.5 attention_in.1
  63.5 1.3 %shard_map.141 = (bf16[24,32,128]{2,1,0:T(8,128)(2,1)S(1)}, bf16[24,32,128]{2,1,0:T(8,128)(2,1)S(1)}, bf16[24,32,128]{2,1,0:T(8,128)(2,1)S(1)}, bf16[24,32,128]{2,1,0:T(8,128)(2,1)S(1)}) custom-call(s32[1]{0:T(128)} %bitcast.me_ref, bf16[54,2,8,128]{3,2,1,0:T(8,128)(2,1)S(1)} %get-tuple-element.32.rest_0_.refs_0_, ...), custom_call_target="tpu_custom_call" | custom-call | flops 201326592 | bytes 4000000 | tf_op jit(solution)/shard_map/pallas_call | solution.py:456
  64.8 1.2 %collective-permute-done.4.refs_5_ = bf16[48,1,8,128]{3,2,1,0:T(8,128)(2,1)S(1)} collective-permute-done((bf16[48,1,8,128]{3,2,1,0:T(8,128)(2,1)S(1)}, bf16[48,1,8,128]{3,2,1,0:T(8,128)(2,1)S(1)}, u32[]{:S(2)}, u32[]{:S(2)}) %collective-permute-start.4) | collective-permute-done | bytes 98336 | tf_op jit(solution)/shard_map/ppermute | solution.py:334
  66.0 0.9 collective-permute-start.20
  66.9 2.8 %collective-permute-start.22 = (bf16[24,32,128]{2,1,0:T(8,128)(2,1)S(1)}, bf16[24,32,128]{2,1,0:T(8,128)(2,1)S(1)}, u32[]{:S(2)}, u32[]{:S(2)}) collective-permute-start(bf16[24,32,128]{2,1,0:T(8,128)(2,1)S(1)} %get-tuple-element.57), channel_id=1, source_target_pairs={{0,3},{1,2},{2,1},{3,0},{4,7},{5,6},{6,5},{7,4},{8,11},{9,10},{10,... | collective-permute-start | bytes 589832 | tf_op jit(solution)/shard_map/ppermute | solution.py:334
  69.9 3.3 %collective-permute-start.3 = (bf16[48,1,8,128]{3,2,1,0:T(8,128)(2,1)S(1)}, bf16[48,1,8,128]{3,2,1,0:T(8,128)(2,1)S(1)}, u32[]{:S(2)}, u32[]{:S(2)}) collective-permute-start(bf16[48,1,8,128]{3,2,1,0:T(8,128)(2,1)S(1)} %get-tuple-element.34.refs_0_._), channel_id=1, source_target_pairs={{0,4},{1,5},{2,6},{3,7},{4,0},{5,1},{6,2},{7,3},{8,12},{9,13},{10,... | collective-permute-start | bytes 294920 | tf_op jit(solution)/shard_map/ppermute | solution.py:334
  73.3 2.0 %gate.1 = f32[24,192,128]{2,1,0:T(8,128)S(1)} custom-call(f32[24,192,128]{2,1,0:T(8,128)S(1)} %copy-done, bf16[128,128]{1,0:T(8,128)(2,1)S(1)} %copy-done.11, bf16[48,1,8,128]{3,2,1,0:T(8,128)(2,1)S(1)} %get-tuple-element.34.refs_0_._), custom_call_target="tpu_custom_call" | custom-call | flops 150994944 | bytes 4000000 | tf_op jit(solution)/shard_map/gate/pallas_call | solution.py:422
  75.2 5.3 %collective-permute-done.2.refs_3_ = bf16[48,1,8,128]{3,2,1,0:T(8,128)(2,1)S(1)} collective-permute-done((bf16[48,1,8,128]{3,2,1,0:T(8,128)(2,1)S(1)}, bf16[48,1,8,128]{3,2,1,0:T(8,128)(2,1)S(1)}, u32[]{:S(2)}, u32[]{:S(2)}) %collective-permute-start.2) | collective-permute-done | bytes 98336 | tf_op jit(solution)/shard_map/ppermute | solution.py:334
  80.5 1.2 %shard_map.140 = (bf16[24,16,128]{2,1,0:T(8,128)(2,1)S(1)}, bf16[24,16,128]{2,1,0:T(8,128)(2,1)S(1)}, bf16[24,16,128]{2,1,0:T(8,128)(2,1)S(1)}, bf16[24,16,128]{2,1,0:T(8,128)(2,1)S(1)}) custom-call(s32[1]{0:T(128)} %bitcast.me_ref, bf16[48,1,8,128]{3,2,1,0:T(8,128)(2,1)S(1)} %get-tuple-element.34.refs_0_._, ...), custom_call_target="tpu_custom_call" | custom-call | flops 201326592 | bytes 4000000 | tf_op jit(solution)/shard_map/pallas_call | solution.py:456
  81.7 0.7 collective-permute-start.17
  82.4 0.9 collective-permute-start.18
  83.4 1.9 %collective-permute-start.19 = (bf16[24,16,128]{2,1,0:T(8,128)(2,1)S(1)}, bf16[24,16,128]{2,1,0:T(8,128)(2,1)S(1)}, u32[]{:S(2)}, u32[]{:S(2)}) collective-permute-start(bf16[24,16,128]{2,1,0:T(8,128)(2,1)S(1)} %get-tuple-element.48), channel_id=1, source_target_pairs={{0,3},{1,2},{2,1},{3,0},{4,7},{5,6},{6,5},{7,4},{8,11},{9,10},{10,... | collective-permute-start | bytes 294920 | tf_op jit(solution)/shard_map/ppermute | solution.py:334
  85.3 6.7 %shard_map.142 = (f32[24,8,3,8,128]{4,3,2,1,0:T(8,128)}, f32[24,16,128]{2,1,0:T(8,128)S(1)}) custom-call(s32[1]{0:T(128)} %bitcast.me_ref, bf16[24,32,128]{2,1,0:T(8,128)(2,1)S(1)} %get-tuple-element.54.refs_0_, bf16[24,32,128]{2,1,0:T(8,128)(2,1)S(1)} %collective-permute-done.20.refs_1_, bf16[24,32,128]{2,1,0:T(8,128)(2,1)S(1)} %collective-permute-done.21.refs_2_, ...), custom_call_target="tpu_custom_call" | custom-call | flops 1308622848 | bytes 4000000 | tf_op jit(solution)/shard_map/pallas_call | solution.py:498
  92.1 4.2 %shard_map.143 = (f32[24,8,3,8,128]{4,3,2,1,0:T(8,128)}, f32[24,384]{1,0:T(8,128)}) custom-call(s32[1]{0:T(128)} %bitcast.me_ref, bf16[24,16,128]{2,1,0:T(8,128)(2,1)S(1)} %get-tuple-element.45.refs_0_, bf16[24,16,128]{2,1,0:T(8,128)(2,1)S(1)} %collective-permute-done.17.refs_1_, ...), custom_call_target="tpu_custom_call", output_to_operand_aliasing={{0}: (20, {})} | custom-call | flops 654311424 | bytes 4000000 | tf_op jit(solution)/shard_map/pallas_call | solution.py:498
  (49 shorter events, 0.3 us)
Async XLA Ops:
  0.6 15.6 %copy-start = (f32[24,192,128]{2,1,0:T(8,128)S(1)}, f32[24,192,128]{2,1,0:T(8,128)}, u32[]{:S(2)}) copy-start(f32[24,192,128]{2,1,0:T(8,128)} %pair_ref.7) | copy-start | bytes 7077892
  0.6 15.6 %copy-start.10 = (s32[192]{0:T(256)S(1)}, s32[192]{0:T(256)}, u32[]{:S(2)}) copy-start(s32[192]{0:T(256)} %refs_13_.1) | copy-start | bytes 2308
  0.7 15.6 %copy-start.1 = (bf16[128,512]{1,0:T(8,128)(2,1)S(1)}, bf16[128,512]{1,0:T(8,128)(2,1)}, u32[]{:S(2)}) copy-start(bf16[128,512]{1,0:T(8,128)(2,1)} %w_ref.5) | copy-start | bytes 393220
  0.7 42.5 %copy-start.8 = (f32[24,384]{1,0:T(8,128)S(1)}, f32[24,384]{1,0:T(8,128)}, u32[]{:S(2)}) copy-start(f32[24,384]{1,0:T(8,128)} %single_ref.3) | copy-start | bytes 110596
  5.2 21.7 %collective-permute-start.14 = (bf16[54,2,8,128]{3,2,1,0:T(8,128)(2,1)S(1)}, bf16[54,2,8,128]{3,2,1,0:T(8,128)(2,1)S(1)}, u32[]{:S(2)}, u32[]{:S(2)}) collective-permute-start(bf16[54,2,8,128]{3,2,1,0:T(8,128)(2,1)S(1)} %get-tuple-element.41), channel_id=1, source_target_pairs={{0,5},{1,4},{2,7},{3,6},{4,1},{5,0},{6,3},{7,2},{8,13},{9,12},{10,... | collective-permute-start | bytes 663560 | tf_op jit(solution)/shard_map/ppermute | solution.py:334
  10.3 18.7 %collective-permute-start.10 = (bf16[54,2,8,128]{3,2,1,0:T(8,128)(2,1)S(1)}, bf16[54,2,8,128]{3,2,1,0:T(8,128)(2,1)S(1)}, u32[]{:S(2)}, u32[]{:S(2)}) collective-permute-start(bf16[54,2,8,128]{3,2,1,0:T(8,128)(2,1)S(1)} %get-tuple-element.41), channel_id=1, source_target_pairs={{0,1},{1,0},{2,3},{3,2},{4,5},{5,4},{6,7},{7,6},{8,9},{9,8},{10,11... | collective-permute-start | bytes 663560 | tf_op jit(solution)/shard_map/ppermute | solution.py:334
  10.8 18.2 %collective-permute-start.15 = (bf16[54,2,8,128]{3,2,1,0:T(8,128)(2,1)S(1)}, bf16[54,2,8,128]{3,2,1,0:T(8,128)(2,1)S(1)}, u32[]{:S(2)}, u32[]{:S(2)}) collective-permute-start(bf16[54,2,8,128]{3,2,1,0:T(8,128)(2,1)S(1)} %get-tuple-element.42), channel_id=1, source_target_pairs={{0,6},{1,7},{2,4},{3,5},{4,2},{5,3},{6,0},{7,1},{8,14},{9,15},{10,... | collective-permute-start | bytes 663560 | tf_op jit(solution)/shard_map/ppermute | solution.py:334
  12.1 24.0 %collective-permute-start.11 = (bf16[54,2,8,128]{3,2,1,0:T(8,128)(2,1)S(1)}, bf16[54,2,8,128]{3,2,1,0:T(8,128)(2,1)S(1)}, u32[]{:S(2)}, u32[]{:S(2)}) collective-permute-start(bf16[54,2,8,128]{3,2,1,0:T(8,128)(2,1)S(1)} %get-tuple-element.42), channel_id=1, source_target_pairs={{0,2},{1,3},{2,0},{3,1},{4,6},{5,7},{6,4},{7,5},{8,10},{9,11},{10,... | collective-permute-start | bytes 663560 | tf_op jit(solution)/shard_map/ppermute | solution.py:334
  12.3 23.8 %collective-permute-start.16 = (bf16[54,2,8,128]{3,2,1,0:T(8,128)(2,1)S(1)}, bf16[54,2,8,128]{3,2,1,0:T(8,128)(2,1)S(1)}, u32[]{:S(2)}, u32[]{:S(2)}) collective-permute-start(bf16[54,2,8,128]{3,2,1,0:T(8,128)(2,1)S(1)} %get-tuple-element.43), channel_id=1, source_target_pairs={{0,7},{1,6},{2,5},{3,4},{4,3},{5,2},{6,1},{7,0},{8,15},{9,14},{10,... | collective-permute-start | bytes 663560 | tf_op jit(solution)/shard_map/ppermute | solution.py:334
  16.2 46.8 %copy-start.3 = (bf16[384,768]{1,0:T(8,128)(2,1)S(1)}, bf16[384,768]{1,0:T(8,128)(2,1)}, u32[]{:S(2)}) copy-start(bf16[384,768]{1,0:T(8,128)(2,1)} %refs_10_.1) | copy-start | bytes 1769476
  16.2 46.8 %copy-start.5 = (bf16[384,384]{1,0:T(8,128)(2,1)S(1)}, bf16[384,384]{1,0:T(8,128)(2,1)}, u32[]{:S(2)}) copy-start(bf16[384,384]{1,0:T(8,128)(2,1)} %refs_8_.3) | copy-start | bytes 884740
  16.2 46.8 %copy-start.6 = (bf16[384,384]{1,0:T(8,128)(2,1)S(1)}, bf16[384,384]{1,0:T(8,128)(2,1)}, u32[]{:S(2)}) copy-start(bf16[384,384]{1,0:T(8,128)(2,1)} %refs_9_.1) | copy-start | bytes 884740
  26.9 29.8 %collective-permute-start.7 = (bf16[48,3,8,128]{3,2,1,0:T(8,128)(2,1)S(1)}, bf16[48,3,8,128]{3,2,1,0:T(8,128)(2,1)S(1)}, u32[]{:S(2)}, u32[]{:S(2)}) collective-permute-start(bf16[48,3,8,128]{3,2,1,0:T(8,128)(2,1)S(1)} %get-tuple-element.38), channel_id=1, source_target_pairs={{0,1},{1,0},{2,3},{3,2},{4,5},{5,4},{6,7},{7,6},{8,9},{9,8},{10,11... | collective-permute-start | bytes 884744 | tf_op jit(solution)/shard_map/ppermute | solution.py:334
  28.9 29.7 %collective-permute-start.8 = (bf16[48,3,8,128]{3,2,1,0:T(8,128)(2,1)S(1)}, bf16[48,3,8,128]{3,2,1,0:T(8,128)(2,1)S(1)}, u32[]{:S(2)}, u32[]{:S(2)}) collective-permute-start(bf16[48,3,8,128]{3,2,1,0:T(8,128)(2,1)S(1)} %get-tuple-element.39), channel_id=1, source_target_pairs={{0,2},{1,3},{2,0},{3,1},{4,6},{5,7},{6,4},{7,5},{8,10},{9,11},{10,... | collective-permute-start | bytes 884744 | tf_op jit(solution)/shard_map/ppermute | solution.py:334
  28.9 31.3 %collective-permute-start.9 = (bf16[48,3,8,128]{3,2,1,0:T(8,128)(2,1)S(1)}, bf16[48,3,8,128]{3,2,1,0:T(8,128)(2,1)S(1)}, u32[]{:S(2)}, u32[]{:S(2)}) collective-permute-start(bf16[48,3,8,128]{3,2,1,0:T(8,128)(2,1)S(1)} %get-tuple-element.40), channel_id=1, source_target_pairs={{0,3},{1,2},{2,1},{3,0},{4,7},{5,6},{6,5},{7,4},{8,11},{9,10},{10,... | collective-permute-start | bytes 884744 | tf_op jit(solution)/shard_map/ppermute | solution.py:334
  36.1 18.5 %collective-permute-start.12 = (bf16[54,2,8,128]{3,2,1,0:T(8,128)(2,1)S(1)}, bf16[54,2,8,128]{3,2,1,0:T(8,128)(2,1)S(1)}, u32[]{:S(2)}, u32[]{:S(2)}) collective-permute-start(bf16[54,2,8,128]{3,2,1,0:T(8,128)(2,1)S(1)} %get-tuple-element.43), channel_id=1, source_target_pairs={{0,3},{1,2},{2,1},{3,0},{4,7},{5,6},{6,5},{7,4},{8,11},{9,10},{10,... | collective-permute-start | bytes 663560 | tf_op jit(solution)/shard_map/ppermute | solution.py:334
  36.1 20.1 %collective-permute-start.13 = (bf16[54,2,8,128]{3,2,1,0:T(8,128)(2,1)S(1)}, bf16[54,2,8,128]{3,2,1,0:T(8,128)(2,1)S(1)}, u32[]{:S(2)}, u32[]{:S(2)}) collective-permute-start(bf16[54,2,8,128]{3,2,1,0:T(8,128)(2,1)S(1)} %get-tuple-element.32.rest_0_.refs_0_), channel_id=1, source_target_pairs={{0,4},{1,5},{2,6},{3,7},{4,0},{5,1},{6,2},{7,3},{8,12},{9,13},{10,... | collective-permute-start | bytes 663560 | tf_op jit(solution)/shard_map/ppermute | solution.py:334
  54.6 11.3 %collective-permute-start.4 = (bf16[48,1,8,128]{3,2,1,0:T(8,128)(2,1)S(1)}, bf16[48,1,8,128]{3,2,1,0:T(8,128)(2,1)S(1)}, u32[]{:S(2)}, u32[]{:S(2)}) collective-permute-start(bf16[48,1,8,128]{3,2,1,0:T(8,128)(2,1)S(1)} %get-tuple-element.35), channel_id=1, source_target_pairs={{0,5},{1,4},{2,7},{3,6},{4,1},{5,0},{6,3},{7,2},{8,13},{9,12},{10,... | collective-permute-start | bytes 294920 | tf_op jit(solution)/shard_map/ppermute | solution.py:334
  56.2 10.7 %collective-permute-start = (bf16[48,1,8,128]{3,2,1,0:T(8,128)(2,1)S(1)}, bf16[48,1,8,128]{3,2,1,0:T(8,128)(2,1)S(1)}, u32[]{:S(2)}, u32[]{:S(2)}) collective-permute-start(bf16[48,1,8,128]{3,2,1,0:T(8,128)(2,1)S(1)} %get-tuple-element.35), channel_id=1, source_target_pairs={{0,1},{1,0},{2,3},{3,2},{4,5},{5,4},{6,7},{7,6},{8,9},{9,8},{10,11... | collective-permute-start | bytes 294920 | tf_op jit(solution)/shard_map/ppermute | solution.py:334
  56.7 10.2 %collective-permute-start.5 = (bf16[48,1,8,128]{3,2,1,0:T(8,128)(2,1)S(1)}, bf16[48,1,8,128]{3,2,1,0:T(8,128)(2,1)S(1)}, u32[]{:S(2)}, u32[]{:S(2)}) collective-permute-start(bf16[48,1,8,128]{3,2,1,0:T(8,128)(2,1)S(1)} %get-tuple-element.36), channel_id=1, source_target_pairs={{0,6},{1,7},{2,4},{3,5},{4,2},{5,3},{6,0},{7,1},{8,14},{9,15},{10,... | collective-permute-start | bytes 294920 | tf_op jit(solution)/shard_map/ppermute | solution.py:334
  58.6 11.0 %collective-permute-start.1 = (bf16[48,1,8,128]{3,2,1,0:T(8,128)(2,1)S(1)}, bf16[48,1,8,128]{3,2,1,0:T(8,128)(2,1)S(1)}, u32[]{:S(2)}, u32[]{:S(2)}) collective-permute-start(bf16[48,1,8,128]{3,2,1,0:T(8,128)(2,1)S(1)} %get-tuple-element.36), channel_id=1, source_target_pairs={{0,2},{1,3},{2,0},{3,1},{4,6},{5,7},{6,4},{7,5},{8,10},{9,11},{10,... | collective-permute-start | bytes 294920 | tf_op jit(solution)/shard_map/ppermute | solution.py:334
  60.2 9.7 %collective-permute-start.6 = (bf16[48,1,8,128]{3,2,1,0:T(8,128)(2,1)S(1)}, bf16[48,1,8,128]{3,2,1,0:T(8,128)(2,1)S(1)}, u32[]{:S(2)}, u32[]{:S(2)}) collective-permute-start(bf16[48,1,8,128]{3,2,1,0:T(8,128)(2,1)S(1)} %get-tuple-element.37), channel_id=1, source_target_pairs={{0,7},{1,6},{2,5},{3,4},{4,3},{5,2},{6,1},{7,0},{8,15},{9,14},{10,... | collective-permute-start | bytes 294920 | tf_op jit(solution)/shard_map/ppermute | solution.py:334
  66.0 17.4 %collective-permute-start.20 = (bf16[24,32,128]{2,1,0:T(8,128)(2,1)S(1)}, bf16[24,32,128]{2,1,0:T(8,128)(2,1)S(1)}, u32[]{:S(2)}, u32[]{:S(2)}) collective-permute-start(bf16[24,32,128]{2,1,0:T(8,128)(2,1)S(1)} %get-tuple-element.55), channel_id=1, source_target_pairs={{0,1},{1,0},{2,3},{3,2},{4,5},{5,4},{6,7},{7,6},{8,9},{9,8},{10,11... | collective-permute-start | bytes 589832 | tf_op jit(solution)/shard_map/ppermute | solution.py:334
  66.9 18.4 %collective-permute-start.21 = (bf16[24,32,128]{2,1,0:T(8,128)(2,1)S(1)}, bf16[24,32,128]{2,1,0:T(8,128)(2,1)S(1)}, u32[]{:S(2)}, u32[]{:S(2)}) collective-permute-start(bf16[24,32,128]{2,1,0:T(8,128)(2,1)S(1)} %get-tuple-element.56), channel_id=1, source_target_pairs={{0,2},{1,3},{2,0},{3,1},{4,6},{5,7},{6,4},{7,5},{8,10},{9,11},{10,... | collective-permute-start | bytes 589832 | tf_op jit(solution)/shard_map/ppermute | solution.py:334
  66.9 18.4 %collective-permute-start.22 = (bf16[24,32,128]{2,1,0:T(8,128)(2,1)S(1)}, bf16[24,32,128]{2,1,0:T(8,128)(2,1)S(1)}, u32[]{:S(2)}, u32[]{:S(2)}) collective-permute-start(bf16[24,32,128]{2,1,0:T(8,128)(2,1)S(1)} %get-tuple-element.57), channel_id=1, source_target_pairs={{0,3},{1,2},{2,1},{3,0},{4,7},{5,6},{6,5},{7,4},{8,11},{9,10},{10,... | collective-permute-start | bytes 589832 | tf_op jit(solution)/shard_map/ppermute | solution.py:334
  69.7 10.8 %collective-permute-start.2 = (bf16[48,1,8,128]{3,2,1,0:T(8,128)(2,1)S(1)}, bf16[48,1,8,128]{3,2,1,0:T(8,128)(2,1)S(1)}, u32[]{:S(2)}, u32[]{:S(2)}) collective-permute-start(bf16[48,1,8,128]{3,2,1,0:T(8,128)(2,1)S(1)} %get-tuple-element.37), channel_id=1, source_target_pairs={{0,3},{1,2},{2,1},{3,0},{4,7},{5,6},{6,5},{7,4},{8,11},{9,10},{10,... | collective-permute-start | bytes 294920 | tf_op jit(solution)/shard_map/ppermute | solution.py:334
  69.9 15.4 %copy-start.9 = (bf16[128,128]{1,0:T(8,128)(2,1)S(1)}, bf16[128,128]{1,0:T(8,128)(2,1)}, u32[]{:S(2)}) copy-start(bf16[128,128]{1,0:T(8,128)(2,1)} %param.18) | copy-start | bytes 98308
  69.9 15.4 %copy-start.12 = (bf16[128,16]{0,1:T(8,128)(2,1)S(1)}, bf16[128,16]{0,1:T(8,128)(2,1)}, u32[]{:S(2)}) copy-start(bf16[128,16]{0,1:T(8,128)(2,1)} %param.21) | copy-start | bytes 12292
  69.9 10.6 %collective-permute-start.3 = (bf16[48,1,8,128]{3,2,1,0:T(8,128)(2,1)S(1)}, bf16[48,1,8,128]{3,2,1,0:T(8,128)(2,1)S(1)}, u32[]{:S(2)}, u32[]{:S(2)}) collective-permute-start(bf16[48,1,8,128]{3,2,1,0:T(8,128)(2,1)S(1)} %get-tuple-element.34.refs_0_._), channel_id=1, source_target_pairs={{0,4},{1,5},{2,6},{3,7},{4,0},{5,1},{6,2},{7,3},{8,12},{9,13},{10,... | collective-permute-start | bytes 294920 | tf_op jit(solution)/shard_map/ppermute | solution.py:334
  81.7 10.3 %collective-permute-start.17 = (bf16[24,16,128]{2,1,0:T(8,128)(2,1)S(1)}, bf16[24,16,128]{2,1,0:T(8,128)(2,1)S(1)}, u32[]{:S(2)}, u32[]{:S(2)}) collective-permute-start(bf16[24,16,128]{2,1,0:T(8,128)(2,1)S(1)} %get-tuple-element.46), channel_id=1, source_target_pairs={{0,1},{1,0},{2,3},{3,2},{4,5},{5,4},{6,7},{7,6},{8,9},{9,8},{10,11... | collective-permute-start | bytes 294920 | tf_op jit(solution)/shard_map/ppermute | solution.py:334
  82.4 9.7 %collective-permute-start.18 = (bf16[24,16,128]{2,1,0:T(8,128)(2,1)S(1)}, bf16[24,16,128]{2,1,0:T(8,128)(2,1)S(1)}, u32[]{:S(2)}, u32[]{:S(2)}) collective-permute-start(bf16[24,16,128]{2,1,0:T(8,128)(2,1)S(1)} %get-tuple-element.47), channel_id=1, source_target_pairs={{0,2},{1,3},{2,0},{3,1},{4,6},{5,7},{6,4},{7,5},{8,10},{9,11},{10,... | collective-permute-start | bytes 294920 | tf_op jit(solution)/shard_map/ppermute | solution.py:334
  83.4 8.7 %collective-permute-start.19 = (bf16[24,16,128]{2,1,0:T(8,128)(2,1)S(1)}, bf16[24,16,128]{2,1,0:T(8,128)(2,1)S(1)}, u32[]{:S(2)}, u32[]{:S(2)}) collective-permute-start(bf16[24,16,128]{2,1,0:T(8,128)(2,1)S(1)} %get-tuple-element.48), channel_id=1, source_target_pairs={{0,3},{1,2},{2,1},{3,0},{4,7},{5,6},{6,5},{7,4},{8,11},{9,10},{10,... | collective-permute-start | bytes 294920 | tf_op jit(solution)/shard_map/ppermute | solution.py:334
  (4 other events, 50.6 us)

commit v4 on v3

--- a/solution.py
+++ b/solution.py
@@ -55,25 +55,15 @@
             part = edge[s * per_set : (s + 1) * per_set]
             head_ref[pl.ds(at, per_set), :] = part[:, :LANES]
             rest_ref[pl.ds(at, per_set), :] = part[:, LANES:]
-    step = pl.program_id(0)
+    step, tiles = pl.program_id(0), pl.num_programs(0)
     low = first_half_lanes((SUB, LANES))
     for q in range(sets):
         for c in range(pairs):
             a = pl.ds(q * per_set + c, SUB, stride=stride)
             b = pl.ds(q * per_set + pairs + c, SUB, stride=stride)
-            out_refs[q][c, step] = head_ref[a, :].astype(bf16)
-            out_refs[q][pairs + c, step] = head_ref[b, :].astype(bf16)
-            out_refs[q][per_set + c, step] = jnp.where(low, rest_ref[a, :], rest_ref[b, :]).astype(bf16)
-
-
-def single_places(shape, tiles):
-    pieces = shape[1] // LANES * (shape[0] // SUB)
-    return {n: divmod(n, tiles) for n in range(pieces)}
-
-
-def single_slabs(shape, tiles, message):
-    least = -(-(shape[1] // LANES * (shape[0] // SUB)) // tiles)
-    return next(n for n in range(least, message + 1) if message % n == 0)
+            out_refs[q][c * tiles + step] = head_ref[a, :].astype(bf16)
+            out_refs[q][(pairs + c) * tiles + step] = head_ref[b, :].astype(bf16)
+            out_refs[q][(per_set + c) * tiles + step] = jnp.where(low, rest_ref[a, :], rest_ref[b, :]).astype(bf16)
 
 
 def right_kernel(hidden, full, sets, row_count, offset, single_tiles, me_ref, mask_ref, pair_ref, single_ref, live_ref, w_ref, *rest):
@@ -89,18 +79,16 @@
     rows_of = lambda j: layer_norm(pair_ref[at + j], 1).astype(bf16)
     edges_to_messages(me_ref, mask_ref, live_ref, wt_ref, rows_of, head_ref, rest_ref, out_refs, first, hidden, full)
     if single_tiles:
-        single_normed = layer_norm(single_ref[...], 1)
-        base = hidden // sets * 3 // 2
-        for g in range(single_tiles):
-
-            @pl.when(pl.program_id(0) == g)
-            def _():
-                for n, (slab, tile) in single_places(single_ref.shape, single_tiles).items():
-                    if tile == g:
-                        t, at = divmod(n, row_count // SUB)
-                        part = single_normed[at * SUB : (at + 1) * SUB, t * LANES : (t + 1) * LANES].astype(bf16)
-                        for q in range(sets):
-                            out_refs[q][base + slab, tile] = part
+
+        @pl.when(pl.program_id(0) == 0)
+        def _():
+            single_normed = layer_norm(single_ref[...], 1)
+            base = hidden // sets * 3 // 2 * single_tiles
+            for n in range(single_ref.shape[1] // LANES * (row_count // SUB)):
+                t, at = divmod(n, row_count // SUB)
+                part = single_normed[at * SUB : (at + 1) * SUB, t * LANES : (t + 1) * LANES].astype(bf16)
+                for q in range(sets):
+                    out_refs[q][base + n] = part
 
 
 def left_kernel(hidden, full, sets, row_count, me_ref, mask_ref, pair_ref, live_ref, w_ref, *rest):
@@ -134,31 +122,31 @@
     return wide.reshape(wide.shape[0] * wide.shape[1], wide.shape[2])
 
 
-def triangle_kernel(groups, sets, per_set, me_ref, *refs):
+def triangle_kernel(groups, sets, per_set, here, me_ref, *refs):
     right_refs, left_refs = refs[:groups], refs[groups : groups + sets]
     out_refs = refs[-sets - 3 : -3]
     head_ref, rest_ref, sums_ref = refs[-3:]
     pairs = per_set // 2
-    rows = left_refs[0].shape[1] * SUB
-    here = right_refs[0].shape[1] * SUB
+    rows = left_refs[0].shape[0] // (per_set + pairs) * SUB
     columns = groups * here
     me = me_ref[0]
     total = sets * rows
     stride = total + SUB
     low = first_half_lanes((total, LANES))
+    mine = lambda r, c: plain_rows(r[c * rows // SUB : (c + 1) * rows // SUB])
     fill = lambda x: x if columns == LANES else jnp.concatenate([x, x], axis=0)
     for s in range(groups):
         d = lax.bitwise_xor(me, s)
-        wide = right_refs[s][: per_set + pairs].astype(f32).reshape(per_set + pairs, here, LANES)
+        wide = right_refs[s][: (per_set + pairs) * here // SUB].astype(f32).reshape(per_set + pairs, here, LANES)
         head_ref[:, d] = wide[:per_set]
         rest_ref[:, d] = wide[per_set:]
     for c in range(pairs):
         right_rest = fill(rest_ref[c].reshape(columns, LANES)).astype(bf16)
-        left_rest = jnp.concatenate([plain_rows(r[per_set + c]) for r in left_refs], axis=0)
+        left_rest = jnp.concatenate([mine(r, per_set + c) for r in left_refs], axis=0)
         for p in range(2):
             channel = p * pairs + c
             right = fill(head_ref[channel].reshape(columns, LANES)).astype(bf16)
-            left = jnp.concatenate([plain_rows(r[channel]) for r in left_refs], axis=0).astype(bf16)
+            left = jnp.concatenate([mine(r, channel) for r in left_refs], axis=0).astype(bf16)
             kept = jnp.where(low if p == 0 else jnp.logical_not(low), left_rest, 0.0).astype(bf16)
             sums_ref[channel * stride : channel * stride + total, :] = lax.dot_general(
                 jnp.concatenate([left, kept], axis=1),
@@ -176,26 +164,24 @@
 
 
 def attention_in_kernel(groups, chunks, message, me_ref, *refs):
-    n = len(chunks)
+    count = len(chunks)
     right_refs = refs[:groups]
     w_query_ref, w_key_ref, w_value_gate_ref, q_ref, g_ref = refs[groups : groups + 5]
-    k_refs, v_refs = refs[groups + 5 : groups + 5 + n], refs[groups + 5 + n : groups + 5 + 2 * n]
+    k_refs, v_refs = refs[groups + 5 : groups + 5 + count], refs[groups + 5 + count : groups + 5 + 2 * count]
     all_ref = refs[-1]
     channels = w_query_ref.shape[0]
     me = me_ref[0]
     tiles = all_ref.shape[1] // SUB
     for s in range(groups):
         d = lax.bitwise_xor(me, s)
-        for place, (slab, tile) in single_places(q_ref.shape, right_refs[s].shape[1]).items():
-            t, at = divmod(place, tiles)
-            all_ref[d, at * SUB : (at + 1) * SUB, t * LANES : (t + 1) * LANES] = right_refs[s][
-                message + slab, tile
-            ].astype(f32)
+        for n in range(channels // LANES * tiles):
+            t, at = divmod(n, tiles)
+            all_ref[d, at * SUB : (at + 1) * SUB, t * LANES : (t + 1) * LANES] = right_refs[s][message + n].astype(f32)
     own = all_ref[me].astype(bf16)
     q_ref[...] = jnp.dot(own, w_query_ref[...], preferred_element_type=f32).astype(bf16)
     g_ref[...] = sigmoid(jnp.dot(own, w_value_gate_ref[:, channels:], preferred_element_type=f32))
     first = 0
-    for k in range(n):
+    for k in range(count):
         every = all_ref[:, first * SUB : (first + chunks[k]) * SUB].reshape(k_refs[k].shape).astype(bf16)
         k_refs[k][...] = jnp.dot(every, w_key_ref[...], preferred_element_type=f32).astype(bf16)
         v_refs[k][...] = jnp.dot(every, w_value_gate_ref[:, :channels], preferred_element_type=f32).astype(bf16)
@@ -352,10 +338,10 @@
     inner_width = w_trans_out.shape[0]
     heads = w_bias.shape[1]
     channels = single.shape[1]
-    slabs = single_slabs(single.shape, chunk_tiles(row_count // SUB, groups)[0], message)
     full = length // LANES * LANES
     lanes = full + LANES
     tiles = row_count // SUB
+    singles = channels // LANES * tiles
     chunks = chunk_tiles(tiles, groups)
     starts = [sum(chunks[:k]) for k in range(len(chunks))]
     me = lax.axis_index("row").astype(jnp.int32).reshape(1)
@@ -366,7 +352,7 @@
 
     def right_edges(k, after):
         at = starts[k]
-        size = message + (0 if k else slabs)
+        size = message * chunks[k] + (0 if k else singles)
         return pl.pallas_call(
             functools.partial(right_kernel, hidden, full, sets, row_count, at * SUB, 0 if k else chunks[0]),
             name="right",
@@ -383,7 +369,7 @@
                 out_specs=in_vmem([None] * sets),
                 scratch_shapes=edge_scratch,
             ),
-            out_shape=[sds((size, chunks[k], SUB, LANES), bf16)] * sets,
+            out_shape=[sds((size, SUB, LANES), bf16)] * sets,
             compiler_params=params(vmem_limit_bytes=24 * 2**20),
             cost_estimate=cost(edge_flops * chunks[k]),
         )(me, token_mask, *([near, single, token_mask, w_tri_proj] if k else kept([pair, single, token_mask, w_tri_proj])), *after)
@@ -404,7 +390,7 @@
                 out_specs=in_vmem([None] * sets),
                 scratch_shapes=edge_scratch,
             ),
-            out_shape=[sds((message, tiles, SUB, LANES), bf16)] * sets,
+            out_shape=[sds((message * tiles, SUB, LANES), bf16)] * sets,
             compiler_params=params(vmem_limit_bytes=24 * 2**20),
             cost_estimate=cost(edge_flops * tiles),
         )(me, token_mask, near, token_mask, w_tri_proj, *after)
@@ -431,7 +417,7 @@
 
     tokens = [groups * n * SUB for n in chunks]
     queries, att_gate, *keys_values = pl.pallas_call(
-        functools.partial(attention_in_kernel, groups, chunks, message),
+        functools.partial(attention_in_kernel, groups, chunks, message * chunks[0]),
         name="attention_in",
         grid_spec=pltpu.PrefetchScalarGridSpec(
             num_scalar_prefetch=1,
@@ -454,7 +440,7 @@
         columns = groups * chunks[k] * SUB
         sums_shape = (row_count, per_set * columns // LANES, LANES)
         sums = pl.pallas_call(
-            functools.partial(triangle_kernel, groups, sets, per_set),
+            functools.partial(triangle_kernel, groups, sets, per_set, chunks[k] * SUB),
             grid_spec=pltpu.PrefetchScalarGridSpec(
                 num_scalar_prefetch=1,
                 grid=(1,),
@@ -479,7 +465,7 @@
         attends = len(chunks) if k == len(chunks) - 1 else 0
         columns = tokens[k]
         together = LANES // columns
-        take = row_count if attends else SUB
+        take = row_count
         slab = take // together
         at = starts[k] // n
         part_rows = pl.BlockSpec((take, groups, n, SUB, width), lambda g, *_, at=at: (g, 0, at, 0, 0))
@@ -503,7 +489,7 @@
                 in_specs=in_specs,
                 out_specs=[
                     part_rows,
-                    whole_block(single.shape) if attends else pl.BlockSpec((SUB, heads, LANES), lambda g, *_: (g, 0, 0)),
+                    whole_block(single.shape) if attends else pl.BlockSpec((take, heads, LANES), lambda g, *_: (g, 0, 0)),
                 ],
                 scratch_shapes=([pltpu.VMEM(bias_shape, f32)] if attends else []) + weights,
             ),

time: 96.4 us -> 94.7 us (0.982)
    pallas_call x2, Pallas kernels: 10.9 us -> 9.73 us  [fast_body(): pl.pallas_call(functools.partial(tail_kernel, sets, per_set, heads, slab,...]
  transfers between devices with their start and end apart: 23 -> 23, of which waited for: 4 -> 4; matrix products, arithmetic and copies ran while one was open for 0% -> 0% of each run, Pallas kernels for 18% -> 17%
where the time goes in v4:
time: 94.7 us; the launch traced here: 94.5 us
  starting transfers between devices  46 us (49%)
  Pallas kernels  25.2 us (27%)
  waiting for transfers between devices  22.3 us (24%)
    ppermute x23, starting transfers between devices, exchange(): lax.ppermute(x, 'row', [(r, r ^ s) for r in range(groups)])  46 us
    ppermute x23, waiting for transfers between devices, exchange(): lax.ppermute(x, 'row', [(r, r ^ s) for r in range(groups)])  22.3 us
    pallas_call x2, Pallas kernels, fast_body(): pl.pallas_call(functools.partial(tail_kernel, sets, per_set, heads, slab,...  9.73 us
    pallas_call x2, Pallas kernels, right_edges(): pl.pallas_call(functools.partial(right_kernel, hidden, full, sets, row_co...  6.38 us
    pallas_call x1, Pallas kernels, left_edges(): pl.pallas_call(functools.partial(left_kernel, hidden, full, sets, row_cou...  4.08 us
    pallas_call x2, Pallas kernels, fast_body(): pl.pallas_call(functools.partial(triangle_kernel, groups, sets, per_set,...  2.44 us
    pallas_call x1, Pallas kernels, fast_body(): pl.pallas_call(gate_kernel, name='gate', in_specs=in_vmem([near, w_tri_ga...  2.13 us
  transfers between devices with their start and end apart: 23, of which 4 were waited for; matrix products, arithmetic and copies ran while one was open for 0% of the time, Pallas kernels for 17%

profile of v4, /device:TPU:0, one launch (start us, length us, event | category | flops | bytes accessed | tf_op | source)
XLA Modules:
  0.0 94.5 jit_solution(12510234053444158196)
XLA Ops:
  0.7 4.6 %right.2 = (bf16[105,8,128]{2,1,0:T(8,128)(2,1)S(1)}, bf16[105,8,128]{2,1,0:T(8,128)(2,1)S(1)}, bf16[105,8,128]{2,1,0:T(8,128)(2,1)S(1)}, bf16[105,8,128]{2,1,0:T(8,128)(2,1)S(1)}) custom-call(s32[1]{0:T(128)} %bitcast.me_ref, s32[192]{0:T(256)} %refs_13_.1, f32[24,192,128]{2,1,0:T(8,128)} %pair_ref.7, f32[24,384]{1,0:T(8,128)} %single_ref.3, s32[192]{0:T(256)} %refs_13_.1, ...), custom_call_target="tpu_custom_call" | custom-call | flops 268435456 | bytes 4000000 | tf_op jit(solution)/shard_map/right/pallas_call | solution.py:356
  5.3 5.1 %collective-permute-start.14 = (bf16[105,8,128]{2,1,0:T(8,128)(2,1)S(1)}, bf16[105,8,128]{2,1,0:T(8,128)(2,1)S(1)}, u32[]{:S(2)}, u32[]{:S(2)}) collective-permute-start(bf16[105,8,128]{2,1,0:T(8,128)(2,1)S(1)} %get-tuple-element.41), channel_id=1, source_target_pairs={{0,5},{1,4},{2,7},{3,6},{4,1},{5,0},{6,3},{7,2},{8,13},{9,12},{10,... | collective-permute-start | bytes 645128 | tf_op jit(solution)/shard_map/ppermute | solution.py:320
  10.4 0.5 collective-permute-start.10
  10.9 1.4 %collective-permute-start.15 = (bf16[105,8,128]{2,1,0:T(8,128)(2,1)S(1)}, bf16[105,8,128]{2,1,0:T(8,128)(2,1)S(1)}, u32[]{:S(2)}, u32[]{:S(2)}) collective-permute-start(bf16[105,8,128]{2,1,0:T(8,128)(2,1)S(1)} %get-tuple-element.42), channel_id=1, source_target_pairs={{0,6},{1,7},{2,4},{3,5},{4,2},{5,3},{6,0},{7,1},{8,14},{9,15},{10,... | collective-permute-start | bytes 645128 | tf_op jit(solution)/shard_map/ppermute | solution.py:320
  12.3 0.2 collective-permute-start.11
  12.5 3.9 %collective-permute-start.16 = (bf16[105,8,128]{2,1,0:T(8,128)(2,1)S(1)}, bf16[105,8,128]{2,1,0:T(8,128)(2,1)S(1)}, u32[]{:S(2)}, u32[]{:S(2)}) collective-permute-start(bf16[105,8,128]{2,1,0:T(8,128)(2,1)S(1)} %get-tuple-element.43), channel_id=1, source_target_pairs={{0,7},{1,6},{2,5},{3,4},{4,3},{5,2},{6,1},{7,0},{8,15},{9,14},{10,... | collective-permute-start | bytes 645128 | tf_op jit(solution)/shard_map/ppermute | solution.py:320
  16.4 4.1 %left.1 = (bf16[144,8,128]{2,1,0:T(8,128)(2,1)S(1)}, bf16[144,8,128]{2,1,0:T(8,128)(2,1)S(1)}, bf16[144,8,128]{2,1,0:T(8,128)(2,1)S(1)}, bf16[144,8,128]{2,1,0:T(8,128)(2,1)S(1)}) custom-call(s32[1]{0:T(128)} %bitcast.me_ref, s32[192]{0:T(256)S(1)} %copy-done.10, f32[24,192,128]{2,1,0:T(8,128)S(1)} %copy-done, s32[192]{0:T(256)S(1)} %copy-done.10, ...), custom_call_target="tpu_custom_call" | custom-call | flops 402653184 | bytes 4000000 | tf_op jit(solution)/shard_map/left/pallas_call | solution.py:378
  20.5 6.1 %collective-permute-done.14.refs_5_ = bf16[105,8,128]{2,1,0:T(8,128)(2,1)S(1)} collective-permute-done((bf16[105,8,128]{2,1,0:T(8,128)(2,1)S(1)}, bf16[105,8,128]{2,1,0:T(8,128)(2,1)S(1)}, u32[]{:S(2)}, u32[]{:S(2)}) %collective-permute-start.14) | collective-permute-done | bytes 215072 | tf_op jit(solution)/shard_map/ppermute | solution.py:320
  26.6 2.0 %collective-permute-start.7 = (bf16[144,8,128]{2,1,0:T(8,128)(2,1)S(1)}, bf16[144,8,128]{2,1,0:T(8,128)(2,1)S(1)}, u32[]{:S(2)}, u32[]{:S(2)}) collective-permute-start(bf16[144,8,128]{2,1,0:T(8,128)(2,1)S(1)} %get-tuple-element.38), channel_id=1, source_target_pairs={{0,1},{1,0},{2,3},{3,2},{4,5},{5,4},{6,7},{7,6},{8,9},{9,8},{10,11... | collective-permute-start | bytes 884744 | tf_op jit(solution)/shard_map/ppermute | solution.py:320
  28.7 6.9 %collective-permute-start.9 = (bf16[144,8,128]{2,1,0:T(8,128)(2,1)S(1)}, bf16[144,8,128]{2,1,0:T(8,128)(2,1)S(1)}, u32[]{:S(2)}, u32[]{:S(2)}) collective-permute-start(bf16[144,8,128]{2,1,0:T(8,128)(2,1)S(1)} %get-tuple-element.40), channel_id=1, source_target_pairs={{0,3},{1,2},{2,1},{3,0},{4,7},{5,6},{6,5},{7,4},{8,11},{9,10},{10,... | collective-permute-start | bytes 884744 | tf_op jit(solution)/shard_map/ppermute | solution.py:320
  35.6 6.8 %collective-permute-start.13 = (bf16[105,8,128]{2,1,0:T(8,128)(2,1)S(1)}, bf16[105,8,128]{2,1,0:T(8,128)(2,1)S(1)}, u32[]{:S(2)}, u32[]{:S(2)}) collective-permute-start(bf16[105,8,128]{2,1,0:T(8,128)(2,1)S(1)} %get-tuple-element.32.rest_0_.refs_0_), channel_id=1, source_target_pairs={{0,4},{1,5},{2,6},{3,7},{4,0},{5,1},{6,2},{7,3},{8,12},{9,13},{10,... | collective-permute-start | bytes 645128 | tf_op jit(solution)/shard_map/ppermute | solution.py:320
  42.4 1.7 %right.3 = (bf16[48,8,128]{2,1,0:T(8,128)(2,1)S(1)}, bf16[48,8,128]{2,1,0:T(8,128)(2,1)S(1)}, bf16[48,8,128]{2,1,0:T(8,128)(2,1)S(1)}, bf16[48,8,128]{2,1,0:T(8,128)(2,1)S(1)}) custom-call(s32[1]{0:T(128)} %bitcast.me_ref, s32[192]{0:T(256)S(1)} %copy-done.10, f32[24,192,128]{2,1,0:T(8,128)S(1)} %copy-done, f32[24,384]{1,0:T(8,128)S(1)} %copy-done.8, ...), custom_call_target="tpu_custom_call" | custom-call | flops 134217728 | bytes 4000000 | tf_op jit(solution)/shard_map/right/pallas_call | solution.py:356
  44.2 9.8 %collective-permute-done.12.refs_3_ = bf16[105,8,128]{2,1,0:T(8,128)(2,1)S(1)} collective-permute-done((bf16[105,8,128]{2,1,0:T(8,128)(2,1)S(1)}, bf16[105,8,128]{2,1,0:T(8,128)(2,1)S(1)}, u32[]{:S(2)}, u32[]{:S(2)}) %collective-permute-start.12) | collective-permute-done | bytes 215072 | tf_op jit(solution)/shard_map/ppermute | solution.py:320
  54.0 1.6 %collective-permute-start.4 = (bf16[48,8,128]{2,1,0:T(8,128)(2,1)S(1)}, bf16[48,8,128]{2,1,0:T(8,128)(2,1)S(1)}, u32[]{:S(2)}, u32[]{:S(2)}) collective-permute-start(bf16[48,8,128]{2,1,0:T(8,128)(2,1)S(1)} %get-tuple-element.35), channel_id=1, source_target_pairs={{0,5},{1,4},{2,7},{3,6},{4,1},{5,0},{6,3},{7,2},{8,13},{9,12},{10,... | collective-permute-start | bytes 294920 | tf_op jit(solution)/shard_map/ppermute | solution.py:320
  55.6 0.5 collective-permute-start
  56.1 1.9 %collective-permute-start.5 = (bf16[48,8,128]{2,1,0:T(8,128)(2,1)S(1)}, bf16[48,8,128]{2,1,0:T(8,128)(2,1)S(1)}, u32[]{:S(2)}, u32[]{:S(2)}) collective-permute-start(bf16[48,8,128]{2,1,0:T(8,128)(2,1)S(1)} %get-tuple-element.36), channel_id=1, source_target_pairs={{0,6},{1,7},{2,4},{3,5},{4,2},{5,3},{6,0},{7,1},{8,14},{9,15},{10,... | collective-permute-start | bytes 294920 | tf_op jit(solution)/shard_map/ppermute | solution.py:320
  58.0 1.6 %collective-permute-start.1 = (bf16[48,8,128]{2,1,0:T(8,128)(2,1)S(1)}, bf16[48,8,128]{2,1,0:T(8,128)(2,1)S(1)}, u32[]{:S(2)}, u32[]{:S(2)}) collective-permute-start(bf16[48,8,128]{2,1,0:T(8,128)(2,1)S(1)} %get-tuple-element.36), channel_id=1, source_target_pairs={{0,2},{1,3},{2,0},{3,1},{4,6},{5,7},{6,4},{7,5},{8,10},{9,11},{10,... | collective-permute-start | bytes 294920 | tf_op jit(solution)/shard_map/ppermute | solution.py:320
  59.6 2.8 %collective-permute-start.6 = (bf16[48,8,128]{2,1,0:T(8,128)(2,1)S(1)}, bf16[48,8,128]{2,1,0:T(8,128)(2,1)S(1)}, u32[]{:S(2)}, u32[]{:S(2)}) collective-permute-start(bf16[48,8,128]{2,1,0:T(8,128)(2,1)S(1)} %get-tuple-element.37), channel_id=1, source_target_pairs={{0,7},{1,6},{2,5},{3,4},{4,3},{5,2},{6,1},{7,0},{8,15},{9,14},{10,... | collective-permute-start | bytes 294920 | tf_op jit(solution)/shard_map/ppermute | solution.py:320
  62.4 0.5 attention_in.1
  62.9 1.3 %shard_map.141 = (bf16[24,32,128]{2,1,0:T(8,128)(2,1)S(1)}, bf16[24,32,128]{2,1,0:T(8,128)(2,1)S(1)}, bf16[24,32,128]{2,1,0:T(8,128)(2,1)S(1)}, bf16[24,32,128]{2,1,0:T(8,128)(2,1)S(1)}) custom-call(s32[1]{0:T(128)} %bitcast.me_ref, bf16[105,8,128]{2,1,0:T(8,128)(2,1)S(1)} %get-tuple-element.32.rest_0_.refs_0_, ...), custom_call_target="tpu_custom_call" | custom-call | flops 201326592 | bytes 4000000 | tf_op jit(solution)/shard_map/pallas_call | solution.py:442
  64.1 1.2 %collective-permute-done.4.refs_5_ = bf16[48,8,128]{2,1,0:T(8,128)(2,1)S(1)} collective-permute-done((bf16[48,8,128]{2,1,0:T(8,128)(2,1)S(1)}, bf16[48,8,128]{2,1,0:T(8,128)(2,1)S(1)}, u32[]{:S(2)}, u32[]{:S(2)}) %collective-permute-start.4) | collective-permute-done | bytes 98336 | tf_op jit(solution)/shard_map/ppermute | solution.py:320
  65.3 0.7 collective-permute-start.20
  66.1 3.0 %collective-permute-start.22 = (bf16[24,32,128]{2,1,0:T(8,128)(2,1)S(1)}, bf16[24,32,128]{2,1,0:T(8,128)(2,1)S(1)}, u32[]{:S(2)}, u32[]{:S(2)}) collective-permute-start(bf16[24,32,128]{2,1,0:T(8,128)(2,1)S(1)} %get-tuple-element.57), channel_id=1, source_target_pairs={{0,3},{1,2},{2,1},{3,0},{4,7},{5,6},{6,5},{7,4},{8,11},{9,10},{10,... | collective-permute-start | bytes 589832 | tf_op jit(solution)/shard_map/ppermute | solution.py:320
  69.1 3.6 %collective-permute-start.3 = (bf16[48,8,128]{2,1,0:T(8,128)(2,1)S(1)}, bf16[48,8,128]{2,1,0:T(8,128)(2,1)S(1)}, u32[]{:S(2)}, u32[]{:S(2)}) collective-permute-start(bf16[48,8,128]{2,1,0:T(8,128)(2,1)S(1)} %get-tuple-element.34.refs_0_._), channel_id=1, source_target_pairs={{0,4},{1,5},{2,6},{3,7},{4,0},{5,1},{6,2},{7,3},{8,12},{9,13},{10,... | collective-permute-start | bytes 294920 | tf_op jit(solution)/shard_map/ppermute | solution.py:320
  72.7 2.1 %gate.1 = f32[24,192,128]{2,1,0:T(8,128)S(1)} custom-call(f32[24,192,128]{2,1,0:T(8,128)S(1)} %copy-done, bf16[128,128]{1,0:T(8,128)(2,1)S(1)} %copy-done.11, bf16[48,8,128]{2,1,0:T(8,128)(2,1)S(1)} %get-tuple-element.34.refs_0_._), custom_call_target="tpu_custom_call" | custom-call | flops 150994944 | bytes 4000000 | tf_op jit(solution)/shard_map/gate/pallas_call | solution.py:408
  74.8 5.1 %collective-permute-done.2.refs_3_ = bf16[48,8,128]{2,1,0:T(8,128)(2,1)S(1)} collective-permute-done((bf16[48,8,128]{2,1,0:T(8,128)(2,1)S(1)}, bf16[48,8,128]{2,1,0:T(8,128)(2,1)S(1)}, u32[]{:S(2)}, u32[]{:S(2)}) %collective-permute-start.2) | collective-permute-done | bytes 98336 | tf_op jit(solution)/shard_map/ppermute | solution.py:320
  80.0 1.2 %shard_map.140 = (bf16[24,16,128]{2,1,0:T(8,128)(2,1)S(1)}, bf16[24,16,128]{2,1,0:T(8,128)(2,1)S(1)}, bf16[24,16,128]{2,1,0:T(8,128)(2,1)S(1)}, bf16[24,16,128]{2,1,0:T(8,128)(2,1)S(1)}) custom-call(s32[1]{0:T(128)} %bitcast.me_ref, bf16[48,8,128]{2,1,0:T(8,128)(2,1)S(1)} %get-tuple-element.34.refs_0_._, ...), custom_call_target="tpu_custom_call" | custom-call | flops 201326592 | bytes 4000000 | tf_op jit(solution)/shard_map/pallas_call | solution.py:442
  81.1 0.7 collective-permute-start.17
  81.8 1.1 %collective-permute-start.18 = (bf16[24,16,128]{2,1,0:T(8,128)(2,1)S(1)}, bf16[24,16,128]{2,1,0:T(8,128)(2,1)S(1)}, u32[]{:S(2)}, u32[]{:S(2)}) collective-permute-start(bf16[24,16,128]{2,1,0:T(8,128)(2,1)S(1)} %get-tuple-element.47), channel_id=1, source_target_pairs={{0,2},{1,3},{2,0},{3,1},{4,6},{5,7},{6,4},{7,5},{8,10},{9,11},{10,... | collective-permute-start | bytes 294920 | tf_op jit(solution)/shard_map/ppermute | solution.py:320
  82.9 1.8 %collective-permute-start.19 = (bf16[24,16,128]{2,1,0:T(8,128)(2,1)S(1)}, bf16[24,16,128]{2,1,0:T(8,128)(2,1)S(1)}, u32[]{:S(2)}, u32[]{:S(2)}) collective-permute-start(bf16[24,16,128]{2,1,0:T(8,128)(2,1)S(1)} %get-tuple-element.48), channel_id=1, source_target_pairs={{0,3},{1,2},{2,1},{3,0},{4,7},{5,6},{6,5},{7,4},{8,11},{9,10},{10,... | collective-permute-start | bytes 294920 | tf_op jit(solution)/shard_map/ppermute | solution.py:320
  84.8 5.6 %shard_map.142 = (f32[24,8,3,8,128]{4,3,2,1,0:T(8,128)}, f32[24,16,128]{2,1,0:T(8,128)S(1)}) custom-call(s32[1]{0:T(128)} %bitcast.me_ref, bf16[24,32,128]{2,1,0:T(8,128)(2,1)S(1)} %get-tuple-element.54.refs_0_, bf16[24,32,128]{2,1,0:T(8,128)(2,1)S(1)} %collective-permute-done.20.refs_1_, bf16[24,32,128]{2,1,0:T(8,128)(2,1)S(1)} %collective-permute-done.21.refs_2_, ...), custom_call_target="tpu_custom_call" | custom-call | flops 1308622848 | bytes 4000000 | tf_op jit(solution)/shard_map/pallas_call | solution.py:484
  90.3 4.2 %shard_map.143 = (f32[24,8,3,8,128]{4,3,2,1,0:T(8,128)}, f32[24,384]{1,0:T(8,128)}) custom-call(s32[1]{0:T(128)} %bitcast.me_ref, bf16[24,16,128]{2,1,0:T(8,128)(2,1)S(1)} %get-tuple-element.45.refs_0_, bf16[24,16,128]{2,1,0:T(8,128)(2,1)S(1)} %collective-permute-done.17.refs_1_, ...), custom_call_target="tpu_custom_call", output_to_operand_aliasing={{0}: (20, {})} | custom-call | flops 654311424 | bytes 4000000 | tf_op jit(solution)/shard_map/pallas_call | solution.py:484
  (49 shorter events, 0.2 us)
Async XLA Ops:
  0.6 15.7 %copy-start = (f32[24,192,128]{2,1,0:T(8,128)S(1)}, f32[24,192,128]{2,1,0:T(8,128)}, u32[]{:S(2)}) copy-start(f32[24,192,128]{2,1,0:T(8,128)} %pair_ref.7) | copy-start | bytes 7077892
  0.6 15.7 %copy-start.10 = (s32[192]{0:T(256)S(1)}, s32[192]{0:T(256)}, u32[]{:S(2)}) copy-start(s32[192]{0:T(256)} %refs_13_.1) | copy-start | bytes 2308
  0.7 15.7 %copy-start.1 = (bf16[128,512]{1,0:T(8,128)(2,1)S(1)}, bf16[128,512]{1,0:T(8,128)(2,1)}, u32[]{:S(2)}) copy-start(bf16[128,512]{1,0:T(8,128)(2,1)} %w_ref.5) | copy-start | bytes 393220
  0.7 41.7 %copy-start.8 = (f32[24,384]{1,0:T(8,128)S(1)}, f32[24,384]{1,0:T(8,128)}, u32[]{:S(2)}) copy-start(f32[24,384]{1,0:T(8,128)} %single_ref.3) | copy-start | bytes 110596
  5.3 21.3 %collective-permute-start.14 = (bf16[105,8,128]{2,1,0:T(8,128)(2,1)S(1)}, bf16[105,8,128]{2,1,0:T(8,128)(2,1)S(1)}, u32[]{:S(2)}, u32[]{:S(2)}) collective-permute-start(bf16[105,8,128]{2,1,0:T(8,128)(2,1)S(1)} %get-tuple-element.41), channel_id=1, source_target_pairs={{0,5},{1,4},{2,7},{3,6},{4,1},{5,0},{6,3},{7,2},{8,13},{9,12},{10,... | collective-permute-start | bytes 645128 | tf_op jit(solution)/shard_map/ppermute | solution.py:320
  10.4 18.3 %collective-permute-start.10 = (bf16[105,8,128]{2,1,0:T(8,128)(2,1)S(1)}, bf16[105,8,128]{2,1,0:T(8,128)(2,1)S(1)}, u32[]{:S(2)}, u32[]{:S(2)}) collective-permute-start(bf16[105,8,128]{2,1,0:T(8,128)(2,1)S(1)} %get-tuple-element.41), channel_id=1, source_target_pairs={{0,1},{1,0},{2,3},{3,2},{4,5},{5,4},{6,7},{7,6},{8,9},{9,8},{10,11... | collective-permute-start | bytes 645128 | tf_op jit(solution)/shard_map/ppermute | solution.py:320
  10.9 17.8 %collective-permute-start.15 = (bf16[105,8,128]{2,1,0:T(8,128)(2,1)S(1)}, bf16[105,8,128]{2,1,0:T(8,128)(2,1)S(1)}, u32[]{:S(2)}, u32[]{:S(2)}) collective-permute-start(bf16[105,8,128]{2,1,0:T(8,128)(2,1)S(1)} %get-tuple-element.42), channel_id=1, source_target_pairs={{0,6},{1,7},{2,4},{3,5},{4,2},{5,3},{6,0},{7,1},{8,14},{9,15},{10,... | collective-permute-start | bytes 645128 | tf_op jit(solution)/shard_map/ppermute | solution.py:320
  12.3 23.3 %collective-permute-start.11 = (bf16[105,8,128]{2,1,0:T(8,128)(2,1)S(1)}, bf16[105,8,128]{2,1,0:T(8,128)(2,1)S(1)}, u32[]{:S(2)}, u32[]{:S(2)}) collective-permute-start(bf16[105,8,128]{2,1,0:T(8,128)(2,1)S(1)} %get-tuple-element.42), channel_id=1, source_target_pairs={{0,2},{1,3},{2,0},{3,1},{4,6},{5,7},{6,4},{7,5},{8,10},{9,11},{10,... | collective-permute-start | bytes 645128 | tf_op jit(solution)/shard_map/ppermute | solution.py:320
  12.5 23.1 %collective-permute-start.16 = (bf16[105,8,128]{2,1,0:T(8,128)(2,1)S(1)}, bf16[105,8,128]{2,1,0:T(8,128)(2,1)S(1)}, u32[]{:S(2)}, u32[]{:S(2)}) collective-permute-start(bf16[105,8,128]{2,1,0:T(8,128)(2,1)S(1)} %get-tuple-element.43), channel_id=1, source_target_pairs={{0,7},{1,6},{2,5},{3,4},{4,3},{5,2},{6,1},{7,0},{8,15},{9,14},{10,... | collective-permute-start | bytes 645128 | tf_op jit(solution)/shard_map/ppermute | solution.py:320
  16.4 46.0 %copy-start.3 = (bf16[384,768]{1,0:T(8,128)(2,1)S(1)}, bf16[384,768]{1,0:T(8,128)(2,1)}, u32[]{:S(2)}) copy-start(bf16[384,768]{1,0:T(8,128)(2,1)} %refs_10_.1) | copy-start | bytes 1769476
  16.4 46.0 %copy-start.5 = (bf16[384,384]{1,0:T(8,128)(2,1)S(1)}, bf16[384,384]{1,0:T(8,128)(2,1)}, u32[]{:S(2)}) copy-start(bf16[384,384]{1,0:T(8,128)(2,1)} %refs_8_.3) | copy-start | bytes 884740
  16.4 46.0 %copy-start.6 = (bf16[384,384]{1,0:T(8,128)(2,1)S(1)}, bf16[384,384]{1,0:T(8,128)(2,1)}, u32[]{:S(2)}) copy-start(bf16[384,384]{1,0:T(8,128)(2,1)} %refs_9_.1) | copy-start | bytes 884740
  26.6 29.4 %collective-permute-start.7 = (bf16[144,8,128]{2,1,0:T(8,128)(2,1)S(1)}, bf16[144,8,128]{2,1,0:T(8,128)(2,1)S(1)}, u32[]{:S(2)}, u32[]{:S(2)}) collective-permute-start(bf16[144,8,128]{2,1,0:T(8,128)(2,1)S(1)} %get-tuple-element.38), channel_id=1, source_target_pairs={{0,1},{1,0},{2,3},{3,2},{4,5},{5,4},{6,7},{7,6},{8,9},{9,8},{10,11... | collective-permute-start | bytes 884744 | tf_op jit(solution)/shard_map/ppermute | solution.py:320
  28.7 29.3 %collective-permute-start.8 = (bf16[144,8,128]{2,1,0:T(8,128)(2,1)S(1)}, bf16[144,8,128]{2,1,0:T(8,128)(2,1)S(1)}, u32[]{:S(2)}, u32[]{:S(2)}) collective-permute-start(bf16[144,8,128]{2,1,0:T(8,128)(2,1)S(1)} %get-tuple-element.39), channel_id=1, source_target_pairs={{0,2},{1,3},{2,0},{3,1},{4,6},{5,7},{6,4},{7,5},{8,10},{9,11},{10,... | collective-permute-start | bytes 884744 | tf_op jit(solution)/shard_map/ppermute | solution.py:320
  28.7 30.9 %collective-permute-start.9 = (bf16[144,8,128]{2,1,0:T(8,128)(2,1)S(1)}, bf16[144,8,128]{2,1,0:T(8,128)(2,1)S(1)}, u32[]{:S(2)}, u32[]{:S(2)}) collective-permute-start(bf16[144,8,128]{2,1,0:T(8,128)(2,1)S(1)} %get-tuple-element.40), channel_id=1, source_target_pairs={{0,3},{1,2},{2,1},{3,0},{4,7},{5,6},{6,5},{7,4},{8,11},{9,10},{10,... | collective-permute-start | bytes 884744 | tf_op jit(solution)/shard_map/ppermute | solution.py:320
  35.6 18.4 %collective-permute-start.12 = (bf16[105,8,128]{2,1,0:T(8,128)(2,1)S(1)}, bf16[105,8,128]{2,1,0:T(8,128)(2,1)S(1)}, u32[]{:S(2)}, u32[]{:S(2)}) collective-permute-start(bf16[105,8,128]{2,1,0:T(8,128)(2,1)S(1)} %get-tuple-element.43), channel_id=1, source_target_pairs={{0,3},{1,2},{2,1},{3,0},{4,7},{5,6},{6,5},{7,4},{8,11},{9,10},{10,... | collective-permute-start | bytes 645128 | tf_op jit(solution)/shard_map/ppermute | solution.py:320
  35.6 19.9 %collective-permute-start.13 = (bf16[105,8,128]{2,1,0:T(8,128)(2,1)S(1)}, bf16[105,8,128]{2,1,0:T(8,128)(2,1)S(1)}, u32[]{:S(2)}, u32[]{:S(2)}) collective-permute-start(bf16[105,8,128]{2,1,0:T(8,128)(2,1)S(1)} %get-tuple-element.32.rest_0_.refs_0_), channel_id=1, source_target_pairs={{0,4},{1,5},{2,6},{3,7},{4,0},{5,1},{6,2},{7,3},{8,12},{9,13},{10,... | collective-permute-start | bytes 645128 | tf_op jit(solution)/shard_map/ppermute | solution.py:320
  54.0 11.3 %collective-permute-start.4 = (bf16[48,8,128]{2,1,0:T(8,128)(2,1)S(1)}, bf16[48,8,128]{2,1,0:T(8,128)(2,1)S(1)}, u32[]{:S(2)}, u32[]{:S(2)}) collective-permute-start(bf16[48,8,128]{2,1,0:T(8,128)(2,1)S(1)} %get-tuple-element.35), channel_id=1, source_target_pairs={{0,5},{1,4},{2,7},{3,6},{4,1},{5,0},{6,3},{7,2},{8,13},{9,12},{10,... | collective-permute-start | bytes 294920 | tf_op jit(solution)/shard_map/ppermute | solution.py:320
  55.6 10.5 %collective-permute-start = (bf16[48,8,128]{2,1,0:T(8,128)(2,1)S(1)}, bf16[48,8,128]{2,1,0:T(8,128)(2,1)S(1)}, u32[]{:S(2)}, u32[]{:S(2)}) collective-permute-start(bf16[48,8,128]{2,1,0:T(8,128)(2,1)S(1)} %get-tuple-element.35), channel_id=1, source_target_pairs={{0,1},{1,0},{2,3},{3,2},{4,5},{5,4},{6,7},{7,6},{8,9},{9,8},{10,11... | collective-permute-start | bytes 294920 | tf_op jit(solution)/shard_map/ppermute | solution.py:320
  56.1 10.0 %collective-permute-start.5 = (bf16[48,8,128]{2,1,0:T(8,128)(2,1)S(1)}, bf16[48,8,128]{2,1,0:T(8,128)(2,1)S(1)}, u32[]{:S(2)}, u32[]{:S(2)}) collective-permute-start(bf16[48,8,128]{2,1,0:T(8,128)(2,1)S(1)} %get-tuple-element.36), channel_id=1, source_target_pairs={{0,6},{1,7},{2,4},{3,5},{4,2},{5,3},{6,0},{7,1},{8,14},{9,15},{10,... | collective-permute-start | bytes 294920 | tf_op jit(solution)/shard_map/ppermute | solution.py:320
  58.0 11.1 %collective-permute-start.1 = (bf16[48,8,128]{2,1,0:T(8,128)(2,1)S(1)}, bf16[48,8,128]{2,1,0:T(8,128)(2,1)S(1)}, u32[]{:S(2)}, u32[]{:S(2)}) collective-permute-start(bf16[48,8,128]{2,1,0:T(8,128)(2,1)S(1)} %get-tuple-element.36), channel_id=1, source_target_pairs={{0,2},{1,3},{2,0},{3,1},{4,6},{5,7},{6,4},{7,5},{8,10},{9,11},{10,... | collective-permute-start | bytes 294920 | tf_op jit(solution)/shard_map/ppermute | solution.py:320
  59.6 9.5 %collective-permute-start.6 = (bf16[48,8,128]{2,1,0:T(8,128)(2,1)S(1)}, bf16[48,8,128]{2,1,0:T(8,128)(2,1)S(1)}, u32[]{:S(2)}, u32[]{:S(2)}) collective-permute-start(bf16[48,8,128]{2,1,0:T(8,128)(2,1)S(1)} %get-tuple-element.37), channel_id=1, source_target_pairs={{0,7},{1,6},{2,5},{3,4},{4,3},{5,2},{6,1},{7,0},{8,15},{9,14},{10,... | collective-permute-start | bytes 294920 | tf_op jit(solution)/shard_map/ppermute | solution.py:320
  65.3 17.6 %collective-permute-start.20 = (bf16[24,32,128]{2,1,0:T(8,128)(2,1)S(1)}, bf16[24,32,128]{2,1,0:T(8,128)(2,1)S(1)}, u32[]{:S(2)}, u32[]{:S(2)}) collective-permute-start(bf16[24,32,128]{2,1,0:T(8,128)(2,1)S(1)} %get-tuple-element.55), channel_id=1, source_target_pairs={{0,1},{1,0},{2,3},{3,2},{4,5},{5,4},{6,7},{7,6},{8,9},{9,8},{10,11... | collective-permute-start | bytes 589832 | tf_op jit(solution)/shard_map/ppermute | solution.py:320
  66.0 18.7 %collective-permute-start.21 = (bf16[24,32,128]{2,1,0:T(8,128)(2,1)S(1)}, bf16[24,32,128]{2,1,0:T(8,128)(2,1)S(1)}, u32[]{:S(2)}, u32[]{:S(2)}) collective-permute-start(bf16[24,32,128]{2,1,0:T(8,128)(2,1)S(1)} %get-tuple-element.56), channel_id=1, source_target_pairs={{0,2},{1,3},{2,0},{3,1},{4,6},{5,7},{6,4},{7,5},{8,10},{9,11},{10,... | collective-permute-start | bytes 589832 | tf_op jit(solution)/shard_map/ppermute | solution.py:320
  66.1 18.7 %collective-permute-start.22 = (bf16[24,32,128]{2,1,0:T(8,128)(2,1)S(1)}, bf16[24,32,128]{2,1,0:T(8,128)(2,1)S(1)}, u32[]{:S(2)}, u32[]{:S(2)}) collective-permute-start(bf16[24,32,128]{2,1,0:T(8,128)(2,1)S(1)} %get-tuple-element.57), channel_id=1, source_target_pairs={{0,3},{1,2},{2,1},{3,0},{4,7},{5,6},{6,5},{7,4},{8,11},{9,10},{10,... | collective-permute-start | bytes 589832 | tf_op jit(solution)/shard_map/ppermute | solution.py:320
  69.0 10.9 %collective-permute-start.2 = (bf16[48,8,128]{2,1,0:T(8,128)(2,1)S(1)}, bf16[48,8,128]{2,1,0:T(8,128)(2,1)S(1)}, u32[]{:S(2)}, u32[]{:S(2)}) collective-permute-start(bf16[48,8,128]{2,1,0:T(8,128)(2,1)S(1)} %get-tuple-element.37), channel_id=1, source_target_pairs={{0,3},{1,2},{2,1},{3,0},{4,7},{5,6},{6,5},{7,4},{8,11},{9,10},{10,... | collective-permute-start | bytes 294920 | tf_op jit(solution)/shard_map/ppermute | solution.py:320
  69.1 15.6 %copy-start.9 = (bf16[128,128]{1,0:T(8,128)(2,1)S(1)}, bf16[128,128]{1,0:T(8,128)(2,1)}, u32[]{:S(2)}) copy-start(bf16[128,128]{1,0:T(8,128)(2,1)} %param.18) | copy-start | bytes 98308
  69.1 15.6 %copy-start.12 = (bf16[128,16]{0,1:T(8,128)(2,1)S(1)}, bf16[128,16]{0,1:T(8,128)(2,1)}, u32[]{:S(2)}) copy-start(bf16[128,16]{0,1:T(8,128)(2,1)} %param.21) | copy-start | bytes 12292
  69.1 10.8 %collective-permute-start.3 = (bf16[48,8,128]{2,1,0:T(8,128)(2,1)S(1)}, bf16[48,8,128]{2,1,0:T(8,128)(2,1)S(1)}, u32[]{:S(2)}, u32[]{:S(2)}) collective-permute-start(bf16[48,8,128]{2,1,0:T(8,128)(2,1)S(1)} %get-tuple-element.34.refs_0_._), channel_id=1, source_target_pairs={{0,4},{1,5},{2,6},{3,7},{4,0},{5,1},{6,2},{7,3},{8,12},{9,13},{10,... | collective-permute-start | bytes 294920 | tf_op jit(solution)/shard_map/ppermute | solution.py:320
  81.1 9.2 %collective-permute-start.17 = (bf16[24,16,128]{2,1,0:T(8,128)(2,1)S(1)}, bf16[24,16,128]{2,1,0:T(8,128)(2,1)S(1)}, u32[]{:S(2)}, u32[]{:S(2)}) collective-permute-start(bf16[24,16,128]{2,1,0:T(8,128)(2,1)S(1)} %get-tuple-element.46), channel_id=1, source_target_pairs={{0,1},{1,0},{2,3},{3,2},{4,5},{5,4},{6,7},{7,6},{8,9},{9,8},{10,11... | collective-permute-start | bytes 294920 | tf_op jit(solution)/shard_map/ppermute | solution.py:320
  81.8 8.5 %collective-permute-start.18 = (bf16[24,16,128]{2,1,0:T(8,128)(2,1)S(1)}, bf16[24,16,128]{2,1,0:T(8,128)(2,1)S(1)}, u32[]{:S(2)}, u32[]{:S(2)}) collective-permute-start(bf16[24,16,128]{2,1,0:T(8,128)(2,1)S(1)} %get-tuple-element.47), channel_id=1, source_target_pairs={{0,2},{1,3},{2,0},{3,1},{4,6},{5,7},{6,4},{7,5},{8,10},{9,11},{10,... | collective-permute-start | bytes 294920 | tf_op jit(solution)/shard_map/ppermute | solution.py:320
  82.9 7.4 %collective-permute-start.19 = (bf16[24,16,128]{2,1,0:T(8,128)(2,1)S(1)}, bf16[24,16,128]{2,1,0:T(8,128)(2,1)S(1)}, u32[]{:S(2)}, u32[]{:S(2)}) collective-permute-start(bf16[24,16,128]{2,1,0:T(8,128)(2,1)S(1)} %get-tuple-element.48), channel_id=1, source_target_pairs={{0,3},{1,2},{2,1},{3,0},{4,7},{5,6},{6,5},{7,4},{8,11},{9,10},{10,... | collective-permute-start | bytes 294920 | tf_op jit(solution)/shard_map/ppermute | solution.py:320
  (4 other events, 50.0 us)

commit v5 on v4

--- a/solution.py
+++ b/solution.py
@@ -163,10 +163,17 @@
             out_refs[a][i] = x.astype(bf16)
 
 
-def attention_in_kernel(groups, chunks, message, me_ref, *refs):
+def own_lanes(row_count, heads, channels):
+    head_size = channels // heads
+    of_head = lax.broadcasted_iota(jnp.int32, (row_count, heads, channels), 1)
+    lane = lax.broadcasted_iota(jnp.int32, (row_count, heads, channels), 2)
+    return jnp.logical_and(lane >= of_head * head_size, lane < (of_head + 1) * head_size)
+
+
+def attention_in_kernel(groups, chunks, message, heads, me_ref, *refs):
     count = len(chunks)
     right_refs = refs[:groups]
-    w_query_ref, w_key_ref, w_value_gate_ref, q_ref, g_ref = refs[groups : groups + 5]
+    w_query_ref, w_key_ref, w_value_gate_ref, g_ref, late_ref = refs[groups : groups + 5]
     k_refs, v_refs = refs[groups + 5 : groups + 5 + count], refs[groups + 5 + count : groups + 5 + 2 * count]
     all_ref = refs[-1]
     channels = w_query_ref.shape[0]
@@ -178,12 +185,18 @@
             t, at = divmod(n, tiles)
             all_ref[d, at * SUB : (at + 1) * SUB, t * LANES : (t + 1) * LANES] = right_refs[s][message + n].astype(f32)
     own = all_ref[me].astype(bf16)
-    q_ref[...] = jnp.dot(own, w_query_ref[...], preferred_element_type=f32).astype(bf16)
+    queries = jnp.dot(own, w_query_ref[...], preferred_element_type=f32).astype(bf16)
+    late_ref[...] = queries
+    mine = own_lanes(own.shape[0], heads, channels)
+    spread = jnp.where(mine, jnp.broadcast_to(queries.astype(f32)[:, None, :], mine.shape), 0.0)
+    spread = spread.reshape(own.shape[0] * heads, channels).astype(bf16)
     g_ref[...] = sigmoid(jnp.dot(own, w_value_gate_ref[:, channels:], preferred_element_type=f32))
     first = 0
     for k in range(count):
-        every = all_ref[:, first * SUB : (first + chunks[k]) * SUB].reshape(k_refs[k].shape).astype(bf16)
-        k_refs[k][...] = jnp.dot(every, w_key_ref[...], preferred_element_type=f32).astype(bf16)
+        every = all_ref[:, first * SUB : (first + chunks[k]) * SUB].reshape(v_refs[k].shape).astype(bf16)
+        keys = jnp.dot(every, w_key_ref[...], preferred_element_type=f32).astype(bf16)
+        scores = lax.dot_general(spread, keys, NT, preferred_element_type=f32)
+        k_refs[k][...] = scores / jnp.sqrt(f32(channels // heads))
         v_refs[k][...] = jnp.dot(every, w_value_gate_ref[:, :channels], preferred_element_type=f32).astype(bf16)
         first += chunks[k]
 
@@ -256,22 +269,17 @@
 
 
 def attention(heads, n, groups, refs, last_bias_ref, single_ref):
-    q_ref, g_ref, w_out_ref, mask_ref = refs[:4]
-    k_refs, v_refs = refs[4 : 4 + n], refs[4 + n : 4 + 2 * n]
-    bias_refs = [*refs[4 + 2 * n : 3 + 3 * n], last_bias_ref]
+    g_ref, w_out_ref, mask_ref = refs[:3]
+    score_refs, v_refs = refs[3 : 3 + n], refs[3 + n : 3 + 2 * n]
+    bias_refs = [*refs[3 + 2 * n : 2 + 3 * n], last_bias_ref]
     count = jnp.sum(mask_ref[...].astype(f32).reshape(1, mask_ref.shape[0]), axis=1, keepdims=True)
-    row_count, channels = q_ref.shape
-    head_size = channels // heads
-    of_head = lax.broadcasted_iota(jnp.int32, (row_count, heads, channels), 1)
-    lane = lax.broadcasted_iota(jnp.int32, (row_count, heads, channels), 2)
-    mine = jnp.logical_and(lane >= of_head * head_size, lane < (of_head + 1) * head_size)
-    spread = jnp.where(mine, jnp.broadcast_to(q_ref[...].astype(f32)[:, None, :], mine.shape), 0.0)
-    spread = spread.reshape(row_count * heads, channels).astype(bf16)
+    row_count, channels = g_ref.shape
+    mine = own_lanes(row_count, heads, channels)
     scores, first = [], 0
     for k in range(n):
-        part = lax.dot_general(spread, k_refs[k][...], NT, preferred_element_type=f32)
+        part = score_refs[k][...]
         bias = bias_refs[k][...].reshape(row_count * heads, LANES)[:, : part.shape[1]]
-        part = part / jnp.sqrt(f32(head_size)) + bias
+        part = part + bias
         column = lax.broadcasted_iota(jnp.int32, (1, part.shape[1]), 1)
         size = part.shape[1] // groups
         token = column // size * row_count + first + column % size
@@ -416,19 +424,22 @@
     )(near, w_tri_gate, *after)
 
     tokens = [groups * n * SUB for n in chunks]
-    queries, att_gate, *keys_values = pl.pallas_call(
-        functools.partial(attention_in_kernel, groups, chunks, message * chunks[0]),
+    att_gate, queries, *keys_values = pl.pallas_call(
+        functools.partial(attention_in_kernel, groups, chunks, message * chunks[0], heads),
         name="attention_in",
         grid_spec=pltpu.PrefetchScalarGridSpec(
             num_scalar_prefetch=1,
             grid=(1,),
             in_specs=in_vmem(right_in[0])
             + [whole_block(w_query.shape), whole_block(w_key.shape), whole_block(w_value_gate.shape)],
-            out_specs=[whole_block((row_count, channels))] * 2 + [whole_block((n, channels)) for n in tokens + tokens],
+            out_specs=[whole_block((row_count, channels))] * 2
+            + [whole_block((row_count * heads, n)) for n in tokens]
+            + [whole_block((n, channels)) for n in tokens],
             scratch_shapes=[pltpu.VMEM((groups, row_count, channels), f32)],
         ),
-        out_shape=[sds((row_count, channels), bf16), sds((row_count, channels), f32)]
-        + [sds((n, channels), bf16) for n in tokens + tokens],
+        out_shape=[sds((row_count, channels), f32), sds((row_count, channels), bf16)]
+        + [sds((row_count * heads, n), f32) for n in tokens]
+        + [sds((n, channels), bf16) for n in tokens],
         compiler_params=params(vmem_limit_bytes=16 * 2**20),
         cost_estimate=cost(2 * length * channels * channels * 3),
     )(me, *arrived(right_in[0]), w_query, w_key, w_value_gate)
@@ -472,7 +483,7 @@
         operands = [*arrived(tri_in[k]), pair_tiled, gate_tiled, w_tri_out.reshape(sets, per_set, width), w_trans_in, w_trans_out, w_bias.T]
         in_specs = in_vmem(operands[: sets + 2])
         if attends:
-            operands += [queries, att_gate, w_out, token_mask, *keys_values, *biases]
+            operands += [att_gate, w_out, token_mask, *keys_values, *biases]
         in_specs += [whole_block(x.shape) for x in operands[sets + 2 :]]
         aliases = {}
         if new is not None:

time: 94.7 us -> 94.8 us (level)
  transfers between devices with their start and end apart: 23 -> 23, of which waited for: 4 -> 4; matrix products, arithmetic and copies ran while one was open for 0% -> 0% of each run, Pallas kernels for 17% -> 18%
where the time goes in v5:
time: 94.8 us; the launch traced here: 94.6 us
  starting transfers between devices  46 us (49%)
  Pallas kernels  25.8 us (27%)
  waiting for transfers between devices  21.9 us (23%)
    ppermute x23, starting transfers between devices, exchange(): lax.ppermute(x, 'row', [(r, r ^ s) for r in range(groups)])  46 us
    ppermute x23, waiting for transfers between devices, exchange(): lax.ppermute(x, 'row', [(r, r ^ s) for r in range(groups)])  21.9 us
    pallas_call x2, Pallas kernels, fast_body(): pl.pallas_call(functools.partial(tail_kernel, sets, per_set, heads, slab,...  9.85 us
    pallas_call x2, Pallas kernels, right_edges(): pl.pallas_call(functools.partial(right_kernel, hidden, full, sets, row_co...  6.38 us
    pallas_call x1, Pallas kernels, left_edges(): pl.pallas_call(functools.partial(left_kernel, hidden, full, sets, row_cou...  4.08 us
    pallas_call x2, Pallas kernels, fast_body(): pl.pallas_call(functools.partial(triangle_kernel, groups, sets, per_set,...  2.44 us
    pallas_call x1, Pallas kernels, fast_body(): pl.pallas_call(gate_kernel, name='gate', in_specs=in_vmem([near, w_tri_ga...  2.13 us
  transfers between devices with their start and end apart: 23, of which 4 were waited for; matrix products, arithmetic and copies ran while one was open for 0% of the time, Pallas kernels for 18%

profile of v5, /device:TPU:0, one launch (start us, length us, event | category | flops | bytes accessed | tf_op | source)
XLA Modules:
  0.0 94.6 jit_solution(2724515665154785484)
XLA Ops:
  0.7 4.6 %right.2 = (bf16[105,8,128]{2,1,0:T(8,128)(2,1)S(1)}, bf16[105,8,128]{2,1,0:T(8,128)(2,1)S(1)}, bf16[105,8,128]{2,1,0:T(8,128)(2,1)S(1)}, bf16[105,8,128]{2,1,0:T(8,128)(2,1)S(1)}) custom-call(s32[1]{0:T(128)} %bitcast.me_ref, s32[192]{0:T(256)} %refs_12_.1, f32[24,192,128]{2,1,0:T(8,128)} %pair_ref.7, f32[24,384]{1,0:T(8,128)} %single_ref.3, s32[192]{0:T(256)} %refs_12_.1, ...), custom_call_target="tpu_custom_call" | custom-call | flops 268435456 | bytes 4000000 | tf_op jit(solution)/shard_map/right/pallas_call | solution.py:364
  5.3 5.1 %collective-permute-start.14 = (bf16[105,8,128]{2,1,0:T(8,128)(2,1)S(1)}, bf16[105,8,128]{2,1,0:T(8,128)(2,1)S(1)}, u32[]{:S(2)}, u32[]{:S(2)}) collective-permute-start(bf16[105,8,128]{2,1,0:T(8,128)(2,1)S(1)} %get-tuple-element.41), channel_id=1, source_target_pairs={{0,5},{1,4},{2,7},{3,6},{4,1},{5,0},{6,3},{7,2},{8,13},{9,12},{10,... | collective-permute-start | bytes 645128 | tf_op jit(solution)/shard_map/ppermute | solution.py:328
  10.4 0.5 collective-permute-start.10
  10.9 1.4 %collective-permute-start.15 = (bf16[105,8,128]{2,1,0:T(8,128)(2,1)S(1)}, bf16[105,8,128]{2,1,0:T(8,128)(2,1)S(1)}, u32[]{:S(2)}, u32[]{:S(2)}) collective-permute-start(bf16[105,8,128]{2,1,0:T(8,128)(2,1)S(1)} %get-tuple-element.42), channel_id=1, source_target_pairs={{0,6},{1,7},{2,4},{3,5},{4,2},{5,3},{6,0},{7,1},{8,14},{9,15},{10,... | collective-permute-start | bytes 645128 | tf_op jit(solution)/shard_map/ppermute | solution.py:328
  12.3 0.2 collective-permute-start.11
  12.5 3.9 %collective-permute-start.16 = (bf16[105,8,128]{2,1,0:T(8,128)(2,1)S(1)}, bf16[105,8,128]{2,1,0:T(8,128)(2,1)S(1)}, u32[]{:S(2)}, u32[]{:S(2)}) collective-permute-start(bf16[105,8,128]{2,1,0:T(8,128)(2,1)S(1)} %get-tuple-element.43), channel_id=1, source_target_pairs={{0,7},{1,6},{2,5},{3,4},{4,3},{5,2},{6,1},{7,0},{8,15},{9,14},{10,... | collective-permute-start | bytes 645128 | tf_op jit(solution)/shard_map/ppermute | solution.py:328
  16.4 4.1 %left.1 = (bf16[144,8,128]{2,1,0:T(8,128)(2,1)S(1)}, bf16[144,8,128]{2,1,0:T(8,128)(2,1)S(1)}, bf16[144,8,128]{2,1,0:T(8,128)(2,1)S(1)}, bf16[144,8,128]{2,1,0:T(8,128)(2,1)S(1)}) custom-call(s32[1]{0:T(128)} %bitcast.me_ref, s32[192]{0:T(256)S(1)} %copy-done.10, f32[24,192,128]{2,1,0:T(8,128)S(1)} %copy-done, s32[192]{0:T(256)S(1)} %copy-done.10, ...), custom_call_target="tpu_custom_call" | custom-call | flops 402653184 | bytes 4000000 | tf_op jit(solution)/shard_map/left/pallas_call | solution.py:386
  20.5 6.1 %collective-permute-done.14.refs_5_ = bf16[105,8,128]{2,1,0:T(8,128)(2,1)S(1)} collective-permute-done((bf16[105,8,128]{2,1,0:T(8,128)(2,1)S(1)}, bf16[105,8,128]{2,1,0:T(8,128)(2,1)S(1)}, u32[]{:S(2)}, u32[]{:S(2)}) %collective-permute-start.14) | collective-permute-done | bytes 215072 | tf_op jit(solution)/shard_map/ppermute | solution.py:328
  26.6 2.0 %collective-permute-start.7 = (bf16[144,8,128]{2,1,0:T(8,128)(2,1)S(1)}, bf16[144,8,128]{2,1,0:T(8,128)(2,1)S(1)}, u32[]{:S(2)}, u32[]{:S(2)}) collective-permute-start(bf16[144,8,128]{2,1,0:T(8,128)(2,1)S(1)} %get-tuple-element.38), channel_id=1, source_target_pairs={{0,1},{1,0},{2,3},{3,2},{4,5},{5,4},{6,7},{7,6},{8,9},{9,8},{10,11... | collective-permute-start | bytes 884744 | tf_op jit(solution)/shard_map/ppermute | solution.py:328
  28.7 6.9 %collective-permute-start.9 = (bf16[144,8,128]{2,1,0:T(8,128)(2,1)S(1)}, bf16[144,8,128]{2,1,0:T(8,128)(2,1)S(1)}, u32[]{:S(2)}, u32[]{:S(2)}) collective-permute-start(bf16[144,8,128]{2,1,0:T(8,128)(2,1)S(1)} %get-tuple-element.40), channel_id=1, source_target_pairs={{0,3},{1,2},{2,1},{3,0},{4,7},{5,6},{6,5},{7,4},{8,11},{9,10},{10,... | collective-permute-start | bytes 884744 | tf_op jit(solution)/shard_map/ppermute | solution.py:328
  35.6 6.8 %collective-permute-start.13 = (bf16[105,8,128]{2,1,0:T(8,128)(2,1)S(1)}, bf16[105,8,128]{2,1,0:T(8,128)(2,1)S(1)}, u32[]{:S(2)}, u32[]{:S(2)}) collective-permute-start(bf16[105,8,128]{2,1,0:T(8,128)(2,1)S(1)} %get-tuple-element.32.rest_0_.refs_0_), channel_id=1, source_target_pairs={{0,4},{1,5},{2,6},{3,7},{4,0},{5,1},{6,2},{7,3},{8,12},{9,13},{10,... | collective-permute-start | bytes 645128 | tf_op jit(solution)/shard_map/ppermute | solution.py:328
  42.4 1.7 %right.3 = (bf16[48,8,128]{2,1,0:T(8,128)(2,1)S(1)}, bf16[48,8,128]{2,1,0:T(8,128)(2,1)S(1)}, bf16[48,8,128]{2,1,0:T(8,128)(2,1)S(1)}, bf16[48,8,128]{2,1,0:T(8,128)(2,1)S(1)}) custom-call(s32[1]{0:T(128)} %bitcast.me_ref, s32[192]{0:T(256)S(1)} %copy-done.10, f32[24,192,128]{2,1,0:T(8,128)S(1)} %copy-done, f32[24,384]{1,0:T(8,128)S(1)} %copy-done.8, ...), custom_call_target="tpu_custom_call" | custom-call | flops 134217728 | bytes 4000000 | tf_op jit(solution)/shard_map/right/pallas_call | solution.py:364
  44.2 9.8 %collective-permute-done.12.refs_3_ = bf16[105,8,128]{2,1,0:T(8,128)(2,1)S(1)} collective-permute-done((bf16[105,8,128]{2,1,0:T(8,128)(2,1)S(1)}, bf16[105,8,128]{2,1,0:T(8,128)(2,1)S(1)}, u32[]{:S(2)}, u32[]{:S(2)}) %collective-permute-start.12) | collective-permute-done | bytes 215072 | tf_op jit(solution)/shard_map/ppermute | solution.py:328
  54.0 1.6 %collective-permute-start.4 = (bf16[48,8,128]{2,1,0:T(8,128)(2,1)S(1)}, bf16[48,8,128]{2,1,0:T(8,128)(2,1)S(1)}, u32[]{:S(2)}, u32[]{:S(2)}) collective-permute-start(bf16[48,8,128]{2,1,0:T(8,128)(2,1)S(1)} %get-tuple-element.35), channel_id=1, source_target_pairs={{0,5},{1,4},{2,7},{3,6},{4,1},{5,0},{6,3},{7,2},{8,13},{9,12},{10,... | collective-permute-start | bytes 294920 | tf_op jit(solution)/shard_map/ppermute | solution.py:328
  55.6 0.5 collective-permute-start
  56.1 1.9 %collective-permute-start.5 = (bf16[48,8,128]{2,1,0:T(8,128)(2,1)S(1)}, bf16[48,8,128]{2,1,0:T(8,128)(2,1)S(1)}, u32[]{:S(2)}, u32[]{:S(2)}) collective-permute-start(bf16[48,8,128]{2,1,0:T(8,128)(2,1)S(1)} %get-tuple-element.36), channel_id=1, source_target_pairs={{0,6},{1,7},{2,4},{3,5},{4,2},{5,3},{6,0},{7,1},{8,14},{9,15},{10,... | collective-permute-start | bytes 294920 | tf_op jit(solution)/shard_map/ppermute | solution.py:328
  58.0 1.6 %collective-permute-start.1 = (bf16[48,8,128]{2,1,0:T(8,128)(2,1)S(1)}, bf16[48,8,128]{2,1,0:T(8,128)(2,1)S(1)}, u32[]{:S(2)}, u32[]{:S(2)}) collective-permute-start(bf16[48,8,128]{2,1,0:T(8,128)(2,1)S(1)} %get-tuple-element.36), channel_id=1, source_target_pairs={{0,2},{1,3},{2,0},{3,1},{4,6},{5,7},{6,4},{7,5},{8,10},{9,11},{10,... | collective-permute-start | bytes 294920 | tf_op jit(solution)/shard_map/ppermute | solution.py:328
  59.6 2.8 %collective-permute-start.6 = (bf16[48,8,128]{2,1,0:T(8,128)(2,1)S(1)}, bf16[48,8,128]{2,1,0:T(8,128)(2,1)S(1)}, u32[]{:S(2)}, u32[]{:S(2)}) collective-permute-start(bf16[48,8,128]{2,1,0:T(8,128)(2,1)S(1)} %get-tuple-element.37), channel_id=1, source_target_pairs={{0,7},{1,6},{2,5},{3,4},{4,3},{5,2},{6,1},{7,0},{8,15},{9,14},{10,... | collective-permute-start | bytes 294920 | tf_op jit(solution)/shard_map/ppermute | solution.py:328
  62.4 0.9 attention_in.1
  63.3 1.3 %shard_map.141 = (bf16[24,32,128]{2,1,0:T(8,128)(2,1)S(1)}, bf16[24,32,128]{2,1,0:T(8,128)(2,1)S(1)}, bf16[24,32,128]{2,1,0:T(8,128)(2,1)S(1)}, bf16[24,32,128]{2,1,0:T(8,128)(2,1)S(1)}) custom-call(s32[1]{0:T(128)} %bitcast.me_ref, bf16[105,8,128]{2,1,0:T(8,128)(2,1)S(1)} %get-tuple-element.32.rest_0_.refs_0_, ...), custom_call_target="tpu_custom_call" | custom-call | flops 201326592 | bytes 4000000 | tf_op jit(solution)/shard_map/pallas_call | solution.py:453
  64.6 0.8 collective-permute-done.4.refs_5_
  65.3 0.8 collective-permute-start.20
  66.2 2.9 %collective-permute-start.22 = (bf16[24,32,128]{2,1,0:T(8,128)(2,1)S(1)}, bf16[24,32,128]{2,1,0:T(8,128)(2,1)S(1)}, u32[]{:S(2)}, u32[]{:S(2)}) collective-permute-start(bf16[24,32,128]{2,1,0:T(8,128)(2,1)S(1)} %get-tuple-element.57), channel_id=1, source_target_pairs={{0,3},{1,2},{2,1},{3,0},{4,7},{5,6},{6,5},{7,4},{8,11},{9,10},{10,... | collective-permute-start | bytes 589832 | tf_op jit(solution)/shard_map/ppermute | solution.py:328
  69.2 3.5 %collective-permute-start.3 = (bf16[48,8,128]{2,1,0:T(8,128)(2,1)S(1)}, bf16[48,8,128]{2,1,0:T(8,128)(2,1)S(1)}, u32[]{:S(2)}, u32[]{:S(2)}) collective-permute-start(bf16[48,8,128]{2,1,0:T(8,128)(2,1)S(1)} %get-tuple-element.34.refs_0_._), channel_id=1, source_target_pairs={{0,4},{1,5},{2,6},{3,7},{4,0},{5,1},{6,2},{7,3},{8,12},{9,13},{10,... | collective-permute-start | bytes 294920 | tf_op jit(solution)/shard_map/ppermute | solution.py:328
  72.7 2.1 %gate.1 = f32[24,192,128]{2,1,0:T(8,128)S(1)} custom-call(f32[24,192,128]{2,1,0:T(8,128)S(1)} %copy-done, bf16[128,128]{1,0:T(8,128)(2,1)S(1)} %copy-done.11, bf16[48,8,128]{2,1,0:T(8,128)(2,1)S(1)} %get-tuple-element.34.refs_0_._), custom_call_target="tpu_custom_call" | custom-call | flops 150994944 | bytes 4000000 | tf_op jit(solution)/shard_map/gate/pallas_call | solution.py:416
  74.8 5.1 %collective-permute-done.2.refs_3_ = bf16[48,8,128]{2,1,0:T(8,128)(2,1)S(1)} collective-permute-done((bf16[48,8,128]{2,1,0:T(8,128)(2,1)S(1)}, bf16[48,8,128]{2,1,0:T(8,128)(2,1)S(1)}, u32[]{:S(2)}, u32[]{:S(2)}) %collective-permute-start.2) | collective-permute-done | bytes 98336 | tf_op jit(solution)/shard_map/ppermute | solution.py:328
  80.0 1.2 %shard_map.140 = (bf16[24,16,128]{2,1,0:T(8,128)(2,1)S(1)}, bf16[24,16,128]{2,1,0:T(8,128)(2,1)S(1)}, bf16[24,16,128]{2,1,0:T(8,128)(2,1)S(1)}, bf16[24,16,128]{2,1,0:T(8,128)(2,1)S(1)}) custom-call(s32[1]{0:T(128)} %bitcast.me_ref, bf16[48,8,128]{2,1,0:T(8,128)(2,1)S(1)} %get-tuple-element.34.refs_0_._, ...), custom_call_target="tpu_custom_call" | custom-call | flops 201326592 | bytes 4000000 | tf_op jit(solution)/shard_map/pallas_call | solution.py:453
  81.1 0.8 collective-permute-start.17
  81.9 0.9 collective-permute-start.18
  82.9 1.8 %collective-permute-start.19 = (bf16[24,16,128]{2,1,0:T(8,128)(2,1)S(1)}, bf16[24,16,128]{2,1,0:T(8,128)(2,1)S(1)}, u32[]{:S(2)}, u32[]{:S(2)}) collective-permute-start(bf16[24,16,128]{2,1,0:T(8,128)(2,1)S(1)} %get-tuple-element.48), channel_id=1, source_target_pairs={{0,3},{1,2},{2,1},{3,0},{4,7},{5,6},{6,5},{7,4},{8,11},{9,10},{10,... | collective-permute-start | bytes 294920 | tf_op jit(solution)/shard_map/ppermute | solution.py:328
  84.8 5.6 %shard_map.142 = (f32[24,8,3,8,128]{4,3,2,1,0:T(8,128)}, f32[24,16,128]{2,1,0:T(8,128)S(1)}) custom-call(s32[1]{0:T(128)} %bitcast.me_ref, bf16[24,32,128]{2,1,0:T(8,128)(2,1)S(1)} %get-tuple-element.54.refs_0_, bf16[24,32,128]{2,1,0:T(8,128)(2,1)S(1)} %collective-permute-done.20.refs_1_, bf16[24,32,128]{2,1,0:T(8,128)(2,1)S(1)} %collective-permute-done.21.refs_2_, ...), custom_call_target="tpu_custom_call" | custom-call | flops 1308622848 | bytes 4000000 | tf_op jit(solution)/shard_map/pallas_call | solution.py:495
  90.4 4.3 %shard_map.143 = (f32[24,8,3,8,128]{4,3,2,1,0:T(8,128)}, f32[24,384]{1,0:T(8,128)}) custom-call(s32[1]{0:T(128)} %bitcast.me_ref, bf16[24,16,128]{2,1,0:T(8,128)(2,1)S(1)} %get-tuple-element.45.refs_0_, bf16[24,16,128]{2,1,0:T(8,128)(2,1)S(1)} %collective-permute-done.17.refs_1_, ...), custom_call_target="tpu_custom_call", output_to_operand_aliasing={{0}: (19, {})} | custom-call | flops 654311424 | bytes 4000000 | tf_op jit(solution)/shard_map/pallas_call | solution.py:495
  (49 shorter events, 0.2 us)
Async XLA Ops:
  0.6 15.7 %copy-start = (f32[24,192,128]{2,1,0:T(8,128)S(1)}, f32[24,192,128]{2,1,0:T(8,128)}, u32[]{:S(2)}) copy-start(f32[24,192,128]{2,1,0:T(8,128)} %pair_ref.7) | copy-start | bytes 7077892
  0.6 15.7 %copy-start.10 = (s32[192]{0:T(256)S(1)}, s32[192]{0:T(256)}, u32[]{:S(2)}) copy-start(s32[192]{0:T(256)} %refs_12_.1) | copy-start | bytes 2308
  0.7 15.7 %copy-start.1 = (bf16[128,512]{1,0:T(8,128)(2,1)S(1)}, bf16[128,512]{1,0:T(8,128)(2,1)}, u32[]{:S(2)}) copy-start(bf16[128,512]{1,0:T(8,128)(2,1)} %w_ref.5) | copy-start | bytes 393220
  0.7 41.7 %copy-start.8 = (f32[24,384]{1,0:T(8,128)S(1)}, f32[24,384]{1,0:T(8,128)}, u32[]{:S(2)}) copy-start(f32[24,384]{1,0:T(8,128)} %single_ref.3) | copy-start | bytes 110596
  5.3 21.3 %collective-permute-start.14 = (bf16[105,8,128]{2,1,0:T(8,128)(2,1)S(1)}, bf16[105,8,128]{2,1,0:T(8,128)(2,1)S(1)}, u32[]{:S(2)}, u32[]{:S(2)}) collective-permute-start(bf16[105,8,128]{2,1,0:T(8,128)(2,1)S(1)} %get-tuple-element.41), channel_id=1, source_target_pairs={{0,5},{1,4},{2,7},{3,6},{4,1},{5,0},{6,3},{7,2},{8,13},{9,12},{10,... | collective-permute-start | bytes 645128 | tf_op jit(solution)/shard_map/ppermute | solution.py:328
  10.4 18.3 %collective-permute-start.10 = (bf16[105,8,128]{2,1,0:T(8,128)(2,1)S(1)}, bf16[105,8,128]{2,1,0:T(8,128)(2,1)S(1)}, u32[]{:S(2)}, u32[]{:S(2)}) collective-permute-start(bf16[105,8,128]{2,1,0:T(8,128)(2,1)S(1)} %get-tuple-element.41), channel_id=1, source_target_pairs={{0,1},{1,0},{2,3},{3,2},{4,5},{5,4},{6,7},{7,6},{8,9},{9,8},{10,11... | collective-permute-start | bytes 645128 | tf_op jit(solution)/shard_map/ppermute | solution.py:328
  10.9 17.8 %collective-permute-start.15 = (bf16[105,8,128]{2,1,0:T(8,128)(2,1)S(1)}, bf16[105,8,128]{2,1,0:T(8,128)(2,1)S(1)}, u32[]{:S(2)}, u32[]{:S(2)}) collective-permute-start(bf16[105,8,128]{2,1,0:T(8,128)(2,1)S(1)} %get-tuple-element.42), channel_id=1, source_target_pairs={{0,6},{1,7},{2,4},{3,5},{4,2},{5,3},{6,0},{7,1},{8,14},{9,15},{10,... | collective-permute-start | bytes 645128 | tf_op jit(solution)/shard_map/ppermute | solution.py:328
  12.3 23.3 %collective-permute-start.11 = (bf16[105,8,128]{2,1,0:T(8,128)(2,1)S(1)}, bf16[105,8,128]{2,1,0:T(8,128)(2,1)S(1)}, u32[]{:S(2)}, u32[]{:S(2)}) collective-permute-start(bf16[105,8,128]{2,1,0:T(8,128)(2,1)S(1)} %get-tuple-element.42), channel_id=1, source_target_pairs={{0,2},{1,3},{2,0},{3,1},{4,6},{5,7},{6,4},{7,5},{8,10},{9,11},{10,... | collective-permute-start | bytes 645128 | tf_op jit(solution)/shard_map/ppermute | solution.py:328
  12.5 23.1 %collective-permute-start.16 = (bf16[105,8,128]{2,1,0:T(8,128)(2,1)S(1)}, bf16[105,8,128]{2,1,0:T(8,128)(2,1)S(1)}, u32[]{:S(2)}, u32[]{:S(2)}) collective-permute-start(bf16[105,8,128]{2,1,0:T(8,128)(2,1)S(1)} %get-tuple-element.43), channel_id=1, source_target_pairs={{0,7},{1,6},{2,5},{3,4},{4,3},{5,2},{6,1},{7,0},{8,15},{9,14},{10,... | collective-permute-start | bytes 645128 | tf_op jit(solution)/shard_map/ppermute | solution.py:328
  16.4 46.0 %copy-start.3 = (bf16[384,768]{1,0:T(8,128)(2,1)S(1)}, bf16[384,768]{1,0:T(8,128)(2,1)}, u32[]{:S(2)}) copy-start(bf16[384,768]{1,0:T(8,128)(2,1)} %refs_10_.1) | copy-start | bytes 1769476
  16.4 46.0 %copy-start.5 = (bf16[384,384]{1,0:T(8,128)(2,1)S(1)}, bf16[384,384]{1,0:T(8,128)(2,1)}, u32[]{:S(2)}) copy-start(bf16[384,384]{1,0:T(8,128)(2,1)} %refs_8_.3) | copy-start | bytes 884740
  16.4 46.0 %copy-start.6 = (bf16[384,384]{1,0:T(8,128)(2,1)S(1)}, bf16[384,384]{1,0:T(8,128)(2,1)}, u32[]{:S(2)}) copy-start(bf16[384,384]{1,0:T(8,128)(2,1)} %refs_9_.1) | copy-start | bytes 884740
  26.6 29.4 %collective-permute-start.7 = (bf16[144,8,128]{2,1,0:T(8,128)(2,1)S(1)}, bf16[144,8,128]{2,1,0:T(8,128)(2,1)S(1)}, u32[]{:S(2)}, u32[]{:S(2)}) collective-permute-start(bf16[144,8,128]{2,1,0:T(8,128)(2,1)S(1)} %get-tuple-element.38), channel_id=1, source_target_pairs={{0,1},{1,0},{2,3},{3,2},{4,5},{5,4},{6,7},{7,6},{8,9},{9,8},{10,11... | collective-permute-start | bytes 884744 | tf_op jit(solution)/shard_map/ppermute | solution.py:328
  28.7 29.3 %collective-permute-start.8 = (bf16[144,8,128]{2,1,0:T(8,128)(2,1)S(1)}, bf16[144,8,128]{2,1,0:T(8,128)(2,1)S(1)}, u32[]{:S(2)}, u32[]{:S(2)}) collective-permute-start(bf16[144,8,128]{2,1,0:T(8,128)(2,1)S(1)} %get-tuple-element.39), channel_id=1, source_target_pairs={{0,2},{1,3},{2,0},{3,1},{4,6},{5,7},{6,4},{7,5},{8,10},{9,11},{10,... | collective-permute-start | bytes 884744 | tf_op jit(solution)/shard_map/ppermute | solution.py:328
  28.7 30.9 %collective-permute-start.9 = (bf16[144,8,128]{2,1,0:T(8,128)(2,1)S(1)}, bf16[144,8,128]{2,1,0:T(8,128)(2,1)S(1)}, u32[]{:S(2)}, u32[]{:S(2)}) collective-permute-start(bf16[144,8,128]{2,1,0:T(8,128)(2,1)S(1)} %get-tuple-element.40), channel_id=1, source_target_pairs={{0,3},{1,2},{2,1},{3,0},{4,7},{5,6},{6,5},{7,4},{8,11},{9,10},{10,... | collective-permute-start | bytes 884744 | tf_op jit(solution)/shard_map/ppermute | solution.py:328
  35.6 18.4 %collective-permute-start.12 = (bf16[105,8,128]{2,1,0:T(8,128)(2,1)S(1)}, bf16[105,8,128]{2,1,0:T(8,128)(2,1)S(1)}, u32[]{:S(2)}, u32[]{:S(2)}) collective-permute-start(bf16[105,8,128]{2,1,0:T(8,128)(2,1)S(1)} %get-tuple-element.43), channel_id=1, source_target_pairs={{0,3},{1,2},{2,1},{3,0},{4,7},{5,6},{6,5},{7,4},{8,11},{9,10},{10,... | collective-permute-start | bytes 645128 | tf_op jit(solution)/shard_map/ppermute | solution.py:328
  35.6 19.9 %collective-permute-start.13 = (bf16[105,8,128]{2,1,0:T(8,128)(2,1)S(1)}, bf16[105,8,128]{2,1,0:T(8,128)(2,1)S(1)}, u32[]{:S(2)}, u32[]{:S(2)}) collective-permute-start(bf16[105,8,128]{2,1,0:T(8,128)(2,1)S(1)} %get-tuple-element.32.rest_0_.refs_0_), channel_id=1, source_target_pairs={{0,4},{1,5},{2,6},{3,7},{4,0},{5,1},{6,2},{7,3},{8,12},{9,13},{10,... | collective-permute-start | bytes 645128 | tf_op jit(solution)/shard_map/ppermute | solution.py:328
  54.0 11.3 %collective-permute-start.4 = (bf16[48,8,128]{2,1,0:T(8,128)(2,1)S(1)}, bf16[48,8,128]{2,1,0:T(8,128)(2,1)S(1)}, u32[]{:S(2)}, u32[]{:S(2)}) collective-permute-start(bf16[48,8,128]{2,1,0:T(8,128)(2,1)S(1)} %get-tuple-element.35), channel_id=1, source_target_pairs={{0,5},{1,4},{2,7},{3,6},{4,1},{5,0},{6,3},{7,2},{8,13},{9,12},{10,... | collective-permute-start | bytes 294920 | tf_op jit(solution)/shard_map/ppermute | solution.py:328
  55.6 10.6 %collective-permute-start = (bf16[48,8,128]{2,1,0:T(8,128)(2,1)S(1)}, bf16[48,8,128]{2,1,0:T(8,128)(2,1)S(1)}, u32[]{:S(2)}, u32[]{:S(2)}) collective-permute-start(bf16[48,8,128]{2,1,0:T(8,128)(2,1)S(1)} %get-tuple-element.35), channel_id=1, source_target_pairs={{0,1},{1,0},{2,3},{3,2},{4,5},{5,4},{6,7},{7,6},{8,9},{9,8},{10,11... | collective-permute-start | bytes 294920 | tf_op jit(solution)/shard_map/ppermute | solution.py:328
  56.1 10.1 %collective-permute-start.5 = (bf16[48,8,128]{2,1,0:T(8,128)(2,1)S(1)}, bf16[48,8,128]{2,1,0:T(8,128)(2,1)S(1)}, u32[]{:S(2)}, u32[]{:S(2)}) collective-permute-start(bf16[48,8,128]{2,1,0:T(8,128)(2,1)S(1)} %get-tuple-element.36), channel_id=1, source_target_pairs={{0,6},{1,7},{2,4},{3,5},{4,2},{5,3},{6,0},{7,1},{8,14},{9,15},{10,... | collective-permute-start | bytes 294920 | tf_op jit(solution)/shard_map/ppermute | solution.py:328
  58.0 11.1 %collective-permute-start.1 = (bf16[48,8,128]{2,1,0:T(8,128)(2,1)S(1)}, bf16[48,8,128]{2,1,0:T(8,128)(2,1)S(1)}, u32[]{:S(2)}, u32[]{:S(2)}) collective-permute-start(bf16[48,8,128]{2,1,0:T(8,128)(2,1)S(1)} %get-tuple-element.36), channel_id=1, source_target_pairs={{0,2},{1,3},{2,0},{3,1},{4,6},{5,7},{6,4},{7,5},{8,10},{9,11},{10,... | collective-permute-start | bytes 294920 | tf_op jit(solution)/shard_map/ppermute | solution.py:328
  59.6 9.6 %collective-permute-start.6 = (bf16[48,8,128]{2,1,0:T(8,128)(2,1)S(1)}, bf16[48,8,128]{2,1,0:T(8,128)(2,1)S(1)}, u32[]{:S(2)}, u32[]{:S(2)}) collective-permute-start(bf16[48,8,128]{2,1,0:T(8,128)(2,1)S(1)} %get-tuple-element.37), channel_id=1, source_target_pairs={{0,7},{1,6},{2,5},{3,4},{4,3},{5,2},{6,1},{7,0},{8,15},{9,14},{10,... | collective-permute-start | bytes 294920 | tf_op jit(solution)/shard_map/ppermute | solution.py:328
  65.3 17.6 %collective-permute-start.20 = (bf16[24,32,128]{2,1,0:T(8,128)(2,1)S(1)}, bf16[24,32,128]{2,1,0:T(8,128)(2,1)S(1)}, u32[]{:S(2)}, u32[]{:S(2)}) collective-permute-start(bf16[24,32,128]{2,1,0:T(8,128)(2,1)S(1)} %get-tuple-element.55), channel_id=1, source_target_pairs={{0,1},{1,0},{2,3},{3,2},{4,5},{5,4},{6,7},{7,6},{8,9},{9,8},{10,11... | collective-permute-start | bytes 589832 | tf_op jit(solution)/shard_map/ppermute | solution.py:328
  66.1 18.6 %collective-permute-start.21 = (bf16[24,32,128]{2,1,0:T(8,128)(2,1)S(1)}, bf16[24,32,128]{2,1,0:T(8,128)(2,1)S(1)}, u32[]{:S(2)}, u32[]{:S(2)}) collective-permute-start(bf16[24,32,128]{2,1,0:T(8,128)(2,1)S(1)} %get-tuple-element.56), channel_id=1, source_target_pairs={{0,2},{1,3},{2,0},{3,1},{4,6},{5,7},{6,4},{7,5},{8,10},{9,11},{10,... | collective-permute-start | bytes 589832 | tf_op jit(solution)/shard_map/ppermute | solution.py:328
  66.2 18.6 %collective-permute-start.22 = (bf16[24,32,128]{2,1,0:T(8,128)(2,1)S(1)}, bf16[24,32,128]{2,1,0:T(8,128)(2,1)S(1)}, u32[]{:S(2)}, u32[]{:S(2)}) collective-permute-start(bf16[24,32,128]{2,1,0:T(8,128)(2,1)S(1)} %get-tuple-element.57), channel_id=1, source_target_pairs={{0,3},{1,2},{2,1},{3,0},{4,7},{5,6},{6,5},{7,4},{8,11},{9,10},{10,... | collective-permute-start | bytes 589832 | tf_op jit(solution)/shard_map/ppermute | solution.py:328
  69.0 10.9 %collective-permute-start.2 = (bf16[48,8,128]{2,1,0:T(8,128)(2,1)S(1)}, bf16[48,8,128]{2,1,0:T(8,128)(2,1)S(1)}, u32[]{:S(2)}, u32[]{:S(2)}) collective-permute-start(bf16[48,8,128]{2,1,0:T(8,128)(2,1)S(1)} %get-tuple-element.37), channel_id=1, source_target_pairs={{0,3},{1,2},{2,1},{3,0},{4,7},{5,6},{6,5},{7,4},{8,11},{9,10},{10,... | collective-permute-start | bytes 294920 | tf_op jit(solution)/shard_map/ppermute | solution.py:328
  69.2 15.6 %copy-start.9 = (bf16[128,128]{1,0:T(8,128)(2,1)S(1)}, bf16[128,128]{1,0:T(8,128)(2,1)}, u32[]{:S(2)}) copy-start(bf16[128,128]{1,0:T(8,128)(2,1)} %param.18) | copy-start | bytes 98308
  69.2 15.6 %copy-start.12 = (bf16[128,16]{0,1:T(8,128)(2,1)S(1)}, bf16[128,16]{0,1:T(8,128)(2,1)}, u32[]{:S(2)}) copy-start(bf16[128,16]{0,1:T(8,128)(2,1)} %param.21) | copy-start | bytes 12292
  69.2 10.8 %collective-permute-start.3 = (bf16[48,8,128]{2,1,0:T(8,128)(2,1)S(1)}, bf16[48,8,128]{2,1,0:T(8,128)(2,1)S(1)}, u32[]{:S(2)}, u32[]{:S(2)}) collective-permute-start(bf16[48,8,128]{2,1,0:T(8,128)(2,1)S(1)} %get-tuple-element.34.refs_0_._), channel_id=1, source_target_pairs={{0,4},{1,5},{2,6},{3,7},{4,0},{5,1},{6,2},{7,3},{8,12},{9,13},{10,... | collective-permute-start | bytes 294920 | tf_op jit(solution)/shard_map/ppermute | solution.py:328
  81.1 9.2 %collective-permute-start.17 = (bf16[24,16,128]{2,1,0:T(8,128)(2,1)S(1)}, bf16[24,16,128]{2,1,0:T(8,128)(2,1)S(1)}, u32[]{:S(2)}, u32[]{:S(2)}) collective-permute-start(bf16[24,16,128]{2,1,0:T(8,128)(2,1)S(1)} %get-tuple-element.46), channel_id=1, source_target_pairs={{0,1},{1,0},{2,3},{3,2},{4,5},{5,4},{6,7},{7,6},{8,9},{9,8},{10,11... | collective-permute-start | bytes 294920 | tf_op jit(solution)/shard_map/ppermute | solution.py:328
  81.9 8.4 %collective-permute-start.18 = (bf16[24,16,128]{2,1,0:T(8,128)(2,1)S(1)}, bf16[24,16,128]{2,1,0:T(8,128)(2,1)S(1)}, u32[]{:S(2)}, u32[]{:S(2)}) collective-permute-start(bf16[24,16,128]{2,1,0:T(8,128)(2,1)S(1)} %get-tuple-element.47), channel_id=1, source_target_pairs={{0,2},{1,3},{2,0},{3,1},{4,6},{5,7},{6,4},{7,5},{8,10},{9,11},{10,... | collective-permute-start | bytes 294920 | tf_op jit(solution)/shard_map/ppermute | solution.py:328
  82.9 7.5 %collective-permute-start.19 = (bf16[24,16,128]{2,1,0:T(8,128)(2,1)S(1)}, bf16[24,16,128]{2,1,0:T(8,128)(2,1)S(1)}, u32[]{:S(2)}, u32[]{:S(2)}) collective-permute-start(bf16[24,16,128]{2,1,0:T(8,128)(2,1)S(1)} %get-tuple-element.48), channel_id=1, source_target_pairs={{0,3},{1,2},{2,1},{3,0},{4,7},{5,6},{6,5},{7,4},{8,11},{9,10},{10,... | collective-permute-start | bytes 294920 | tf_op jit(solution)/shard_map/ppermute | solution.py:328
  (4 other events, 49.8 us)
